TPU v7x, 32 devices: a whole 2x2x4 slice. The times are simulated.
32 devices in a mesh: seq: 8 (over z, x), fsdp: 4 (over y, core).
Axes of the slice: x: 2, y: 2, z: 4, core: 2. Of those that a mesh axis runs over, the one named last changes fastest.
Arguments:
- block_input: bfloat16 [2, 4, 6144, 512], P(None, 'fsdp', 'seq'), may hold values from -6 to 6
- seq_ids: int32 [2, 4, 6144], P(None, 'fsdp', 'seq'), may hold values from 0 to 1, as said below
- random_features: bfloat16 [8, 64, 256], replicated, may hold values from -5 to 5
- ln1_gain: bfloat16 [512], P('fsdp'), may hold values from 0.099609375 to 1.8984375
- w_query: bfloat16 [512, 512], P('fsdp'), may hold values from -0.25 to 0.25
- w_key: bfloat16 [512, 512], P('fsdp'), may hold values from -0.25 to 0.25
- w_value: bfloat16 [512, 512], P('fsdp'), may hold values from -0.25 to 0.25
- w_out: bfloat16 [512, 512], P('fsdp'), may hold values from -1 to 1
- ln2_gain: bfloat16 [512], P('fsdp'), may hold values from 0.099609375 to 1.8984375
- w_up: bfloat16 [512, 2048], P('fsdp'), may hold values from -0.25 to 0.25
- w_down: bfloat16 [2048, 512], P('fsdp'), may hold values from -0.125 to 0.125
- cotangent: bfloat16 [2, 4, 6144, 512], P(None, 'fsdp', 'seq'), may hold values from -6 to 6
Outputs:
- block_output: bfloat16 [2, 4, 6144, 512], P(None, 'fsdp', 'seq')
- input_grad: bfloat16 [2, 4, 6144, 512], P(None, 'fsdp', 'seq')
- ln1_gain_grad: float32 [512], P('fsdp')
- w_query_grad: float32 [512, 512], P('fsdp')
- w_key_grad: float32 [512, 512], P('fsdp')
- w_value_grad: float32 [512, 512], P('fsdp')
- w_out_grad: float32 [512, 512], P('fsdp')
- ln2_gain_grad: float32 [512], P('fsdp')
- w_up_grad: float32 [512, 2048], P('fsdp')
- w_down_grad: float32 [2048, 512], P('fsdp')
Inputs may be any that keep to these rules, and one draw needn't show every extreme that they name: `seq_ids`: along each group's tokens the ids never fall; each of the 2 sequences of a group holds 1536 tokens or more.
All inputs are finite; a program needn't handle non-finite values.
Results may differ from a plain program's by a relative error of at most 0.035.
Values may be sent and summed in bfloat16 or wider, within the bound.
A program may use at most 256 MiB of HBM per device.

v0:
```python
import functools
import math

import jax
import jax.numpy as jnp
from jax import lax
from jax.experimental import pallas as pl
from jax.experimental.pallas import tpu as pltpu
from jax.sharding import PartitionSpec as P

EPS = 1e-05
TILE = 256
F32 = jnp.float32
BF16 = jnp.bfloat16
PAD = 16


def dot(a, b):
    return lax.dot_general(a, b, (((1,), (0,)), ((), ())), preferred_element_type=F32)


def dot_nt(a, b):
    return lax.dot_general(a, b, (((1,), (1,)), ((), ())), preferred_element_type=F32)


def norm_parts(v):
    c = v - jnp.mean(v, axis=-1, keepdims=True)
    r = lax.rsqrt(jnp.mean(c * c, axis=-1, keepdims=True) + EPS)
    return c * r, r


def norm_back(grad, normed, rescale, gain):
    e = grad * gain
    return rescale * (
        e
        - jnp.mean(e, axis=-1, keepdims=True)
        - normed * jnp.mean(e * normed, axis=-1, keepdims=True)
    )


def features(scaled, rbd_ref, feat_ref, feats):
    lane = lax.broadcasted_iota(jnp.int32, (scaled.shape[0], 128), 1)
    low = lane < 64
    log_scale = 0.5 * math.log(feats)
    as_float = scaled.astype(F32)
    for quad in range(scaled.shape[1] // 256):
        u = dot(scaled[:, 256 * quad : 256 * quad + 256], rbd_ref[quad])
        for pair in range(2):
            s = as_float[:, 256 * quad + 128 * pair : 256 * quad + 128 * pair + 128]
            s = s * s
            sq_a = jnp.sum(jnp.where(low, s, 0.0), axis=-1, keepdims=True)
            sq_b = jnp.sum(jnp.where(low, 0.0, s), axis=-1, keepdims=True)
            for k, sq in enumerate((sq_a, sq_b)):
                col = feats * (2 * pair + k)
                f = jnp.exp(u[:, col : col + feats] - (0.5 * sq + log_scale))
                base = feats * (4 * quad + 2 * pair + k)
                feat_ref[:, base : base + feats] = f.astype(BF16)


def summary_rows(rows, zrow, mask_t):
    z = mask_t if zrow is None else (mask_t.astype(F32) * zrow).astype(BF16)
    return jnp.concatenate([rows * mask_t[0:1], rows * mask_t[1:2], z], axis=0)


def key_kernel(x_ref, g_ref, wk_ref, wv_ref, rbd_ref, mt_ref, *refs, feats, factor, n_alias):
    a1_ref, ks_ref, vv_ref, fk_ref, p_ref, acc = refs[n_alias:]
    step = pl.program_id(0)

    @pl.when(step == 0)
    def _():
        acc[...] = jnp.zeros_like(acc)

    normed, _ = norm_parts(x_ref[...].astype(F32))
    a1 = (normed * g_ref[...].astype(F32)).astype(BF16)
    a1_ref[...] = a1
    ks = (dot(a1, wk_ref[...]) * factor).astype(BF16)
    ks_ref[...] = ks
    vv = dot(a1, wv_ref[...]).astype(BF16)
    vv_ref[...] = vv
    features(ks, rbd_ref, fk_ref, feats)
    vt = vv.T
    mask_t = mt_ref[...]
    for h in range(vv.shape[1] // 64):
        lt = summary_rows(vt[64 * h : 64 * h + 64], None, mask_t)
        acc[h] += dot(lt, fk_ref[:, feats * h : feats * h + feats])

    @pl.when(step == pl.num_programs(0) - 1)
    def _():
        p_ref[...] = acc[...].astype(BF16)


def query_kernel(a1_ref, wq_ref, rbd_ref, qs_ref, fq_ref, *, feats, factor):
    qs = (dot(a1_ref[...], wq_ref[...]) * factor).astype(BF16)
    qs_ref[...] = qs
    features(qs, rbd_ref, fq_ref, feats)


def mid_kernel(
    x_ref, dy_ref, fq_ref, qs_ref, last_ref, mt_ref, b_ref, wo_ref, g2_ref, wu_ref, wd_ref, rt_ref,
    *refs, feats, factor, n_alias,
):
    out_ref, att_ref, a2_ref, hid_ref, dpre_ref, dmid_ref, dq_ref, p_ref, gg_ref, acc = refs[n_alias:]
    step = pl.program_id(0)

    @pl.when(step == 0)
    def _():
        acc[...] = jnp.zeros_like(acc)
        gg_ref[...] = jnp.zeros_like(gg_ref)

    rows = x_ref.shape[0]
    pairs = x_ref.shape[1] // 128
    last = last_ref[...].astype(F32) > 0.5
    lane = lax.broadcasted_iota(jnp.int32, (rows, 128), 1)
    sel = jnp.logical_xor(lane < 64, last)

    def swap(v):
        return jnp.where(last, pltpu.roll(v, 64, 1), v)

    att_parts, inv_parts = [], []
    for p in range(pairs):
        base = 2 * feats * p
        a = dot_nt(fq_ref[:, base : base + feats], b_ref[2 * p])
        b = dot_nt(fq_ref[:, base + feats : base + 2 * feats], b_ref[2 * p + 1])
        num = jnp.where(sel, a[:, :128], b[:, :128])
        den = jnp.where(sel, a[:, 128:], b[:, 128:])
        inv = 1.0 / den
        att_parts.append(swap(num * inv))
        inv_parts.append(swap(inv))
    att = jnp.concatenate(att_parts, axis=1)
    inv = jnp.concatenate(inv_parts, axis=1)
    att_low = att.astype(BF16)
    att_ref[...] = att_low
    mixed = x_ref[...].astype(F32) + dot(att_low, wo_ref[...])
    normed, rescale = norm_parts(mixed)
    g2 = g2_ref[...].astype(F32)
    a2 = (normed * g2).astype(BF16)
    a2_ref[...] = a2
    dy = dy_ref[...]
    for j in range(wu_ref.shape[1] // 256):
        js = slice(256 * j, 256 * j + 256)
        pre = dot(a2, wu_ref[:, js])
        dh = dot_nt(dy, wd_ref[js, :])
        cdf = 0.5 * (1.0 + lax.erf(pre * 0.7071067811865476))
        slope = cdf + pre * jnp.exp(-0.5 * pre * pre) * 0.3989422804014327
        hid_ref[:, js] = (pre * cdf).astype(BF16)
        dpre_ref[:, js] = (dh * slope).astype(BF16)
    out_ref[...] = (mixed + dot(hid_ref[...], wd_ref[...])).astype(BF16)
    da2 = dot_nt(dpre_ref[...], wu_ref[...])
    gg_ref[...] += jnp.sum(da2 * normed, axis=0, keepdims=True)
    dmid = dy.astype(F32) + norm_back(da2, normed, rescale, g2)
    dmid_low = dmid.astype(BF16)
    dmid_ref[...] = dmid_low
    dnum = dot_nt(dmid_low, wo_ref[...]) * inv
    dpart = -dnum * att
    mask_t = mt_ref[...]
    for p in range(pairs):
        ps = slice(128 * p, 128 * p + 128)
        d, q = dnum[:, ps], dpart[:, ps]
        ds, qs = swap(d), swap(q)
        la = jnp.concatenate([jnp.where(sel, ds, 0.0), jnp.where(sel, qs, 0.0)], axis=1).astype(BF16)
        lb = jnp.concatenate([jnp.where(sel, 0.0, ds), jnp.where(sel, 0.0, qs)], axis=1).astype(BF16)
        base = 2 * feats * p
        fa = fq_ref[:, base : base + feats]
        fb = fq_ref[:, base + feats : base + 2 * feats]
        ga = (dot(la, b_ref[2 * p]) * fa.astype(F32)).astype(BF16)
        gb = (dot(lb, b_ref[2 * p + 1]) * fb.astype(F32)).astype(BF16)
        o = dot(jnp.concatenate([ga, gb], axis=1), rt_ref[p])
        dq_ref[:, ps] = (factor * (o[:, :128] - qs_ref[:, ps].astype(F32) * o[:, 128:])).astype(BF16)
        dt = d.astype(BF16).T
        qt = q.T
        for k, f in enumerate((fa, fb)):
            z = jnp.sum(qt[64 * k : 64 * k + 64], axis=0, keepdims=True)
            lt = summary_rows(dt[64 * k : 64 * k + 64], z, mask_t)
            acc[2 * p + k] += dot(lt, f)

    @pl.when(step == pl.num_programs(0) - 1)
    def _():
        p_ref[...] = acc[...].astype(BF16)


def second_kernel(
    x_ref, dmid_ref, fk_ref, ks_ref, vv_ref, last_ref, dq_ref, b_ref, g1_ref, wq_ref, wk_ref, wv_ref, rt_ref,
    *refs, feats, factor, n_alias,
):
    dx_ref, dk_ref, dv_ref, gg_ref = refs[n_alias:]
    step = pl.program_id(0)

    @pl.when(step == 0)
    def _():
        gg_ref[...] = jnp.zeros_like(gg_ref)

    rows = x_ref.shape[0]
    pairs = x_ref.shape[1] // 128
    last = last_ref[...].astype(F32) > 0.5
    lane = lax.broadcasted_iota(jnp.int32, (rows, 128), 1)
    sel = jnp.logical_xor(lane < 64, last)
    ones_a = jnp.where(sel, 1.0, 0.0).astype(BF16)
    ones_b = jnp.where(sel, 0.0, 1.0).astype(BF16)

    def swap(v):
        return jnp.where(last, pltpu.roll(v, 64, 1), v)

    for p in range(pairs):
        ps = slice(128 * p, 128 * p + 128)
        v = swap(vv_ref[:, ps].astype(F32))
        la = jnp.concatenate([jnp.where(sel, v, 0.0).astype(BF16), ones_a], axis=1)
        lb = jnp.concatenate([jnp.where(sel, 0.0, v).astype(BF16), ones_b], axis=1)
        base = 2 * feats * p
        fa = fk_ref[:, base : base + feats]
        fb = fk_ref[:, base + feats : base + 2 * feats]
        ga = (dot(la, b_ref[2 * p]) * fa.astype(F32)).astype(BF16)
        gb = (dot(lb, b_ref[2 * p + 1]) * fb.astype(F32)).astype(BF16)
        o = dot(jnp.concatenate([ga, gb], axis=1), rt_ref[p])
        dk_ref[:, ps] = (factor * (o[:, :128] - ks_ref[:, ps].astype(F32) * o[:, 128:])).astype(BF16)
        va = dot_nt(fa, b_ref[2 * p, :128])
        vb = dot_nt(fb, b_ref[2 * p + 1, :128])
        dv_ref[:, ps] = swap(jnp.where(sel, va, vb)).astype(BF16)
    da1 = dot_nt(dq_ref[...], wq_ref[...]) + dot_nt(dk_ref[...], wk_ref[...]) + dot_nt(dv_ref[...], wv_ref[...])
    normed, rescale = norm_parts(x_ref[...].astype(F32))
    gg_ref[...] += jnp.sum(da1 * normed, axis=0, keepdims=True)
    grad = norm_back(da1, normed, rescale, g1_ref[...].astype(F32))
    dx_ref[...] = (dmid_ref[...].astype(F32) + grad).astype(BF16)


def tile_spec(cols, off):
    return pl.BlockSpec((TILE, cols), lambda i: (i + off, 0))


def whole_spec(shape):
    zeros = (0,) * len(shape)
    return pl.BlockSpec(shape, lambda i: zeros, pipeline_mode=pl.Buffered(1))


def anyspec():
    return pl.BlockSpec(memory_space=pl.ANY)


def call(body, mb, tiles, tiled, wholes, mask_t, outs_tiled, outs_whole, scratch, previous, flops, name, **static):
    off = mb * tiles
    total = tiled[0].shape[0]
    in_specs = [tile_spec(a.shape[1], off) for a in tiled]
    args = list(tiled)
    for item in wholes:
        if item is mask_t:
            in_specs.append(pl.BlockSpec((PAD, TILE), lambda i: (0, i + off)))
        else:
            in_specs.append(whole_spec(item.shape))
        args.append(item)
    out_shape = [jax.ShapeDtypeStruct((total, c), BF16) for c in outs_tiled]
    out_specs = [tile_spec(c, off) for c in outs_tiled]
    for shape, dtype in outs_whole:
        out_shape.append(jax.ShapeDtypeStruct(shape, dtype))
        out_specs.append(pl.BlockSpec(shape, functools.partial(lambda n, i: (0,) * n, len(shape))))
    alias = {}
    if previous is not None:
        for k, a in enumerate(previous):
            alias[len(args)] = k
            args.append(a)
            in_specs.append(anyspec())
    n_alias = 0 if previous is None else len(previous)
    return pl.pallas_call(
        functools.partial(body, n_alias=n_alias, **static),
        grid=(tiles,),
        in_specs=in_specs,
        out_specs=out_specs,
        out_shape=out_shape,
        scratch_shapes=scratch,
        input_output_aliases=alias,
        compiler_params=pltpu.CompilerParams(dimension_semantics=("arbitrary",)),
        cost_estimate=pl.CostEstimate(flops=int(flops), bytes_accessed=1 << 20, transcendentals=0),
        name=name,
    )(*args)


def block_diag_features(rand):
    heads, dim, feats = rand.shape
    eye = jnp.eye(4, dtype=rand.dtype)
    quads = rand.reshape(heads // 4, 4, dim, feats)
    return jnp.einsum("qadf,ab->qadbf", quads, eye).reshape(heads // 4, 4 * dim, 4 * feats)


def back_features(rand):
    heads, dim, feats = rand.shape
    eye = jnp.eye(2, dtype=rand.dtype)
    pairs = rand.reshape(heads // 2, 2, dim, feats)
    left = jnp.einsum("padf,ab->pafbd", pairs, eye).reshape(heads // 2, 2 * feats, 2 * dim)
    right = jnp.broadcast_to(eye[None, :, None, :, None], (heads // 2, 2, feats, 2, dim))
    return jnp.concatenate([left, right.reshape(left.shape).astype(left.dtype)], axis=2)


def expand(pick, repeat):
    heads, _, feats = pick.shape
    first, second = pick[:, :64], pick[:, 64:128]
    z1, z2 = pick[:, 128:129], pick[:, 129:130]
    if repeat:
        z1, z2 = (jnp.broadcast_to(z, (heads, 64, feats)) for z in (z1, z2))
    else:
        z1, z2 = (jnp.pad(z, ((0, 0), (0, 63), (0, 0))) for z in (z1, z2))
    even = jnp.concatenate([first, second, z1, z2], axis=1)
    odd = jnp.concatenate([second, first, z2, z1], axis=1)
    parity = (jnp.arange(heads) % 2 == 0)[:, None, None]
    return jnp.where(parity, even, odd)


def place(local, ids, seqs):
    if seqs == 2:
        return local[:, None]
    slots = jnp.arange(seqs, dtype=jnp.int32)
    first = (slots == ids[0]).astype(BF16).reshape(1, seqs // 2, 2, 1, 1)
    last = (slots == ids[-1]).astype(BF16).reshape(1, seqs // 2, 2, 1, 1)
    heads, _, feats = local.shape
    rows = local[:, :128].reshape(heads, 1, 2, 64, feats)
    z = local[:, 128:130].reshape(heads, 1, 2, 1, feats)

    def put(v):
        return first * v[:, :, 0:1] + last * v[:, :, 1:2]

    body = put(rows).reshape(heads, seqs // 2, 128, feats)
    tail = jnp.pad(put(z).reshape(heads, seqs // 2, 2, feats), ((0, 0), (0, 0), (0, PAD - 2), (0, 0)))
    return jnp.concatenate([body, tail], axis=2)


def pick_two(dense, ids, seqs):
    if seqs == 2:
        return dense[:, 0]
    heads, _, _, feats = dense.shape
    rows = dense[:, :, :128].reshape(heads, seqs, 64, feats)
    z = dense[:, :, 128:130].reshape(heads, seqs, 1, feats)

    def get(k):
        return (lax.dynamic_index_in_dim(rows, k, 1, False), lax.dynamic_index_in_dim(z, k, 1, False))

    r1, z1 = get(ids[0])
    r2, z2 = get(ids[-1])
    return jnp.pad(jnp.concatenate([r1, r2, z1, z2], axis=1), ((0, 0), (0, PAD - 2), (0, 0)))


def sum_seq(dense):
    return lax.psum(dense, "seq")


def gather(w):
    return lax.all_gather(w, "fsdp", axis=0, tiled=True)


def per_device(block_input, seq_ids, rand, ln1_gain, w_query, w_key, w_value, w_out, ln2_gain, w_up, w_down, cotangent):
    micro, _, toks, width = block_input.shape
    heads, dim, feats = rand.shape
    hidden = w_up.shape[1]
    factor = dim ** (-0.25)
    seqs = max(1, lax.axis_size("seq") // 4)
    tiles = toks // TILE
    x = block_input.reshape(micro * toks, width)
    dy = cotangent.reshape(micro * toks, width)
    ids = seq_ids.reshape(micro, toks)
    last = (ids == (1 if seqs == 2 else ids[:, -1:])).reshape(-1)
    last_cols = jnp.broadcast_to(last.astype(BF16)[:, None], (micro * toks, 128))
    row = jnp.arange(PAD)[:, None]
    mask_t = jnp.where(row == 0, 1.0 - last.astype(F32), jnp.where(row == 1, last.astype(F32), 0.0)).astype(BF16)
    rbd = block_diag_features(rand)
    rt = back_features(rand)
    g1 = gather(ln1_gain).reshape(1, width)
    g2 = gather(ln2_gain).reshape(1, width)
    wq, wk, wv, wo, wu, wd = (gather(w) for w in (w_query, w_key, w_value, w_out, w_up, w_down))
    static = dict(feats=feats, factor=factor)
    rows = 128 + PAD
    summary = ((heads, rows, feats), BF16)
    acc = pltpu.VMEM((heads, rows, feats), F32)
    unit = 2.0 * toks * 256 * 256

    keep, sums = None, []
    for mb in range(micro):
        r = call(key_kernel, mb, tiles, [x], [g1, wk, wv, rbd, mask_t], mask_t,
                 [width, width, width, heads * feats], [summary], [acc], keep, 24 * unit, "keys", **static)
        keep = r[:4]
        sums.append(pick_two(sum_seq(place(r[4], ids[mb], seqs)), ids[mb], seqs))
    a1, ks, vv, fk = keep
    total = micro * toks
    qs, fq = pl.pallas_call(
        functools.partial(query_kernel, **static),
        grid=(micro * tiles,),
        in_specs=[tile_spec(width, 0), whole_spec(wq.shape), whole_spec(rbd.shape)],
        out_specs=[tile_spec(width, 0), tile_spec(heads * feats, 0)],
        out_shape=[jax.ShapeDtypeStruct((total, width), BF16), jax.ShapeDtypeStruct((total, heads * feats), BF16)],
        cost_estimate=pl.CostEstimate(flops=int(24 * unit), bytes_accessed=1 << 20, transcendentals=0),
        name="queries",
    )(a1, wq, rbd)
    keep, grads = None, []
    g2_grad = 0.0
    for mb in range(micro):
        b = expand(sums[mb], True)
        r = call(mid_kernel, mb, tiles, [x, dy, fq, qs, last_cols], [mask_t, b, wo, g2, wu, wd, rt], mask_t,
                 [width, width, width, hidden, hidden, width, width], [summary, ((1, width), F32)], [acc],
                 keep, 100 * unit, "mid", **static)
        keep = r[:7]
        g2_grad = g2_grad + r[8]
        grads.append(pick_two(sum_seq(place(r[7], ids[mb], seqs)), ids[mb], seqs))
    out, att, a2, hid, dpre, dmid, dq = keep
    keep = None
    g1_grad = 0.0
    for mb in range(micro):
        b = expand(grads[mb], False)
        r = call(second_kernel, mb, tiles, [x, dmid, fk, ks, vv, last_cols, dq], [b, g1, wq, wk, wv, rt], mask_t,
                 [width, width, width], [((1, width), F32)], [], keep, 44 * unit, "second", **static)
        keep = r[:3]
        g1_grad = g1_grad + r[3]
    dx, dk, dv = keep

    def weight_grad(left, right):
        return lax.dot_general(left, right, (((0,), (0,)), ((), ())), preferred_element_type=F32).astype(BF16)

    totals = (
        g1_grad.reshape(-1).astype(BF16),
        weight_grad(a1, dq),
        weight_grad(a1, dk),
        weight_grad(a1, dv),
        weight_grad(att, dmid),
        g2_grad.reshape(-1).astype(BF16),
        weight_grad(a2, dpre),
        weight_grad(hid, dy),
    )
    totals = [lax.psum_scatter(t, "fsdp", scatter_dimension=0, tiled=True) for t in totals]
    totals = [lax.psum(t, "seq").astype(F32) for t in totals]
    shape = block_input.shape
    return (out.reshape(shape), dx.reshape(shape), *totals)


def solution(mesh):
    tok = P(None, "fsdp", "seq", None)
    vec, mat = P("fsdp"), P("fsdp", None)
    return jax.shard_map(
        per_device,
        mesh=mesh,
        in_specs=(tok, P(None, "fsdp", "seq"), P(), vec, mat, mat, mat, mat, vec, mat, mat, tok),
        out_specs=(tok, tok, vec, mat, mat, mat, mat, vec, mat, mat),
        check_vma=False,
    )
```

profile of v0, /device:TPU:0, one launch (start us, length us, event | category | flops | bytes accessed | tf_op | source)
XLA Modules:
  0.0 504.9 jit_solution(262067570633033951)
XLA Ops:
  8.8 10.2 %all_gather.25.wk_ref = bf16[512,512]{1,0:T(8,128)(2,1)} all-gather(bf16[128,512]{1,0:T(8,128)(2,1)} %param.17), channel_id=1, replica_groups=mesh['seq'=8,'fsdp'=4] {'fsdp'}, dimensions={0}, use_global_device_ids=true | all-gather | bytes 655360 | tf_op jit(solution)/shard_map/all_gather | solution.py:343
  19.1 7.9 %all_gather.26.wv_ref = bf16[512,512]{1,0:T(8,128)(2,1)} all-gather(bf16[128,512]{1,0:T(8,128)(2,1)} %param.18), channel_id=1, replica_groups=mesh['seq'=8,'fsdp'=4] {'fsdp'}, dimensions={0}, use_global_device_ids=true | all-gather | bytes 655360 | tf_op jit(solution)/shard_map/all_gather | solution.py:343
  27.0 6.7 %all-gather = bf16[4,1,128]{2,1,0:T(2,128)(2,1)} all-gather(bf16[1,1,128]{2,1,0:T(2,128)(2,1)} %bitcast.79), channel_id=1, replica_groups=mesh['seq'=8,'fsdp'=4] {'fsdp'}, dimensions={0}, use_global_device_ids=true | all-gather | bytes 1280 | tf_op jit(solution)/shard_map/all_gather | solution.py:343
  37.4 7.3 %keys.2 = (bf16[1536,512]{1,0:T(8,128)(2,1)}, bf16[1536,512]{1,0:T(8,128)(2,1)}, bf16[1536,512]{1,0:T(8,128)(2,1)}, bf16[1536,2048]{1,0:T(8,128)(2,1)}, bf16[8,144,256]{2,1,0:T(8,128)(2,1)}) custom-call(bf16[1536,512]{1,0:T(8,128)(2,1)} %bitcast.54, bf16[1,512]{1,0:T(2,128)(2,1)} %bitcast.69, bf16[512,512]{1,0:T(8,128)(2,1)} %all_gather.25.wk_ref, ...), custom_call_target="tpu_custom_call" | custom-call | flops 2415919104 | bytes 1048576 | tf_op jit(solution)/shard_map/keys/pallas_call | solution.py:261
  44.8 7.4 %keys.3 = (bf16[1536,512]{1,0:T(8,128)(2,1)}, bf16[1536,512]{1,0:T(8,128)(2,1)}, bf16[1536,512]{1,0:T(8,128)(2,1)}, bf16[1536,2048]{1,0:T(8,128)(2,1)}, bf16[8,144,256]{2,1,0:T(8,128)(2,1)}) custom-call(bf16[1536,512]{1,0:T(8,128)(2,1)} %bitcast.55, ...), custom_call_target="tpu_custom_call", output_to_operand_aliasing={{0}: (6, {}), {1}: (7, {}), {2}: (8, {}), {3}: (9, {})} | custom-call | flops 2415919104 | bytes 1048576 | tf_op jit(solution)/shard_map/keys/pallas_call | solution.py:261
  55.2 5.1 %all-gather.1 = bf16[4,1,128]{2,1,0:T(2,128)(2,1)} all-gather(bf16[1,1,128]{2,1,0:T(2,128)(2,1)S(1)} %bitcast.80), channel_id=1, replica_groups=mesh['seq'=8,'fsdp'=4] {'fsdp'}, dimensions={0}, use_global_device_ids=true | all-gather | bytes 1280 | tf_op jit(solution)/shard_map/all_gather | solution.py:343
  61.5 10.8 %all_gather.27.wq_ref = bf16[512,512]{1,0:T(8,128)(2,1)} all-gather(bf16[128,512]{1,0:T(8,128)(2,1)S(1)} %copy-done.8), channel_id=1, replica_groups=mesh['seq'=8,'fsdp'=4] {'fsdp'}, dimensions={0}, use_global_device_ids=true | all-gather | bytes 655360 | tf_op jit(solution)/shard_map/all_gather | solution.py:343
  72.3 10.1 %all_gather.28.wo_ref = bf16[512,512]{1,0:T(8,128)(2,1)} all-gather(bf16[128,512]{1,0:T(8,128)(2,1)S(1)} %copy-done.9), channel_id=1, replica_groups=mesh['seq'=8,'fsdp'=4] {'fsdp'}, dimensions={0}, use_global_device_ids=true | all-gather | bytes 655360 | tf_op jit(solution)/shard_map/all_gather | solution.py:343
  82.4 8.2 %queries.1 = (bf16[1536,512]{1,0:T(8,128)(2,1)}, bf16[1536,2048]{1,0:T(8,128)(2,1)}) custom-call(bf16[1536,512]{1,0:T(8,128)(2,1)} %get-tuple-element.52.a1_ref, bf16[512,512]{1,0:T(8,128)(2,1)} %all_gather.27.wq_ref, bf16[2,256,1024]{2,1,0:T(8,128)(2,1)} %reshape.108.rbd_ref), custom_call_target="tpu_custom_call" | custom-call | flops 2415919104 | bytes 1048576 | tf_op jit(solution)/shard_map/queries/pallas_call | solution.py:379
  90.6 42.3 %all-reduce.19.cloned.1.call-done = (bf16[8,144,256]{2,1,0:T(8,128)(2,1)}, bf16[8,144,256]{2,1,0:T(8,128)(2,1)}) async-done(((bf16[8,144,256]{2,1,0:T(8,128)(2,1)}, bf16[8,144,256]{2,1,0:T(8,128)(2,1)}), (bf16[8,144,256]{2,1,0:T(8,128)(2,1)}, bf16[8,144,256]{2,1,0:T(8,128)(2,1)})) %all-reduce.19.cloned.1.call-update) | async-done | bytes 1179664 | tf_op jit(solution)/shard_map/psum | solution.py:339
  139.2 20.7 %mid.2 = (bf16[1536,512]{1,0:T(8,128)(2,1)}, bf16[1536,512]{1,0:T(8,128)(2,1)}, bf16[1536,512]{1,0:T(8,128)(2,1)}, bf16[1536,2048]{1,0:T(8,128)(2,1)}, bf16[1536...) custom-call(bf16[1536,512]{1,0:T(8,128)(2,1)} %bitcast.56, ...), custom_call_target="tpu_custom_call" | custom-call | flops 10066329600 | bytes 1048576 | tf_op jit(solution)/shard_map/mid/pallas_call | solution.py:261
  159.8 20.7 %mid.3 = (bf16[1536,512]{1,0:T(8,128)(2,1)}, bf16[1536,512]{1,0:T(8,128)(2,1)}, bf16[1536,512]{1,0:T(8,128)(2,1)}, bf16[1536,2048]{1,0:T(8,128)(2,1)}, bf16[1536...) custom-call(bf16[1536,512]{1,0:T(8,128)(2,1)} %bitcast.57, ...), custom_call_target="tpu_custom_call", output_to_operand_aliasing={{0}: (12, {}), {1}: (13, {}), {2}: (14, {}), {3}: (15, {}),... | custom-call | flops 10066329600 | bytes 1048576 | tf_op jit(solution)/shard_map/mid/pallas_call | solution.py:261
  180.6 3.9 convolution_convert_fusion.2
  186.7 73.5 %all-reduce.17.cloned.1.call-done = (bf16[8,144,256]{2,1,0:T(8,128)(2,1)}, bf16[8,144,256]{2,1,0:T(8,128)(2,1)}) async-done(((bf16[8,144,256]{2,1,0:T(8,128)(2,1)}, bf16[8,144,256]{2,1,0:T(8,128)(2,1)}), (bf16[8,144,256]{2,1,0:T(8,128)(2,1)}, bf16[8,144,256]{2,1,0:T(8,128)(2,1)})) %all-reduce.17.cloned.1.call-update) | async-done | bytes 1179664 | tf_op jit(solution)/shard_map/psum | solution.py:339
  265.4 9.3 %second.2 = (bf16[1536,512]{1,0:T(8,128)(2,1)}, bf16[1536,512]{1,0:T(8,128)(2,1)}, bf16[1536,512]{1,0:T(8,128)(2,1)}, f32[1,512]{1,0:T(1,128)}) custom-call(bf16[1536,512]{1,0:T(8,128)(2,1)} %bitcast.58, bf16[1536,512]{1,0:T(8,128)(2,1)} %get-tuple-element.65.dmid_ref, bf16[1536,2048]{1,0:T(8,128)(2,1)} %get-tuple-element.66.fk_ref, ...), custom_call_target="tpu_custom_call" | custom-call | flops 4429185024 | bytes 1048576 | tf_op jit(solution)/shard_map/second/pallas_call | solution.py:261
  274.7 9.3 %second.3 = (bf16[1536,512]{1,0:T(8,128)(2,1)}, bf16[1536,512]{1,0:T(8,128)(2,1)}, bf16[1536,512]{1,0:T(8,128)(2,1)}, f32[1,512]{1,0:T(1,128)}) custom-call(bf16[1536,512]{1,0:T(8,128)(2,1)} %bitcast.59, bf16[1536,512]{1,0:T(8,128)(2,1)} %get-tuple-element.65.dmid_ref, ...), custom_call_target="tpu_custom_call", output_to_operand_aliasing={{0}: (13, {}), {1}: (14, {}), {2}: (15, {})} | custom-call | flops 4429185024 | bytes 1048576 | tf_op jit(solution)/shard_map/second/pallas_call | solution.py:261
  289.3 8.2 %convolution_convert_fusion.1 = bf16[512,2048]{1,0:T(8,128)(2,1)} fusion(bf16[1536,512]{1,0:T(8,128)(2,1)} %get-tuple-element.83, bf16[1536,2048]{1,0:T(8,128)(2,1)} %get-tuple-element.84), kind=kOutput, calls=%fused_computation.1 | convolution fusion | flops 3222274048 | bytes 9961472 | tf_op jit(solution)/shard_map/dot_general | solution.py:410
  298.9 7.6 %convolution_convert_fusion = bf16[2048,512]{1,0:T(8,128)(2,1)} fusion(bf16[1536,2048]{1,0:T(8,128)(2,1)} %get-tuple-element.85, bf16[1536,512]{1,0:T(8,128)(2,1)S(1)} %bitcast.63), kind=kOutput, calls=%fused_computation | convolution fusion | flops 3222274048 | bytes 9961472 | tf_op jit(solution)/shard_map/dot_general | solution.py:410
  308.2 24.7 %reduce-scatter.9.cloned.1.call-done = bf16[128,512]{1,0:T(8,128)(2,1)} async-done(((bf16[512,512]{1,0:T(8,128)(2,1)}), bf16[128,512]{1,0:T(8,128)(2,1)}) %reduce-scatter.9.cloned.1.call-update) | async-done | bytes 131088 | tf_op jit(solution)/shard_map/reduce_scatter | solution.py:422
  332.9 33.5 %reduce-scatter.15.cloned.1.call-done = bf16[128,2048]{1,0:T(8,128)(2,1)} async-done(((bf16[512,2048]{1,0:T(8,128)(2,1)}), bf16[128,2048]{1,0:T(8,128)(2,1)}) %reduce-scatter.15.cloned.1.call-update) | async-done | bytes 524304 | tf_op jit(solution)/shard_map/reduce_scatter | solution.py:422
  366.5 33.5 %reduce-scatter.17.cloned.1.call-done = bf16[512,512]{1,0:T(8,128)(2,1)} async-done(((bf16[2048,512]{1,0:T(8,128)(2,1)}), bf16[512,512]{1,0:T(8,128)(2,1)}) %reduce-scatter.17.cloned.1.call-update) | async-done | bytes 524304 | tf_op jit(solution)/shard_map/reduce_scatter | solution.py:422
  401.4 5.8 %all-reduce.10 = (bf16[512]{0:T(512)(128)(2,1)S(1)}, bf16[512]{0:T(512)(128)(2,1)S(1)}) all-reduce(bf16[512]{0:T(512)(128)(2,1)S(1)} %convert_reduce_fusion.1, bf16[512]{0:T(512)(128)(2,1)S(1)} %convert_reduce_fusion), channel_id=2, replica_groups=mesh['seq'=8,'fsdp'=4] {'fsdp'}, use_global_device_ids=true, to_apply=%region_4.5.clone | all-reduce | flops 1024 | bytes 4096
  407.3 22.2 %all-reduce.6 = (bf16[128]{0:T(256)(128)(2,1)S(1)}, bf16[128]{0:T(256)(128)(2,1)S(1)}) all-reduce(bf16[128]{0:T(256)(128)(2,1)S(1)} %dynamic-slice.1, bf16[128]{0:T(256)(128)(2,1)S(1)} %dynamic-slice.3), channel_id=1, replica_groups=mesh['seq'=8,'fsdp'=4] {'seq'}, use_global_device_ids=true, to_apply=%region_5.6 | all-reduce | flops 256 | bytes 1024 | tf_op jit(solution)/shard_map/psum | solution.py:423
  430.5 60.0 %all-reduce.15.cloned.1.call-done = (bf16[128,512]{1,0:T(8,128)(2,1)}, bf16[128,512]{1,0:T(8,128)(2,1)}, bf16[128,512]{1,0:T(8,128)(2,1)}, bf16[128,512]{1,0:T(8...) async-done(((bf16[128,512]{1,0:T(8,128)(2,1)}, bf16[128,512]{1,0:T(8,128)(2,1)}, bf16[128,512]{1,0:T(8,128)(2,1)}, bf16[128,512]{1,0:T(8,128)(2,1)}, ...) | async-done | bytes 1572880 | tf_op jit(solution)/shard_map/psum | solution.py:423
  (133 shorter events, 39.6 us)
Async XLA Ops:
  8.0 124.8 %all-reduce.19.cloned.1.call-start = ((), (), s32[]{:S(2)}) async-start(), calls=%async_computation.16 | async-start | bytes 2359296 | tf_op jit(solution)/shard_map/psum | solution.py:339
  52.2 86.0 %all-gather.5.cloned.1.call-start = ((), (), s32[]{:S(2)}) async-start(), calls=%async_computation.6 | async-start | bytes 2621440 | tf_op jit(solution)/shard_map/all_gather | solution.py:343
  52.8 85.4 %all-gather.7.cloned.1.call-start = ((), (), s32[]{:S(2)}) async-start(), calls=%async_computation.7 | async-start | bytes 2621440 | tf_op jit(solution)/shard_map/all_gather | solution.py:343
  53.4 206.8 %all-reduce.17.cloned.1.call-start = ((), (), s32[]{:S(2)}) async-start(), calls=%async_computation.15 | async-start | bytes 2359296 | tf_op jit(solution)/shard_map/psum | solution.py:339
  54.5 6.9 %copy-start.8 = (bf16[128,512]{1,0:T(8,128)(2,1)S(1)}, bf16[128,512]{1,0:T(8,128)(2,1)}, u32[]{:S(2)}) copy-start(bf16[128,512]{1,0:T(8,128)(2,1)} %param.16) | copy-start | bytes 393220
  54.8 17.5 %copy-start.9 = (bf16[128,512]{1,0:T(8,128)(2,1)S(1)}, bf16[128,512]{1,0:T(8,128)(2,1)}, u32[]{:S(2)}) copy-start(bf16[128,512]{1,0:T(8,128)(2,1)} %param.19) | copy-start | bytes 393220
  180.5 126.1 %reduce-scatter.13.cloned.1.call-start = ((), (), s32[]{:S(2)}) async-start(), calls=%async_computation.11 | async-start | bytes 655360 | tf_op jit(solution)/shard_map/reduce_scatter | solution.py:422
  180.6 4.2 copy-start
  180.6 4.2 copy-start.1
  184.5 122.2 %reduce-scatter.7.cloned.1.call-start = ((), (), s32[]{:S(2)}) async-start(), calls=%async_computation.8 | async-start | bytes 655360 | tf_op jit(solution)/shard_map/reduce_scatter | solution.py:422
  186.6 121.6 %reduce-scatter.11.cloned.1.call-start = ((), (), s32[]{:S(2)}) async-start(), calls=%async_computation.10 | async-start | bytes 655360 | tf_op jit(solution)/shard_map/reduce_scatter | solution.py:422
  287.4 45.6 %reduce-scatter.9.cloned.1.call-start = ((), (), s32[]{:S(2)}) async-start(), calls=%async_computation.9 | async-start | bytes 655360 | tf_op jit(solution)/shard_map/reduce_scatter | solution.py:422
  289.2 77.2 %reduce-scatter.15.cloned.1.call-start = ((), (), s32[]{:S(2)}) async-start(), calls=%async_computation.12 | async-start | bytes 2621440 | tf_op jit(solution)/shard_map/reduce_scatter | solution.py:422
  297.5 102.5 %reduce-scatter.17.cloned.1.call-start = ((), (), s32[]{:S(2)}) async-start(), calls=%async_computation.13 | async-start | bytes 2621440 | tf_op jit(solution)/shard_map/reduce_scatter | solution.py:422
  306.5 93.5 %copy-start.20 = (u32[32]{0:T(128)S(1)}, u32[32]{0:T(128)}, u32[]{:S(2)}) copy-start(u32[32]{0:T(128)} %constant.49) | copy-start | bytes 388
  306.5 94.8 %copy-start.15 = (f32[1,512]{1,0:T(1,128)S(1)}, f32[1,512]{1,0:T(1,128)}, u32[]{:S(2)}) copy-start(f32[1,512]{1,0:T(1,128)} %get-tuple-element.81) | copy-start | bytes 6148
  306.5 94.8 %copy-start.16 = (f32[1,512]{1,0:T(1,128)S(1)}, f32[1,512]{1,0:T(1,128)}, u32[]{:S(2)}) copy-start(f32[1,512]{1,0:T(1,128)} %get-tuple-element.82) | copy-start | bytes 6148
  306.5 94.8 %copy-start.17 = (f32[1,512]{1,0:T(1,128)S(1)}, f32[1,512]{1,0:T(1,128)}, u32[]{:S(2)}) copy-start(f32[1,512]{1,0:T(1,128)} %get-tuple-element.76) | copy-start | bytes 6148
  306.5 94.8 %copy-start.18 = (f32[1,512]{1,0:T(1,128)S(1)}, f32[1,512]{1,0:T(1,128)}, u32[]{:S(2)}) copy-start(f32[1,512]{1,0:T(1,128)} %get-tuple-element.77) | copy-start | bytes 6148
  306.6 183.9 %all-reduce.15.cloned.1.call-start = ((), (), s32[]{:S(2)}) async-start(), calls=%async_computation.14 | async-start | bytes 3145728 | tf_op jit(solution)/shard_map/psum | solution.py:423
  490.5 4.3 copy-start.13
  490.5 5.1 %copy-start.12 = (bf16[128,512]{1,0:T(8,128)(2,1)S(1)}, bf16[128,512]{1,0:T(8,128)(2,1)}, u32[]{:S(2)}) copy-start(bf16[128,512]{1,0:T(8,128)(2,1)} %get-tuple-element.119) | copy-start | bytes 393220
  490.5 5.8 %copy-start.11 = (bf16[128,512]{1,0:T(8,128)(2,1)S(1)}, bf16[128,512]{1,0:T(8,128)(2,1)}, u32[]{:S(2)}) copy-start(bf16[128,512]{1,0:T(8,128)(2,1)} %get-tuple-element.120) | copy-start | bytes 393220
  490.5 6.5 %copy-start.10 = (bf16[128,512]{1,0:T(8,128)(2,1)S(1)}, bf16[128,512]{1,0:T(8,128)(2,1)}, u32[]{:S(2)}) copy-start(bf16[128,512]{1,0:T(8,128)(2,1)} %get-tuple-element.121) | copy-start | bytes 393220
  (8 other events, 18.3 us)
Sparse Core Ops, SparseCore 0:
  52.3 80.4 all-reduce.18
  180.7 79.4 all-reduce.16
  400.1 90.3 all-reduce.14
Sparse Core Ops, SparseCore 1:
  54.2 27.8 all-gather.4
  83.5 22.2 all-gather.6
  184.6 20.7 reduce-scatter.12
  207.9 21.6 reduce-scatter.6
  287.4 20.7 reduce-scatter.10
  311.3 21.6 reduce-scatter.8
  335.3 31.1 reduce-scatter.14
  368.9 31.1 reduce-scatter.16
where the time goes:
time: 506 us; the launch traced here: 505 us
  waiting for transfers between devices  270 us (53%)
  Pallas kernels  82.8 us (16%)
  blocking collectives  78.8 us (16%)
  matrix products  26.6 us (5%)
  other arithmetic  16.7 us (3%)
  between operations  16.5 us (3%)
  local copies, waits for them, and re-layouts  12.5 us (2%)
    psum x2, waiting for transfers between devices, sum_seq(): return lax.psum(dense, 'seq')  116 us
    reduce_scatter x6, waiting for transfers between devices, per_device(): lax.psum_scatter(t, 'fsdp', scatter_dimension=0, tiled=True)  93.4 us
    pallas_call x6, Pallas kernels, call(): pl.pallas_call(functools.partial(body, n_alias=n_alias, **static), grid=(...  74.6 us
    psum x1, waiting for transfers between devices, per_device(): totals = [lax.psum(t, 'seq').astype(F32) for t in totals]  60 us
    all_gather x6, blocking collectives, gather(): return lax.all_gather(w, 'fsdp', axis=0, tiled=True)  50.9 us
    dot_general x6, matrix products, weight_grad(): lax.dot_general(left, right, (((0,), (0,)), ((), ())), preferred_element_...  26.6 us
    psum x1, blocking collectives, per_device(): totals = [lax.psum(t, 'seq').astype(F32) for t in totals]  22.2 us
  transfers between devices with their start and end apart: 11, of which 7 were waited for; matrix products, arithmetic and copies ran while one was open for 8% of the time, Pallas kernels for 5%

commit v1 on v0

--- a/solution.py
+++ b/solution.py
@@ -62,120 +62,440 @@
     return jnp.concatenate([rows * mask_t[0:1], rows * mask_t[1:2], z], axis=0)
 
 
-def key_kernel(x_ref, g_ref, wk_ref, wv_ref, rbd_ref, mt_ref, *refs, feats, factor, n_alias):
-    a1_ref, ks_ref, vv_ref, fk_ref, p_ref, acc = refs[n_alias:]
-    step = pl.program_id(0)
-
-    @pl.when(step == 0)
-    def _():
+MESH_ID = pl.DeviceIdType.MESH
+
+
+def rows_at(index, size):
+    return pl.ds(pl.multiple_of(index * size, size), size)
+
+
+class Exchange:
+    def __init__(self):
+        self.s, self.f = lax.axis_index("seq"), lax.axis_index("fsdp")
+        self.ns, self.nf = lax.axis_size("seq"), lax.axis_size("fsdp")
+        self.ny = self.nf // 2
+        self.y, self.c = self.f // 2, self.f % 2
+        self.partner = self.y * 2 + (1 - self.c)
+        self.pending = []
+
+    def seq_peer(self, k):
+        return ((self.s + k) % self.ns, self.f)
+
+    def y_from(self, k):
+        return ((self.y + self.ny - k) % self.ny) * 2 + self.c
+
+    def y_to(self, k):
+        return ((self.y + k) % self.ny) * 2 + self.c
+
+    def barrier(self):
+        sem = pltpu.get_barrier_semaphore()
+        peers = [self.seq_peer(k) for k in range(1, self.ns)]
+        peers += [(self.s, self.partner)] + [(self.s, self.y_to(k)) for k in range(1, self.ny)]
+        for peer in peers:
+            pl.semaphore_signal(sem, inc=1, device_id=peer, device_id_type=MESH_ID)
+        pl.semaphore_wait(sem, len(peers))
+
+    def copy(self, src, dst, send, recv, peer):
+        return pltpu.make_async_remote_copy(
+            src_ref=src, dst_ref=dst, send_sem=send, recv_sem=recv, device_id=peer, device_id_type=MESH_ID
+        )
+
+    def start(self, *args):
+        c = self.copy(*args)
+        c.start()
+        self.pending.append(c)
+
+    def drain(self):
+        for c in self.pending:
+            c.wait_send()
+        self.pending = []
+
+
+class Gather:
+    def __init__(self, ex, shard, full, send, recv, local):
+        self.ex, self.shard, self.full, self.send, self.recv = ex, shard, full, send, recv
+        self.rows = shard.shape[0]
+        self.own = pltpu.make_async_copy(shard, self.part(ex.f), local)
+
+    def part(self, f):
+        return self.full.at[rows_at(f, self.rows), :]
+
+    def begin(self):
+        ex = self.ex
+        for k in range(1, ex.ny):
+            ex.start(self.shard, self.part(ex.f), self.send.at[k], self.recv.at[k], (ex.s, ex.y_to(k)))
+        ex.start(self.shard, self.part(ex.f), self.send.at[0], self.recv.at[0], (ex.s, ex.partner))
+        self.own.start()
+
+    def forward(self):
+        ex = self.ex
+        for k in range(1, ex.ny):
+            part = self.part(ex.y_from(k))
+            ex.copy(part, part, self.send.at[k], self.recv.at[k], (ex.s, ex.f)).wait_recv()
+            j = ex.ny - 1 + k
+            ex.start(part, part, self.send.at[j], self.recv.at[j], (ex.s, ex.partner))
+
+    def finish(self):
+        ex = self.ex
+        part = self.part(ex.partner)
+        ex.copy(part, part, self.send.at[0], self.recv.at[0], (ex.s, ex.f)).wait_recv()
+        for k in range(1, ex.ny):
+            j = ex.ny - 1 + k
+            part = self.part(((ex.y + ex.ny - k) % ex.ny) * 2 + 1 - ex.c)
+            ex.copy(part, part, self.send.at[j], self.recv.at[j], (ex.s, ex.f)).wait_recv()
+        self.own.wait()
+
+
+class Sum:
+    def __init__(self, ex, out, got, full, sems):
+        self.ex, self.out, self.got, self.full = ex, out, got, full
+        self.s1, self.r1, self.s2, self.r2 = sems
+
+    def scatter(self):
+        ex = self.ex
+        for k in range(1, ex.ns):
+            peer = ex.seq_peer(k)
+            ex.start(self.out.at[peer[0]], self.got.at[k - 1], self.s1.at[k - 1], self.r1.at[k - 1], peer)
+
+    def reduce(self):
+        ex = self.ex
+        total = self.out[ex.s].astype(F32)
+        for k in range(1, ex.ns):
+            ex.copy(self.got.at[k - 1], self.got.at[k - 1], self.s1.at[k - 1], self.r1.at[k - 1], ex.seq_peer(k)).wait_recv()
+            total = total + self.got[k - 1].astype(F32)
+        return total.astype(BF16)
+
+    def spread(self, total):
+        ex = self.ex
+        self.full[ex.s] = total
+        mine = self.full.at[ex.s]
+        for k in range(1, ex.ns):
+            ex.start(mine, mine, self.s2.at[k - 1], self.r2.at[k - 1], ex.seq_peer(k))
+
+    def finish(self):
+        ex = self.ex
+        for k in range(1, ex.ns):
+            part = self.full.at[(ex.s + ex.ns - k) % ex.ns]
+            ex.copy(part, part, self.s2.at[k - 1], self.r2.at[k - 1], ex.seq_peer(k)).wait_recv()
+
+
+def mask_rows(ids, last_id):
+    last = (ids == last_id).astype(F32)
+    row = lax.broadcasted_iota(jnp.int32, (PAD, ids.shape[1]), 0)
+    return jnp.where(row == 0, 1.0 - last, jnp.where(row == 1, last, 0.0)).astype(BF16)
+
+
+def last_lanes(ids, last_id):
+    last = (ids == last_id).astype(F32)
+    return jnp.broadcast_to(last, (128, ids.shape[1])).T > 0.5
+
+
+def put_chunks(acc_ref, out_ref, first_id, last_id, seqs):
+    heads = acc_ref.shape[0]
+    if seqs == 2:
+        out_ref[...] = acc_ref[...].astype(BF16)
+        return
+    groups = seqs // 2
+
+    def body(h, carry):
+        a = acc_ref[h]
+        v1, v2, z1, z2 = a[:64], a[64:128], a[128:129], a[129:130]
+        row = lax.broadcasted_iota(jnp.int32, (PAD, a.shape[1]), 0)
+        for g in range(groups):
+            f0, f1 = (jnp.where(first_id == 2 * g + k, 1.0, 0.0) for k in range(2))
+            l0, l1 = (jnp.where(last_id == 2 * g + k, 1.0, 0.0) for k in range(2))
+            z = jnp.where(row == 0, f0 * z1 + l0 * z2, jnp.where(row == 1, f1 * z1 + l1 * z2, 0.0))
+            out_ref[h * groups + g] = jnp.concatenate([f0 * v1 + l0 * v2, f1 * v1 + l1 * v2, z], axis=0).astype(BF16)
+        return carry
+
+    lax.fori_loop(0, heads, body, 0)
+
+
+def take_slots(full_ref, h, first_id, last_id, seqs):
+    if seqs == 2:
+        a = full_ref[h].astype(F32)
+        return a[:64], a[64:128], a[128:129], a[129:130]
+    groups = seqs // 2
+    picks = [None] * 4
+    for g in range(groups):
+        a = full_ref[h * groups + g].astype(F32)
+        for k in range(2):
+            rows, z = a[64 * k : 64 * k + 64], a[128 + k : 129 + k]
+            for which, ident in enumerate((first_id, last_id)):
+                hit = ident == 2 * g + k
+                for slot, v in ((which, rows), (2 + which, z)):
+                    term = jnp.where(hit, v, 0.0)
+                    picks[slot] = term if picks[slot] is None else picks[slot] + term
+    return picks
+
+
+def build_b(full_ref, b_ref, first_id, last_id, seqs, repeat):
+    for h in range(b_ref.shape[0]):
+        r1, r2, z1, z2 = take_slots(full_ref, h, first_id, last_id, seqs)
+        if h % 2:
+            r1, r2, z1, z2 = r2, r1, z2, z1
+        shape = r1.shape
+        if repeat:
+            z1, z2 = (jnp.broadcast_to(z, shape) for z in (z1, z2))
+        else:
+            top = lax.broadcasted_iota(jnp.int32, shape, 0) == 0
+            z1, z2 = (jnp.where(top, jnp.broadcast_to(z, shape), 0.0) for z in (z1, z2))
+        b_ref[h] = jnp.concatenate([r1, r2, z1, z2], axis=0).astype(BF16)
+
+
+def build_features(rand_ref, rbd_ref, rt_ref):
+    heads, dim, feats = rand_ref.shape
+    rbd_ref[...] = jnp.zeros_like(rbd_ref)
+    lane = lax.broadcasted_iota(jnp.int32, (feats, 128), 1)
+    for h in range(heads):
+        q, k = h // 4, h % 4
+        rbd_ref[q, dim * k : dim * k + dim, feats * k : feats * k + feats] = rand_ref[h]
+    for p in range(heads // 2):
+        both = jnp.concatenate([rand_ref[2 * p], rand_ref[2 * p + 1]], axis=0).astype(F32).T
+        for k in range(2):
+            mine = (lane < 64) if k == 0 else (lane >= 64)
+            left = jnp.where(mine, both, 0.0)
+            right = jnp.where(mine, 1.0, 0.0)
+            rt_ref[p, feats * k : feats * k + feats, :] = jnp.concatenate([left, right], axis=1).astype(BF16)
+
+
+TILED_OUT = ("out", "att", "a2", "hid", "dpre", "dmid", "dq")
+
+
+def front_kernel(
+    x_ref, dy_ref, ids_ref, rand_ref, gains_in, wk_in, wv_in, wq_in, wo_in, wu_in, wd_in,
+    out_o, att_o, a2_o, hid_o, dpre_o, dmid_o, dq_o, a1_o, ks_o, vv_o, fk_o, wq_o, wk_o, wv_o, p_o, gain_o, gg_o,
+    a1, ks, vv, fk, qs, fq, t_out, t_att, t_a2, t_hid, t_dpre, t_dmid, t_dq,
+    gains, wk, wv, wq, wo, wu, wd, rbd, rt, b_ref, acc, p_out, p_got, p_full,
+    w_send, w_recv, w_local, r_send, r_recv, g_send, g_recv, o_sem, t_sem,
+    *, micro, seqs, factor,
+):
+    ex = Exchange()
+    heads, _, feats = rand_ref.shape
+    total, width = x_ref.shape
+    toks = total // micro
+    tiles = toks // TILE
+    pairs = width // 128
+    ex.barrier()
+    pieces = []
+    for i, (shard, full) in enumerate(
+        ((gains_in, gains), (wk_in, wk), (wv_in, wv), (wq_in, wq), (wo_in, wo), (wu_in, wu), (wd_in, wd))
+    ):
+        pieces.append(Gather(ex, shard, full, w_send.at[i], w_recv.at[i], w_local.at[i]))
+    for piece in pieces:
+        piece.begin()
+    build_features(rand_ref, rbd, rt)
+    for piece in pieces[:3]:
+        piece.forward()
+    for piece in pieces[:3]:
+        piece.finish()
+    gain_rows = gains.shape[0] // ex.nf
+    both = gains[0:gain_rows, :].astype(F32)
+    for f in range(1, ex.nf):
+        both = both + gains[gain_rows * f : gain_rows * f + gain_rows, :].astype(F32)
+    gain_o[...] = both.astype(BF16)
+    g1, g2 = both[0:1], both[1:2]
+    gg_o[...] = jnp.zeros_like(gg_o)
+
+    def ident(mb):
+        if seqs == 2:
+            return 0, 1
+        return ids_ref[mb : mb + 1, 0:1], ids_ref[mb : mb + 1, toks - 1 : toks]
+
+    def ids_of(mb, t):
+        return ids_ref[mb : mb + 1, pl.ds(pl.multiple_of(t * TILE, TILE), TILE)]
+
+    outs = []
+
+    def emit(src, dst, sem):
+        c = pltpu.make_async_copy(src, dst, sem)
+        c.start()
+        outs.append(c)
+
+    sums = [
+        Sum(ex, p_out.at[mb], p_got.at[mb], p_full.at[mb], (r_send.at[mb], r_recv.at[mb], g_send.at[mb], g_recv.at[mb]))
+        for mb in range(micro)
+    ]
+    for mb in range(micro):
         acc[...] = jnp.zeros_like(acc)
-
-    normed, _ = norm_parts(x_ref[...].astype(F32))
-    a1 = (normed * g_ref[...].astype(F32)).astype(BF16)
-    a1_ref[...] = a1
-    ks = (dot(a1, wk_ref[...]) * factor).astype(BF16)
-    ks_ref[...] = ks
-    vv = dot(a1, wv_ref[...]).astype(BF16)
-    vv_ref[...] = vv
-    features(ks, rbd_ref, fk_ref, feats)
-    vt = vv.T
-    mask_t = mt_ref[...]
-    for h in range(vv.shape[1] // 64):
-        lt = summary_rows(vt[64 * h : 64 * h + 64], None, mask_t)
-        acc[h] += dot(lt, fk_ref[:, feats * h : feats * h + feats])
-
-    @pl.when(step == pl.num_programs(0) - 1)
-    def _():
-        p_ref[...] = acc[...].astype(BF16)
-
-
-def query_kernel(a1_ref, wq_ref, rbd_ref, qs_ref, fq_ref, *, feats, factor):
-    qs = (dot(a1_ref[...], wq_ref[...]) * factor).astype(BF16)
-    qs_ref[...] = qs
-    features(qs, rbd_ref, fq_ref, feats)
-
-
-def mid_kernel(
-    x_ref, dy_ref, fq_ref, qs_ref, last_ref, mt_ref, b_ref, wo_ref, g2_ref, wu_ref, wd_ref, rt_ref,
-    *refs, feats, factor, n_alias,
-):
-    out_ref, att_ref, a2_ref, hid_ref, dpre_ref, dmid_ref, dq_ref, p_ref, gg_ref, acc = refs[n_alias:]
-    step = pl.program_id(0)
-
-    @pl.when(step == 0)
-    def _():
+        first_id, last_id = ident(mb)
+
+        def keys(t, carry, mb=mb, last_id=last_id):
+            r = rows_at(t + mb * tiles, TILE)
+            normed, _ = norm_parts(x_ref[r, :].astype(F32))
+            low = (normed * g1).astype(BF16)
+            a1[r, :] = low
+            k = (dot(low, wk[...]) * factor).astype(BF16)
+            ks[r, :] = k
+            v = dot(low, wv[...]).astype(BF16)
+            vv[r, :] = v
+            features(k, rbd, fk.at[r, :], feats)
+            vt = v.T
+            mask_t = mask_rows(ids_of(mb, t), last_id)
+            for h in range(heads):
+                lt = summary_rows(vt[64 * h : 64 * h + 64], None, mask_t)
+                acc[h] += dot(lt, fk[r, feats * h : feats * h + feats])
+            return carry
+
+        lax.fori_loop(0, tiles, keys, 0)
+        put_chunks(acc, p_out.at[mb], first_id, last_id, seqs)
+        sums[mb].scatter()
+    for i, (src, dst) in enumerate(((a1, a1_o), (ks, ks_o), (vv, vv_o), (fk, fk_o))):
+        emit(src, dst, o_sem.at[i])
+    pieces[3].forward()
+    pieces[3].finish()
+
+    def queries(t, carry):
+        r = rows_at(t, TILE)
+        q = (dot(a1[r, :], wq[...]) * factor).astype(BF16)
+        qs[r, :] = q
+        features(q, rbd, fq.at[r, :], feats)
+        return carry
+
+    lax.fori_loop(0, micro * tiles, queries, 0)
+    for mb in range(micro):
+        sums[mb].spread(sums[mb].reduce())
+    for piece in pieces[4:]:
+        piece.forward()
+    for piece in pieces[4:]:
+        piece.finish()
+    for i, (src, dst) in enumerate(((wq, wq_o), (wk, wk_o), (wv, wv_o))):
+        emit(src, dst, o_sem.at[4 + i])
+    tiled = ((t_out, out_o), (t_att, att_o), (t_a2, a2_o), (t_hid, hid_o), (t_dpre, dpre_o), (t_dmid, dmid_o), (t_dq, dq_o))
+
+    def tile_copies(t, slot):
+        r = rows_at(t, TILE)
+        return [pltpu.make_async_copy(src.at[slot], dst.at[r, :], t_sem.at[slot, i]) for i, (src, dst) in enumerate(tiled)]
+
+    for mb in range(micro):
+        first_id, last_id = ident(mb)
+        sums[mb].finish()
+        build_b(p_full.at[mb], b_ref, first_id, last_id, seqs, True)
         acc[...] = jnp.zeros_like(acc)
-        gg_ref[...] = jnp.zeros_like(gg_ref)
-
-    rows = x_ref.shape[0]
-    pairs = x_ref.shape[1] // 128
-    last = last_ref[...].astype(F32) > 0.5
-    lane = lax.broadcasted_iota(jnp.int32, (rows, 128), 1)
-    sel = jnp.logical_xor(lane < 64, last)
-
-    def swap(v):
-        return jnp.where(last, pltpu.roll(v, 64, 1), v)
-
-    att_parts, inv_parts = [], []
-    for p in range(pairs):
-        base = 2 * feats * p
-        a = dot_nt(fq_ref[:, base : base + feats], b_ref[2 * p])
-        b = dot_nt(fq_ref[:, base + feats : base + 2 * feats], b_ref[2 * p + 1])
-        num = jnp.where(sel, a[:, :128], b[:, :128])
-        den = jnp.where(sel, a[:, 128:], b[:, 128:])
-        inv = 1.0 / den
-        att_parts.append(swap(num * inv))
-        inv_parts.append(swap(inv))
-    att = jnp.concatenate(att_parts, axis=1)
-    inv = jnp.concatenate(inv_parts, axis=1)
-    att_low = att.astype(BF16)
-    att_ref[...] = att_low
-    mixed = x_ref[...].astype(F32) + dot(att_low, wo_ref[...])
-    normed, rescale = norm_parts(mixed)
-    g2 = g2_ref[...].astype(F32)
-    a2 = (normed * g2).astype(BF16)
-    a2_ref[...] = a2
-    dy = dy_ref[...]
-    for j in range(wu_ref.shape[1] // 256):
-        js = slice(256 * j, 256 * j + 256)
-        pre = dot(a2, wu_ref[:, js])
-        dh = dot_nt(dy, wd_ref[js, :])
-        cdf = 0.5 * (1.0 + lax.erf(pre * 0.7071067811865476))
-        slope = cdf + pre * jnp.exp(-0.5 * pre * pre) * 0.3989422804014327
-        hid_ref[:, js] = (pre * cdf).astype(BF16)
-        dpre_ref[:, js] = (dh * slope).astype(BF16)
-    out_ref[...] = (mixed + dot(hid_ref[...], wd_ref[...])).astype(BF16)
-    da2 = dot_nt(dpre_ref[...], wu_ref[...])
-    gg_ref[...] += jnp.sum(da2 * normed, axis=0, keepdims=True)
-    dmid = dy.astype(F32) + norm_back(da2, normed, rescale, g2)
-    dmid_low = dmid.astype(BF16)
-    dmid_ref[...] = dmid_low
-    dnum = dot_nt(dmid_low, wo_ref[...]) * inv
-    dpart = -dnum * att
-    mask_t = mt_ref[...]
-    for p in range(pairs):
-        ps = slice(128 * p, 128 * p + 128)
-        d, q = dnum[:, ps], dpart[:, ps]
-        ds, qs = swap(d), swap(q)
-        la = jnp.concatenate([jnp.where(sel, ds, 0.0), jnp.where(sel, qs, 0.0)], axis=1).astype(BF16)
-        lb = jnp.concatenate([jnp.where(sel, 0.0, ds), jnp.where(sel, 0.0, qs)], axis=1).astype(BF16)
-        base = 2 * feats * p
-        fa = fq_ref[:, base : base + feats]
-        fb = fq_ref[:, base + feats : base + 2 * feats]
-        ga = (dot(la, b_ref[2 * p]) * fa.astype(F32)).astype(BF16)
-        gb = (dot(lb, b_ref[2 * p + 1]) * fb.astype(F32)).astype(BF16)
-        o = dot(jnp.concatenate([ga, gb], axis=1), rt_ref[p])
-        dq_ref[:, ps] = (factor * (o[:, :128] - qs_ref[:, ps].astype(F32) * o[:, 128:])).astype(BF16)
-        dt = d.astype(BF16).T
-        qt = q.T
-        for k, f in enumerate((fa, fb)):
-            z = jnp.sum(qt[64 * k : 64 * k + 64], axis=0, keepdims=True)
-            lt = summary_rows(dt[64 * k : 64 * k + 64], z, mask_t)
-            acc[2 * p + k] += dot(lt, f)
-
-    @pl.when(step == pl.num_programs(0) - 1)
-    def _():
-        p_ref[...] = acc[...].astype(BF16)
+
+        def mid(t, carry, mb=mb, last_id=last_id):
+            g = t + mb * tiles
+            slot = g % 2
+            r = rows_at(g, TILE)
+
+            @pl.when(g >= 2)
+            def _():
+                for c in tile_copies(g - 2, slot):
+                    c.wait()
+
+            ids = ids_of(mb, t)
+            last = last_lanes(ids, last_id)
+            mask_t = mask_rows(ids, last_id)
+            lane = lax.broadcasted_iota(jnp.int32, (TILE, 128), 1)
+            sel = jnp.logical_xor(lane < 64, last)
+
+            def swap(v):
+                return jnp.where(last, pltpu.roll(v, 64, 1), v)
+
+            att_parts, inv_parts = [], []
+            for p in range(pairs):
+                base = 2 * feats * p
+                a = dot_nt(fq[r, base : base + feats], b_ref[2 * p])
+                b = dot_nt(fq[r, base + feats : base + 2 * feats], b_ref[2 * p + 1])
+                inv = 1.0 / jnp.where(sel, a[:, 128:], b[:, 128:])
+                att_parts.append(swap(jnp.where(sel, a[:, :128], b[:, :128]) * inv))
+                inv_parts.append(swap(inv))
+            att = jnp.concatenate(att_parts, axis=1)
+            inv = jnp.concatenate(inv_parts, axis=1)
+            att_low = att.astype(BF16)
+            t_att[slot] = att_low
+            mixed = x_ref[r, :].astype(F32) + dot(att_low, wo[...])
+            normed, rescale = norm_parts(mixed)
+            a2 = (normed * g2).astype(BF16)
+            t_a2[slot] = a2
+            dy = dy_ref[r, :]
+            for j in range(wu.shape[1] // 256):
+                js = slice(256 * j, 256 * j + 256)
+                pre = dot(a2, wu[:, js])
+                dh = dot_nt(dy, wd[js, :])
+                cdf = 0.5 * (1.0 + lax.erf(pre * 0.7071067811865476))
+                slope = cdf + pre * jnp.exp(-0.5 * pre * pre) * 0.3989422804014327
+                t_hid[slot, :, js] = (pre * cdf).astype(BF16)
+                t_dpre[slot, :, js] = (dh * slope).astype(BF16)
+            t_out[slot] = (mixed + dot(t_hid[slot], wd[...])).astype(BF16)
+            da2 = dot_nt(t_dpre[slot], wu[...])
+            gg_o[...] += jnp.sum(da2 * normed, axis=0, keepdims=True)
+            dmid = dy.astype(F32) + norm_back(da2, normed, rescale, g2)
+            dmid_low = dmid.astype(BF16)
+            t_dmid[slot] = dmid_low
+            dnum = dot_nt(dmid_low, wo[...]) * inv
+            dpart = -dnum * att
+            for p in range(pairs):
+                ps = slice(128 * p, 128 * p + 128)
+                d, q = dnum[:, ps], dpart[:, ps]
+                ds, dp = swap(d), swap(q)
+                la = jnp.concatenate([jnp.where(sel, ds, 0.0), jnp.where(sel, dp, 0.0)], axis=1).astype(BF16)
+                lb = jnp.concatenate([jnp.where(sel, 0.0, ds), jnp.where(sel, 0.0, dp)], axis=1).astype(BF16)
+                base = 2 * feats * p
+                fa = fq[r, base : base + feats]
+                fb = fq[r, base + feats : base + 2 * feats]
+                ga = (dot(la, b_ref[2 * p]) * fa.astype(F32)).astype(BF16)
+                gb = (dot(lb, b_ref[2 * p + 1]) * fb.astype(F32)).astype(BF16)
+                o = dot(jnp.concatenate([ga, gb], axis=1), rt[p])
+                t_dq[slot, :, ps] = (factor * (o[:, :128] - qs[r, ps].astype(F32) * o[:, 128:])).astype(BF16)
+                dt = d.astype(BF16).T
+                qt = q.T
+                for k, f in enumerate((fa, fb)):
+                    z = jnp.sum(qt[64 * k : 64 * k + 64], axis=0, keepdims=True)
+                    lt = summary_rows(dt[64 * k : 64 * k + 64], z, mask_t)
+                    acc[2 * p + k] += dot(lt, f)
+            for c in tile_copies(g, slot):
+                c.start()
+            return carry
+
+        lax.fori_loop(0, tiles, mid, 0)
+        put_chunks(acc, p_o.at[mb], first_id, last_id, seqs)
+    last_tile = micro * tiles - 1
+    for g in (last_tile - 1, last_tile):
+        for c in tile_copies(g, g % 2):
+            c.wait()
+    for c in outs:
+        c.wait()
+    ex.drain()
+
+
+def front(x, dy, ids, rand, gains, wk, wv, wq, wo, wu, wd, *, micro, seqs, nf, ns, factor):
+    total, width = x.shape
+    heads, _, feats = rand.shape
+    hidden = wu.shape[1]
+    rows = 128 + PAD
+    chunks = heads * (seqs // 2)
+
+    def bf(*shape):
+        return jax.ShapeDtypeStruct(shape, BF16)
+
+    hbm = pl.BlockSpec(memory_space=pl.ANY)
+    vmem = pl.BlockSpec(memory_space=pltpu.VMEM)
+    out_shape = [
+        bf(total, width), bf(total, width), bf(total, width), bf(total, hidden), bf(total, hidden), bf(total, width),
+        bf(total, width), bf(total, width), bf(total, width), bf(total, width), bf(total, heads * feats),
+        bf(width, width), bf(width, width), bf(width, width), bf(micro, chunks, rows, feats),
+        bf(PAD, width), jax.ShapeDtypeStruct((1, width), F32),
+    ]
+    v = pltpu.VMEM
+    dma = pltpu.SemaphoreType.DMA
+    scratch = [v((total, width), BF16)] * 3 + [v((total, heads * feats), BF16), v((total, width), BF16), v((total, heads * feats), BF16)]
+    scratch += [v((2, TILE, width), BF16)] * 3 + [v((2, TILE, hidden), BF16)] * 2 + [v((2, TILE, width), BF16)] * 2
+    scratch += [v((nf * PAD, width), BF16)] + [v((width, width), BF16)] * 4 + [v((width, hidden), BF16), v((hidden, width), BF16)]
+    scratch += [v((heads // 4, 256, 4 * feats), BF16), v((heads // 2, 2 * feats, 256), BF16), v((heads, 256, feats), BF16)]
+    scratch += [v((heads, rows, feats), F32), v((micro, chunks, rows, feats), BF16)]
+    scratch += [v((micro, ns - 1, rows, feats), BF16), v((micro, ns, rows, feats), BF16)]
+    kinds = nf - 1
+    scratch += [dma((7, kinds)), dma((7, kinds)), dma((7,))] + [dma((micro, ns - 1))] * 4 + [dma((7,)), dma((2, 7))]
+    return pl.pallas_call(
+        functools.partial(front_kernel, micro=micro, seqs=seqs, factor=factor),
+        in_specs=[vmem] * 4 + [hbm] * 7,
+        out_specs=[hbm] * 14 + [vmem] * 3,
+        out_shape=out_shape,
+        scratch_shapes=scratch,
+        compiler_params=pltpu.CompilerParams(collective_id=0, has_side_effects=True, vmem_limit_bytes=63 << 20),
+        name="front",
+    )(x, dy, ids, rand, gains, wk, wv, wq, wo, wu, wd)
 
 
 def second_kernel(
@@ -272,13 +592,6 @@
     )(*args)
 
 
-def block_diag_features(rand):
-    heads, dim, feats = rand.shape
-    eye = jnp.eye(4, dtype=rand.dtype)
-    quads = rand.reshape(heads // 4, 4, dim, feats)
-    return jnp.einsum("qadf,ab->qadbf", quads, eye).reshape(heads // 4, 4 * dim, 4 * feats)
-
-
 def back_features(rand):
     heads, dim, feats = rand.shape
     eye = jnp.eye(2, dtype=rand.dtype)
@@ -346,61 +659,37 @@
 def per_device(block_input, seq_ids, rand, ln1_gain, w_query, w_key, w_value, w_out, ln2_gain, w_up, w_down, cotangent):
     micro, _, toks, width = block_input.shape
     heads, dim, feats = rand.shape
-    hidden = w_up.shape[1]
     factor = dim ** (-0.25)
-    seqs = max(1, lax.axis_size("seq") // 4)
+    ns, nf = lax.axis_size("seq"), lax.axis_size("fsdp")
+    seqs = max(2, ns // 4)
     tiles = toks // TILE
     x = block_input.reshape(micro * toks, width)
     dy = cotangent.reshape(micro * toks, width)
     ids = seq_ids.reshape(micro, toks)
+    shard = ln1_gain.shape[0]
+    mine = (jnp.arange(width) // shard == lax.axis_index("fsdp"))[None, :]
+    row = jnp.arange(PAD)[:, None]
+    gains = jnp.where(row == 0, jnp.tile(ln1_gain, nf)[None, :], jnp.tile(ln2_gain, nf)[None, :])
+    gains = jnp.where(jnp.logical_and(mine, row < 2), gains, jnp.zeros_like(gains))
+    out, att, a2, hid, dpre, dmid, dq, a1, ks, vv, fk, wq, wk, wv, parts, gains, g2_grad = front(
+        x, dy, ids, rand, gains, w_key, w_value, w_query, w_out, w_up, w_down,
+        micro=micro, seqs=seqs, nf=nf, ns=ns, factor=factor,
+    )
     last = (ids == (1 if seqs == 2 else ids[:, -1:])).reshape(-1)
     last_cols = jnp.broadcast_to(last.astype(BF16)[:, None], (micro * toks, 128))
-    row = jnp.arange(PAD)[:, None]
-    mask_t = jnp.where(row == 0, 1.0 - last.astype(F32), jnp.where(row == 1, last.astype(F32), 0.0)).astype(BF16)
-    rbd = block_diag_features(rand)
     rt = back_features(rand)
-    g1 = gather(ln1_gain).reshape(1, width)
-    g2 = gather(ln2_gain).reshape(1, width)
-    wq, wk, wv, wo, wu, wd = (gather(w) for w in (w_query, w_key, w_value, w_out, w_up, w_down))
+    g1 = gains[0:1]
+    grads = []
+    for mb in range(micro):
+        dense = lax.psum(parts[mb], "seq").reshape(heads, seqs // 2, 128 + PAD, feats)
+        grads.append(pick_two(dense, ids[mb], seqs))
     static = dict(feats=feats, factor=factor)
-    rows = 128 + PAD
-    summary = ((heads, rows, feats), BF16)
-    acc = pltpu.VMEM((heads, rows, feats), F32)
     unit = 2.0 * toks * 256 * 256
-
-    keep, sums = None, []
-    for mb in range(micro):
-        r = call(key_kernel, mb, tiles, [x], [g1, wk, wv, rbd, mask_t], mask_t,
-                 [width, width, width, heads * feats], [summary], [acc], keep, 24 * unit, "keys", **static)
-        keep = r[:4]
-        sums.append(pick_two(sum_seq(place(r[4], ids[mb], seqs)), ids[mb], seqs))
-    a1, ks, vv, fk = keep
-    total = micro * toks
-    qs, fq = pl.pallas_call(
-        functools.partial(query_kernel, **static),
-        grid=(micro * tiles,),
-        in_specs=[tile_spec(width, 0), whole_spec(wq.shape), whole_spec(rbd.shape)],
-        out_specs=[tile_spec(width, 0), tile_spec(heads * feats, 0)],
-        out_shape=[jax.ShapeDtypeStruct((total, width), BF16), jax.ShapeDtypeStruct((total, heads * feats), BF16)],
-        cost_estimate=pl.CostEstimate(flops=int(24 * unit), bytes_accessed=1 << 20, transcendentals=0),
-        name="queries",
-    )(a1, wq, rbd)
-    keep, grads = None, []
-    g2_grad = 0.0
-    for mb in range(micro):
-        b = expand(sums[mb], True)
-        r = call(mid_kernel, mb, tiles, [x, dy, fq, qs, last_cols], [mask_t, b, wo, g2, wu, wd, rt], mask_t,
-                 [width, width, width, hidden, hidden, width, width], [summary, ((1, width), F32)], [acc],
-                 keep, 100 * unit, "mid", **static)
-        keep = r[:7]
-        g2_grad = g2_grad + r[8]
-        grads.append(pick_two(sum_seq(place(r[7], ids[mb], seqs)), ids[mb], seqs))
-    out, att, a2, hid, dpre, dmid, dq = keep
     keep = None
     g1_grad = 0.0
     for mb in range(micro):
         b = expand(grads[mb], False)
-        r = call(second_kernel, mb, tiles, [x, dmid, fk, ks, vv, last_cols, dq], [b, g1, wq, wk, wv, rt], mask_t,
+        r = call(second_kernel, mb, tiles, [x, dmid, fk, ks, vv, last_cols, dq], [b, g1, wq, wk, wv, rt], None,
                  [width, width, width], [((1, width), F32)], [], keep, 44 * unit, "second", **static)
         keep = r[:3]
         g1_grad = g1_grad + r[3]

time: 506 us -> 444 us (0.88)
  blocking collectives: 78.8 us -> 27.9 us
  waiting for transfers between devices: 270 us -> 227 us
  Pallas kernels: 82.8 us -> 116 us
    pallas_call x1, Pallas kernels: 8.17 us -> 96.9 us  [front(): pl.pallas_call(functools.partial(front_kernel, micro=micro, seqs=seqs, fa...]
    pallas_call x6 -> x2, Pallas kernels: 74.6 us -> 18.7 us  [call(): pl.pallas_call(functools.partial(body, n_alias=n_alias, **static), grid=(...]
    all_gather x6 -> x0, blocking collectives: 50.9 us -> none  [gather(): return lax.all_gather(w, 'fsdp', axis=0, tiled=True)]
    psum x2 -> x1, waiting for transfers between devices: 116 us -> 73.2 us  [per_device(): lax.psum(parts[mb], 'seq').reshape(heads, seqs // 2, 128 + PAD, feats)]
  transfers between devices with their start and end apart: 11 -> 8, of which waited for: 7 -> 6; matrix products, arithmetic and copies ran while one was open for 8% -> 9% of each run, Pallas kernels for 5% -> 4%
where the time goes in v1:
time: 444 us
  waiting for transfers between devices  227 us (51%)
  Pallas kernels  116 us (26%)
  blocking collectives  27.9 us (6%)
  matrix products  27.5 us (6%)
  between operations  16.6 us (4%)
  local copies, waits for them, and re-layouts  14.4 us (3%)
  other arithmetic  14.2 us (3%)
    pallas_call x1, Pallas kernels, front(): pl.pallas_call(functools.partial(front_kernel, micro=micro, seqs=seqs, fa...  96.9 us
    reduce_scatter x6, waiting for transfers between devices, per_device(): lax.psum_scatter(t, 'fsdp', scatter_dimension=0, tiled=True)  93.8 us
    psum x1, waiting for transfers between devices, per_device(): lax.psum(parts[mb], 'seq').reshape(heads, seqs // 2, 128 + PAD, feats)  73.2 us
    psum x1, waiting for transfers between devices, per_device(): totals = [lax.psum(t, 'seq').astype(F32) for t in totals]  60.1 us
    dot_general x6, matrix products, weight_grad(): lax.dot_general(left, right, (((0,), (0,)), ((), ())), preferred_element_...  27.5 us
    psum x1, blocking collectives, per_device(): totals = [lax.psum(t, 'seq').astype(F32) for t in totals]  22.2 us
    pallas_call x2, Pallas kernels, call(): pl.pallas_call(functools.partial(body, n_alias=n_alias, **static), grid=(...  18.7 us
    convert_element_type x8, other arithmetic, per_device(): totals = [lax.psum(t, 'seq').astype(F32) for t in totals]  9.81 us
  transfers between devices with their start and end apart: 8, of which 6 were waited for; matrix products, arithmetic and copies ran while one was open for 9% of the time, Pallas kernels for 4%

profile of v1, /device:TPU:0, one launch (start us, length us, event | category | flops | bytes accessed | tf_op | source)
XLA Modules:
  0.0 443.8 jit_solution(292991596840731702)
XLA Ops:
  10.7 96.9 %front.1 = (bf16[1536,512]{1,0:T(8,128)(2,1)}, bf16[1536,512]{1,0:T(8,128)(2,1)}, bf16[1536,512]{1,0:T(8,128)(2,1)}, bf16[1536,2048]{1,0:T(8,128)(2,1)}, bf16[15...) custom-call(bf16[1536,512]{1,0:T(8,128)(2,1)} %bitcast.44, ...), custom_call_target="tpu_custom_call" | custom-call | tf_op jit(solution)/shard_map/front/pallas_call | solution.py:490
  107.7 2.4 slice_bitcast_fusion
  110.2 3.3 convolution_convert_fusion.2
  113.6 3.2 convolution_convert_fusion.5
  121.2 73.2 %all-reduce.15.cloned.1.call-done = (bf16[8,144,256]{2,1,0:T(8,128)(2,1)}, bf16[8,144,256]{2,1,0:T(8,128)(2,1)}) async-done(((bf16[8,144,256]{2,1,0:T(8,128)(2,1)}, bf16[8,144,256]{2,1,0:T(8,128)(2,1)}), (bf16[8,144,256]{2,1,0:T(8,128)(2,1)}, bf16[8,144,256]{2,1,0:T(8,128)(2,1)})) %all-reduce.15.cloned.1.call-update) | async-done | bytes 1179664 | tf_op jit(solution)/shard_map/psum | solution.py:684
  197.7 2.1 maximum_select_fusion.1
  200.8 9.3 %second.2 = (bf16[1536,512]{1,0:T(8,128)(2,1)}, bf16[1536,512]{1,0:T(8,128)(2,1)}, bf16[1536,512]{1,0:T(8,128)(2,1)}, f32[1,512]{1,0:T(1,128)}) custom-call(bf16[1536,512]{1,0:T(8,128)(2,1)} %bitcast.45, bf16[1536,512]{1,0:T(8,128)(2,1)} %get-tuple-element.36.dmid_ref, bf16[1536,2048]{1,0:T(8,128)(2,1)} %get-tuple-element.37.fk_ref, ...), custom_call_target="tpu_custom_call" | custom-call | flops 4429185024 | bytes 1048576 | tf_op jit(solution)/shard_map/second/pallas_call | solution.py:581
  210.1 9.3 %second.3 = (bf16[1536,512]{1,0:T(8,128)(2,1)}, bf16[1536,512]{1,0:T(8,128)(2,1)}, bf16[1536,512]{1,0:T(8,128)(2,1)}, f32[1,512]{1,0:T(1,128)}) custom-call(bf16[1536,512]{1,0:T(8,128)(2,1)} %bitcast.46, bf16[1536,512]{1,0:T(8,128)(2,1)} %get-tuple-element.36.dmid_ref, ...), custom_call_target="tpu_custom_call", output_to_operand_aliasing={{0}: (13, {}), {1}: (14, {}), {2}: (15, {})} | custom-call | flops 4429185024 | bytes 1048576 | tf_op jit(solution)/shard_map/second/pallas_call | solution.py:581
  219.4 3.3 convolution_convert_fusion.3
  222.9 1.8 convolution_convert_fusion.4
  224.7 8.2 %convolution_convert_fusion.1 = bf16[512,2048]{1,0:T(8,128)(2,1)} fusion(bf16[1536,512]{1,0:T(8,128)(2,1)} %get-tuple-element.57, bf16[1536,2048]{1,0:T(8,128)(2,1)} %get-tuple-element.58), kind=kOutput, calls=%fused_computation.1 | convolution fusion | flops 3222274048 | bytes 9961472 | tf_op jit(solution)/shard_map/dot_general | solution.py:699
  233.0 1.3 copy-done.5
  234.3 7.7 %convolution_convert_fusion = bf16[2048,512]{1,0:T(8,128)(2,1)} fusion(bf16[1536,2048]{1,0:T(8,128)(2,1)} %get-tuple-element.59, bf16[1536,512]{1,0:T(8,128)(2,1)S(1)} %bitcast.50), kind=kOutput, calls=%fused_computation | convolution fusion | flops 3222274048 | bytes 9961472 | tf_op jit(solution)/shard_map/dot_general | solution.py:699
  242.2 1.5 reduce-scatter.11.cloned.1.call-done
  243.7 24.7 %reduce-scatter.9.cloned.1.call-done = bf16[128,512]{1,0:T(8,128)(2,1)} async-done(((bf16[512,512]{1,0:T(8,128)(2,1)}), bf16[128,512]{1,0:T(8,128)(2,1)}) %reduce-scatter.9.cloned.1.call-update) | async-done | bytes 131088 | tf_op jit(solution)/shard_map/reduce_scatter | solution.py:711
  268.4 33.8 %reduce-scatter.15.cloned.1.call-done = bf16[128,2048]{1,0:T(8,128)(2,1)} async-done(((bf16[512,2048]{1,0:T(8,128)(2,1)}), bf16[128,2048]{1,0:T(8,128)(2,1)}) %reduce-scatter.15.cloned.1.call-update) | async-done | bytes 524304 | tf_op jit(solution)/shard_map/reduce_scatter | solution.py:711
  302.1 33.8 %reduce-scatter.17.cloned.1.call-done = bf16[512,512]{1,0:T(8,128)(2,1)} async-done(((bf16[2048,512]{1,0:T(8,128)(2,1)}), bf16[512,512]{1,0:T(8,128)(2,1)}) %reduce-scatter.17.cloned.1.call-update) | async-done | bytes 524304 | tf_op jit(solution)/shard_map/reduce_scatter | solution.py:711
  337.3 5.8 %all-reduce.9 = (bf16[512]{0:T(512)(128)(2,1)S(1)}, bf16[512]{0:T(512)(128)(2,1)S(1)}) all-reduce(bf16[512]{0:T(512)(128)(2,1)S(1)} %convert_reduce_fusion.1, bf16[512]{0:T(512)(128)(2,1)S(1)} %convert_reduce_fusion), channel_id=2, replica_groups=mesh['seq'=8,'fsdp'=4] {'fsdp'}, use_global_device_ids=true, to_apply=%region_2.3.clone | all-reduce | flops 1024 | bytes 4096
  343.2 22.2 %all-reduce.6 = (bf16[128]{0:T(256)(128)(2,1)S(1)}, bf16[128]{0:T(256)(128)(2,1)S(1)}) all-reduce(bf16[128]{0:T(256)(128)(2,1)S(1)} %dynamic-slice.1, bf16[128]{0:T(256)(128)(2,1)S(1)} %dynamic-slice.3), channel_id=1, replica_groups=mesh['seq'=8,'fsdp'=4] {'seq'}, use_global_device_ids=true, to_apply=%region_3.4 | all-reduce | flops 256 | bytes 1024 | tf_op jit(solution)/shard_map/psum | solution.py:712
  366.4 60.1 %all-reduce.13.cloned.1.call-done = (bf16[128,512]{1,0:T(8,128)(2,1)}, bf16[128,512]{1,0:T(8,128)(2,1)}, bf16[128,512]{1,0:T(8,128)(2,1)}, bf16[128,512]{1,0:T(8...) async-done(((bf16[128,512]{1,0:T(8,128)(2,1)}, bf16[128,512]{1,0:T(8,128)(2,1)}, bf16[128,512]{1,0:T(8,128)(2,1)}, bf16[128,512]{1,0:T(8,128)(2,1)}, ...) | async-done | bytes 1572880 | tf_op jit(solution)/shard_map/psum | solution.py:712
  426.4 1.7 convert_element_type.80
  428.2 1.6 convert_element_type.82
  429.8 1.6 convert_element_type.84
  431.4 1.6 convert_element_type.86
  (85 shorter events, 16.7 us)
Async XLA Ops:
  8.0 186.4 %all-reduce.15.cloned.1.call-start = ((), (), s32[]{:S(2)}) async-start(), calls=%async_computation.13 | async-start | bytes 2359296 | tf_op jit(solution)/shard_map/psum | solution.py:684
  107.7 2.5 copy-start.1
  110.1 132.0 %reduce-scatter.13.cloned.1.call-start = ((), (), s32[]{:S(2)}) async-start(), calls=%async_computation.9 | async-start | bytes 655360 | tf_op jit(solution)/shard_map/reduce_scatter | solution.py:711
  110.2 3.4 copy-start
  113.6 128.6 %reduce-scatter.7.cloned.1.call-start = ((), (), s32[]{:S(2)}) async-start(), calls=%async_computation.6 | async-start | bytes 655360 | tf_op jit(solution)/shard_map/reduce_scatter | solution.py:711
  113.6 3.4 copy-start.9
  113.6 3.7 copy-start.6
  116.9 126.8 %reduce-scatter.11.cloned.1.call-start = ((), (), s32[]{:S(2)}) async-start(), calls=%async_computation.8 | async-start | bytes 655360 | tf_op jit(solution)/shard_map/reduce_scatter | solution.py:711
  194.4 3.0 copy-start.3
  219.4 3.4 copy-start.2
  222.8 45.6 %reduce-scatter.9.cloned.1.call-start = ((), (), s32[]{:S(2)}) async-start(), calls=%async_computation.7 | async-start | bytes 655360 | tf_op jit(solution)/shard_map/reduce_scatter | solution.py:711
  224.7 77.5 %reduce-scatter.15.cloned.1.call-start = ((), (), s32[]{:S(2)}) async-start(), calls=%async_computation.10 | async-start | bytes 2621440 | tf_op jit(solution)/shard_map/reduce_scatter | solution.py:711
  232.9 1.4 copy-start.5
  232.9 103.0 %reduce-scatter.17.cloned.1.call-start = ((), (), s32[]{:S(2)}) async-start(), calls=%async_computation.11 | async-start | bytes 2621440 | tf_op jit(solution)/shard_map/reduce_scatter | solution.py:711
  242.0 93.9 %copy-start.13 = (u32[32]{0:T(128)S(1)}, u32[32]{0:T(128)}, u32[]{:S(2)}) copy-start(u32[32]{0:T(128)} %constant.60) | copy-start | bytes 388
  242.0 95.2 %copy-start.10 = (f32[1,512]{1,0:T(1,128)S(1)}, f32[1,512]{1,0:T(1,128)}, u32[]{:S(2)}) copy-start(f32[1,512]{1,0:T(1,128)} %get-tuple-element.56) | copy-start | bytes 6148
  242.0 95.2 %copy-start.11 = (f32[1,512]{1,0:T(1,128)S(1)}, f32[1,512]{1,0:T(1,128)}, u32[]{:S(2)}) copy-start(f32[1,512]{1,0:T(1,128)} %get-tuple-element.50) | copy-start | bytes 6148
  242.0 95.2 %copy-start.12 = (f32[1,512]{1,0:T(1,128)S(1)}, f32[1,512]{1,0:T(1,128)}, u32[]{:S(2)}) copy-start(f32[1,512]{1,0:T(1,128)} %get-tuple-element.51) | copy-start | bytes 6148
  242.0 184.4 %all-reduce.13.cloned.1.call-start = ((), (), s32[]{:S(2)}) async-start(), calls=%async_computation.12 | async-start | bytes 3145728 | tf_op jit(solution)/shard_map/psum | solution.py:712
  426.4 6.6 %copy-start.8 = (bf16[128,2048]{1,0:T(8,128)(2,1)S(1)}, bf16[128,2048]{1,0:T(8,128)(2,1)}, u32[]{:S(2)}) copy-start(bf16[128,2048]{1,0:T(8,128)(2,1)} %get-tuple-element.96) | copy-start | bytes 1572868
  426.4 7.7 %copy-start.7 = (bf16[512,512]{1,0:T(8,128)(2,1)S(1)}, bf16[512,512]{1,0:T(8,128)(2,1)}, u32[]{:S(2)}) copy-start(bf16[512,512]{1,0:T(8,128)(2,1)} %get-tuple-element.97) | copy-start | bytes 1572868
  433.1 2.2 copy-start.4
Sparse Core Ops, SparseCore 0:
  110.3 84.0 all-reduce.14
  336.1 90.3 all-reduce.12
Sparse Core Ops, SparseCore 1:
  113.6 25.3 reduce-scatter.12
  141.4 21.6 reduce-scatter.6
  222.9 20.7 reduce-scatter.10
  246.7 21.6 reduce-scatter.8
  270.9 31.2 reduce-scatter.14
  304.7 31.2 reduce-scatter.16

commit v2 on v1

--- a/solution.py
+++ b/solution.py
@@ -13,6 +13,7 @@
 F32 = jnp.float32
 BF16 = jnp.bfloat16
 PAD = 16
+SPREAD_AT = 3
 
 
 def dot(a, b):
@@ -59,7 +60,7 @@
 
 def summary_rows(rows, zrow, mask_t):
     z = mask_t if zrow is None else (mask_t.astype(F32) * zrow).astype(BF16)
-    return jnp.concatenate([rows * mask_t[0:1], rows * mask_t[1:2], z], axis=0)
+    return jnp.concatenate([rows * mask_t[0:1], z, rows * mask_t[1:2]], axis=0)
 
 
 MESH_ID = pl.DeviceIdType.MESH
@@ -147,36 +148,78 @@
 
 
 class Sum:
-    def __init__(self, ex, out, got, full, sems):
+    def __init__(self, ex, out, got, full, sems, seqs):
         self.ex, self.out, self.got, self.full = ex, out, got, full
         self.s1, self.r1, self.s2, self.r2 = sems
+        self.rows = out.shape[1]
+        self.edge = ex.ns // (2 * seqs) if seqs == 2 else 0
+        if self.edge:
+            got[...] = jnp.zeros_like(got)
+            full[...] = jnp.zeros_like(full)
+
+    def by_place(self, place, body):
+        if not self.edge:
+            body(pl.ds(0, self.rows))
+            return
+        low, high = place < self.edge, place >= self.ex.ns - self.edge
+        half = 64 + PAD
+
+        @pl.when(low)
+        def _():
+            body(pl.ds(0, half))
+
+        @pl.when(high)
+        def _():
+            body(pl.ds(64, half))
+
+        @pl.when(jnp.logical_not(jnp.logical_or(low, high)))
+        def _():
+            body(pl.ds(0, self.rows))
+
+    def others(self):
+        return range(1, self.ex.ns)
+
+    def scatter_copy(self, k, part):
+        peer = self.ex.seq_peer(k)
+        return self.ex.copy(self.out.at[peer[0], part], self.got.at[k - 1, part], self.s1.at[k - 1], self.r1.at[k - 1], peer)
+
+    def spread_copy(self, k, index, part):
+        ref = self.full.at[index, part]
+        return self.ex.copy(ref, ref, self.s2.at[k - 1], self.r2.at[k - 1], self.ex.seq_peer(k))
 
     def scatter(self):
-        ex = self.ex
-        for k in range(1, ex.ns):
-            peer = ex.seq_peer(k)
-            ex.start(self.out.at[peer[0]], self.got.at[k - 1], self.s1.at[k - 1], self.r1.at[k - 1], peer)
+        self.by_place(self.ex.s, lambda part: [self.scatter_copy(k, part).start() for k in self.others()])
+
+    def scatter_settle(self):
+        self.by_place(self.ex.s, lambda part: [self.scatter_copy(k, part).wait_send() for k in self.others()])
+
+    def from_place(self, k):
+        return (self.ex.s + self.ex.ns - k) % self.ex.ns
 
     def reduce(self):
         ex = self.ex
+        for k in self.others():
+            self.by_place(self.from_place(k), lambda part, k=k: self.scatter_copy(k, part).wait_recv())
         total = self.out[ex.s].astype(F32)
-        for k in range(1, ex.ns):
-            ex.copy(self.got.at[k - 1], self.got.at[k - 1], self.s1.at[k - 1], self.r1.at[k - 1], ex.seq_peer(k)).wait_recv()
+        for k in self.others():
             total = total + self.got[k - 1].astype(F32)
         return total.astype(BF16)
 
     def spread(self, total):
-        ex = self.ex
-        self.full[ex.s] = total
-        mine = self.full.at[ex.s]
-        for k in range(1, ex.ns):
-            ex.start(mine, mine, self.s2.at[k - 1], self.r2.at[k - 1], ex.seq_peer(k))
+        self.full[self.ex.s] = total
+        for k in self.others():
+            to = (self.ex.s + k) % self.ex.ns
+            self.by_place(to, lambda part, k=k: self.spread_copy(k, self.ex.s, part).start())
+
+    def spread_settle(self):
+        for k in self.others():
+            to = (self.ex.s + k) % self.ex.ns
+            self.by_place(to, lambda part, k=k: self.spread_copy(k, self.ex.s, part).wait_send())
 
     def finish(self):
-        ex = self.ex
-        for k in range(1, ex.ns):
-            part = self.full.at[(ex.s + ex.ns - k) % ex.ns]
-            ex.copy(part, part, self.s2.at[k - 1], self.r2.at[k - 1], ex.seq_peer(k)).wait_recv()
+        self.by_place(
+            self.ex.s, lambda part: [self.spread_copy(k, self.from_place(k), part).wait_recv() for k in self.others()]
+        )
 
 
 def mask_rows(ids, last_id):
@@ -199,13 +242,13 @@
 
     def body(h, carry):
         a = acc_ref[h]
-        v1, v2, z1, z2 = a[:64], a[64:128], a[128:129], a[129:130]
+        v1, v2, z1, z2 = a[:64], a[64 + PAD :], a[64:65], a[65:66]
         row = lax.broadcasted_iota(jnp.int32, (PAD, a.shape[1]), 0)
         for g in range(groups):
             f0, f1 = (jnp.where(first_id == 2 * g + k, 1.0, 0.0) for k in range(2))
             l0, l1 = (jnp.where(last_id == 2 * g + k, 1.0, 0.0) for k in range(2))
             z = jnp.where(row == 0, f0 * z1 + l0 * z2, jnp.where(row == 1, f1 * z1 + l1 * z2, 0.0))
-            out_ref[h * groups + g] = jnp.concatenate([f0 * v1 + l0 * v2, f1 * v1 + l1 * v2, z], axis=0).astype(BF16)
+            out_ref[h * groups + g] = jnp.concatenate([f0 * v1 + l0 * v2, z, f1 * v1 + l1 * v2], axis=0).astype(BF16)
         return carry
 
     lax.fori_loop(0, heads, body, 0)
@@ -214,13 +257,13 @@
 def take_slots(full_ref, h, first_id, last_id, seqs):
     if seqs == 2:
         a = full_ref[h].astype(F32)
-        return a[:64], a[64:128], a[128:129], a[129:130]
+        return a[:64], a[64 + PAD :], a[64:65], a[65:66]
     groups = seqs // 2
     picks = [None] * 4
     for g in range(groups):
         a = full_ref[h * groups + g].astype(F32)
         for k in range(2):
-            rows, z = a[64 * k : 64 * k + 64], a[128 + k : 129 + k]
+            rows, z = a[(64 + PAD) * k : (64 + PAD) * k + 64], a[64 + k : 65 + k]
             for which, ident in enumerate((first_id, last_id)):
                 hit = ident == 2 * g + k
                 for slot, v in ((which, rows), (2 + which, z)):
@@ -264,7 +307,7 @@
 
 def front_kernel(
     x_ref, dy_ref, ids_ref, rand_ref, gains_in, wk_in, wv_in, wq_in, wo_in, wu_in, wd_in,
-    out_o, att_o, a2_o, hid_o, dpre_o, dmid_o, dq_o, a1_o, ks_o, vv_o, fk_o, wq_o, wk_o, wv_o, p_o, gain_o, gg_o,
+    out_o, att_o, a2_o, hid_o, dpre_o, dmid_o, dq_o, a1_o, ks_o, vv_o, fk_o, wq_o, wk_o, wv_o, p_o, s_o, gain_o, gg_o,
     a1, ks, vv, fk, qs, fq, t_out, t_att, t_a2, t_hid, t_dpre, t_dmid, t_dq,
     gains, wk, wv, wq, wo, wu, wd, rbd, rt, b_ref, acc, p_out, p_got, p_full,
     w_send, w_recv, w_local, r_send, r_recv, g_send, g_recv, o_sem, t_sem,
@@ -276,6 +319,10 @@
     toks = total // micro
     tiles = toks // TILE
     pairs = width // 128
+    sums = [
+        Sum(ex, p_out.at[mb], p_got.at[mb], p_full.at[mb], (r_send.at[mb], r_recv.at[mb], g_send.at[mb], g_recv.at[mb]), seqs)
+        for mb in range(micro)
+    ]
     ex.barrier()
     pieces = []
     for i, (shard, full) in enumerate(
@@ -312,10 +359,6 @@
         c.start()
         outs.append(c)
 
-    sums = [
-        Sum(ex, p_out.at[mb], p_got.at[mb], p_full.at[mb], (r_send.at[mb], r_recv.at[mb], g_send.at[mb], g_recv.at[mb]))
-        for mb in range(micro)
-    ]
     for mb in range(micro):
         acc[...] = jnp.zeros_like(acc)
         first_id, last_id = ident(mb)
@@ -339,7 +382,8 @@
 
         lax.fori_loop(0, tiles, keys, 0)
         put_chunks(acc, p_out.at[mb], first_id, last_id, seqs)
-        sums[mb].scatter()
+        if mb == 0:
+            sums[mb].scatter()
     for i, (src, dst) in enumerate(((a1, a1_o), (ks, ks_o), (vv, vv_o), (fk, fk_o))):
         emit(src, dst, o_sem.at[i])
     pieces[3].forward()
@@ -352,9 +396,16 @@
         features(q, rbd, fq.at[r, :], feats)
         return carry
 
-    lax.fori_loop(0, micro * tiles, queries, 0)
-    for mb in range(micro):
-        sums[mb].spread(sums[mb].reduce())
+    def queries_and_sums(t, carry):
+        @pl.when(t == SPREAD_AT)
+        def _():
+            sums[0].spread(sums[0].reduce())
+            for other in sums[1:]:
+                other.scatter()
+
+        return queries(t, carry)
+
+    lax.fori_loop(0, micro * tiles, queries_and_sums, 0)
     for piece in pieces[4:]:
         piece.forward()
     for piece in pieces[4:]:
@@ -382,6 +433,13 @@
             def _():
                 for c in tile_copies(g - 2, slot):
                     c.wait()
+
+            if mb == 0:
+
+                @pl.when(t == 1)
+                def _():
+                    for other in sums[1:]:
+                        other.spread(other.reduce())
 
             ids = ids_of(mb, t)
             last = last_lanes(ids, last_id)
@@ -449,13 +507,22 @@
             return carry
 
         lax.fori_loop(0, tiles, mid, 0)
-        put_chunks(acc, p_o.at[mb], first_id, last_id, seqs)
+        if mb == 0:
+            sums[0].scatter_settle()
+            put_chunks(acc, p_out.at[0], first_id, last_id, seqs)
+            sums[0].scatter()
+        else:
+            put_chunks(acc, p_o.at[mb - 1], first_id, last_id, seqs)
+    s_o[...] = sums[0].reduce()
     last_tile = micro * tiles - 1
     for g in (last_tile - 1, last_tile):
         for c in tile_copies(g, g % 2):
             c.wait()
     for c in outs:
         c.wait()
+    for one in sums:
+        one.scatter_settle()
+        one.spread_settle()
     ex.drain()
 
 
@@ -474,7 +541,7 @@
     out_shape = [
         bf(total, width), bf(total, width), bf(total, width), bf(total, hidden), bf(total, hidden), bf(total, width),
         bf(total, width), bf(total, width), bf(total, width), bf(total, width), bf(total, heads * feats),
-        bf(width, width), bf(width, width), bf(width, width), bf(micro, chunks, rows, feats),
+        bf(width, width), bf(width, width), bf(width, width), bf(micro - 1, chunks, rows, feats), bf(rows, feats),
         bf(PAD, width), jax.ShapeDtypeStruct((1, width), F32),
     ]
     v = pltpu.VMEM
@@ -490,7 +557,7 @@
     return pl.pallas_call(
         functools.partial(front_kernel, micro=micro, seqs=seqs, factor=factor),
         in_specs=[vmem] * 4 + [hbm] * 7,
-        out_specs=[hbm] * 14 + [vmem] * 3,
+        out_specs=[hbm] * 14 + [vmem] * 4,
         out_shape=out_shape,
         scratch_shapes=scratch,
         compiler_params=pltpu.CompilerParams(collective_id=0, has_side_effects=True, vmem_limit_bytes=63 << 20),
@@ -498,162 +565,425 @@
     )(x, dy, ids, rand, gains, wk, wv, wq, wo, wu, wd)
 
 
-def second_kernel(
-    x_ref, dmid_ref, fk_ref, ks_ref, vv_ref, last_ref, dq_ref, b_ref, g1_ref, wq_ref, wk_ref, wv_ref, rt_ref,
-    *refs, feats, factor, n_alias,
+class TwoLevel:
+    def __init__(self, ex, out, got1, mid, got2, full, send, recv):
+        self.ex, self.out, self.got1, self.mid, self.got2, self.full = ex, out, got1, mid, got2, full
+        self.send, self.recv = send, recv
+        self.slow = 4 if ex.ns % 4 == 0 else 1
+        self.fast = ex.ns // self.slow
+        self.z, self.x = ex.s // self.fast, ex.s % self.fast
+        self.sent = []
+
+    def device(self, z, x):
+        return (z * self.fast + x, self.ex.f)
+
+    def fast_copy(self, phase, k, src, dst):
+        j = k - 1
+        peer = self.device(self.z, (self.x + k) % self.fast)
+        return self.ex.copy(src, dst, self.send.at[phase, j], self.recv.at[phase, j], peer)
+
+    def slow_copy(self, phase, k, src, dst):
+        j = k - 1
+        peer = self.device((self.z + k) % self.slow, self.x)
+        return self.ex.copy(src, dst, self.send.at[phase, j], self.recv.at[phase, j], peer)
+
+    def start(self, c):
+        c.start()
+        self.ex.pending.append(c)
+
+    def block(self, x):
+        return pl.ds(x * self.slow, self.slow)
+
+    def send1(self):
+        for k in range(1, self.fast):
+            src = self.out.at[self.block((self.x + k) % self.fast)]
+            self.start(self.fast_copy(0, k, src, self.got1.at[k - 1]))
+
+    def sum1(self):
+        for k in range(1, self.fast):
+            self.fast_copy(0, k, self.got1.at[k - 1], self.got1.at[k - 1]).wait_recv()
+        total = self.out[self.block(self.x)].astype(F32)
+        for k in range(1, self.fast):
+            total = total + self.got1[k - 1].astype(F32)
+        self.mid[...] = total.astype(BF16)
+        for k in range(1, self.slow):
+            self.start(self.slow_copy(1, k, self.mid.at[(self.z + k) % self.slow], self.got2.at[k - 1]))
+
+    def sum2(self):
+        for k in range(1, self.slow):
+            self.slow_copy(1, k, self.got2.at[k - 1], self.got2.at[k - 1]).wait_recv()
+        total = self.mid[self.z].astype(F32)
+        for k in range(1, self.slow):
+            total = total + self.got2[k - 1].astype(F32)
+        at = self.x * self.slow + self.z
+        self.full[at] = total.astype(BF16)
+        for k in range(1, self.slow):
+            self.start(self.slow_copy(2, k, self.full.at[at], self.full.at[at]))
+
+    def send4(self):
+        for k in range(1, self.slow):
+            part = self.full.at[self.x * self.slow + (self.z + self.slow - k) % self.slow]
+            self.slow_copy(2, k, part, part).wait_recv()
+        mine = self.full.at[self.block(self.x)]
+        for k in range(1, self.fast):
+            self.start(self.fast_copy(3, k, mine, mine))
+
+    def finish(self):
+        for k in range(1, self.fast):
+            part = self.full.at[self.block((self.x + self.fast - k) % self.fast)]
+            self.fast_copy(3, k, part, part).wait_recv()
+
+
+class Reduce:
+    def __init__(self, ex, part, rc, ry, two, send, recv):
+        self.ex, self.part, self.rc, self.ry, self.two, self.send, self.recv = ex, part, rc, ry, two, send, recv
+
+    def core_copy(self, yy):
+        ex = self.ex
+        f = yy * 2 + (1 - ex.c)
+        return ex.copy(self.part.at[f], self.rc.at[yy], self.send.at[yy], self.recv.at[yy], (ex.s, ex.partner))
+
+    def core_send(self):
+        for yy in range(self.ex.ny):
+            c = self.core_copy(yy)
+            c.start()
+            self.ex.pending.append(c)
+
+    def y_copy(self, k):
+        ex = self.ex
+        f = ex.y_to(k)
+        j = ex.ny + k - 1
+        return ex.copy(self.part.at[f], self.ry.at[k - 1], self.send.at[j], self.recv.at[j], (ex.s, f))
+
+    def core_sum(self):
+        ex = self.ex
+        for yy in range(ex.ny):
+            self.core_copy(yy).wait_recv()
+            f = yy * 2 + ex.c
+            self.part[f] = (self.part[f].astype(F32) + self.rc[yy].astype(F32)).astype(BF16)
+        for k in range(1, ex.ny):
+            c = self.y_copy(k)
+            c.start()
+            ex.pending.append(c)
+
+    def y_sum(self):
+        ex = self.ex
+        for k in range(1, ex.ny):
+            self.y_copy(k).wait_recv()
+        total = self.part[ex.f].astype(F32)
+        for k in range(1, ex.ny):
+            total = total + self.ry[k - 1].astype(F32)
+        self.two.out[...] = total.astype(BF16)
+        self.two.send1()
+
+
+def back_kernel(
+    x_in, dy_in, hid_in, dpre_in, a2_in, att_in, dmid_in, dq_in, a1_in, ks_in, vv_in, fk_in, wq_in, wk_in, wv_in,
+    ids_ref, rand_ref, gain_ref, gg_ref, s0_ref, p1_ref,
+    dx_o, g1_o, g2_o, wq_g, wk_g, wv_g, wo_g, wu_g, wd_g,
+    x, dy, blk, a2, att, dmid, dq, a1, ks, vv, fk, wq, wk, wv, dk, dv, tr, t_dx, rbd, rt, b_ref,
+    p_got, p_full,
+    part_d, rc_d, ry_d, out_d, got1_d, mid_d, got2_d, full_d,
+    part_u, rc_u, ry_u, out_u, got1_u, mid_u, got2_u, full_u,
+    part_q, rc_q, ry_q, out_q, got1_q, mid_q, got2_q, full_q,
+    part_k, rc_k, ry_k, out_k, got1_k, mid_k, got2_k, full_k,
+    gs, gr,
+    l_sem, b_sem, x_sem, r_send, r_recv, g_send, g_recv, c_send, c_recv, t_send, t_recv, n_send, n_recv,
+    *, micro, seqs, factor,
 ):
-    dx_ref, dk_ref, dv_ref, gg_ref = refs[n_alias:]
-    step = pl.program_id(0)
-
-    @pl.when(step == 0)
-    def _():
-        gg_ref[...] = jnp.zeros_like(gg_ref)
-
-    rows = x_ref.shape[0]
-    pairs = x_ref.shape[1] // 128
-    last = last_ref[...].astype(F32) > 0.5
-    lane = lax.broadcasted_iota(jnp.int32, (rows, 128), 1)
-    sel = jnp.logical_xor(lane < 64, last)
-    ones_a = jnp.where(sel, 1.0, 0.0).astype(BF16)
-    ones_b = jnp.where(sel, 0.0, 1.0).astype(BF16)
-
-    def swap(v):
-        return jnp.where(last, pltpu.roll(v, 64, 1), v)
-
-    for p in range(pairs):
-        ps = slice(128 * p, 128 * p + 128)
-        v = swap(vv_ref[:, ps].astype(F32))
-        la = jnp.concatenate([jnp.where(sel, v, 0.0).astype(BF16), ones_a], axis=1)
-        lb = jnp.concatenate([jnp.where(sel, 0.0, v).astype(BF16), ones_b], axis=1)
-        base = 2 * feats * p
-        fa = fk_ref[:, base : base + feats]
-        fb = fk_ref[:, base + feats : base + 2 * feats]
-        ga = (dot(la, b_ref[2 * p]) * fa.astype(F32)).astype(BF16)
-        gb = (dot(lb, b_ref[2 * p + 1]) * fb.astype(F32)).astype(BF16)
-        o = dot(jnp.concatenate([ga, gb], axis=1), rt_ref[p])
-        dk_ref[:, ps] = (factor * (o[:, :128] - ks_ref[:, ps].astype(F32) * o[:, 128:])).astype(BF16)
-        va = dot_nt(fa, b_ref[2 * p, :128])
-        vb = dot_nt(fb, b_ref[2 * p + 1, :128])
-        dv_ref[:, ps] = swap(jnp.where(sel, va, vb)).astype(BF16)
-    da1 = dot_nt(dq_ref[...], wq_ref[...]) + dot_nt(dk_ref[...], wk_ref[...]) + dot_nt(dv_ref[...], wv_ref[...])
-    normed, rescale = norm_parts(x_ref[...].astype(F32))
-    gg_ref[...] += jnp.sum(da1 * normed, axis=0, keepdims=True)
-    grad = norm_back(da1, normed, rescale, g1_ref[...].astype(F32))
-    dx_ref[...] = (dmid_ref[...].astype(F32) + grad).astype(BF16)
-
-
-def tile_spec(cols, off):
-    return pl.BlockSpec((TILE, cols), lambda i: (i + off, 0))
-
-
-def whole_spec(shape):
-    zeros = (0,) * len(shape)
-    return pl.BlockSpec(shape, lambda i: zeros, pipeline_mode=pl.Buffered(1))
-
-
-def anyspec():
-    return pl.BlockSpec(memory_space=pl.ANY)
-
-
-def call(body, mb, tiles, tiled, wholes, mask_t, outs_tiled, outs_whole, scratch, previous, flops, name, **static):
-    off = mb * tiles
-    total = tiled[0].shape[0]
-    in_specs = [tile_spec(a.shape[1], off) for a in tiled]
-    args = list(tiled)
-    for item in wholes:
-        if item is mask_t:
-            in_specs.append(pl.BlockSpec((PAD, TILE), lambda i: (0, i + off)))
+    ex = Exchange()
+    heads, _, feats = rand_ref.shape
+    total_rows, width = x.shape
+    toks = total_rows // micro
+    tiles = toks // TILE
+    pairs = width // 128
+    hidden = hid_in.shape[1]
+    blocks = hidden // 512
+    quarter = ex.ns // 4
+    chunk = out_d.shape[1]
+    shard = quarter * chunk
+    sems = [(r_send, r_recv, g_send.at[mb], g_recv.at[mb]) for mb in range(2)]
+    sums = [Sum(ex, p1_ref, p_got, p_full.at[mb], sems[mb], seqs) for mb in range(2)]
+
+    loads = {}
+    order = (
+        ("dy", dy_in, dy), ("a2", a2_in, a2), ("att", att_in, att), ("dmid", dmid_in, dmid), ("a1", a1_in, a1), ("dq", dq_in, dq),
+        ("vv", vv_in, vv), ("fk", fk_in, fk), ("ks", ks_in, ks), ("wq", wq_in, wq), ("wk", wk_in, wk), ("wv", wv_in, wv),
+        ("x", x_in, x),
+    )
+
+    def block_copy(src, b):
+        return pltpu.make_async_copy(src.at[:, pl.ds(pl.multiple_of(b * 512, 512), 512)], blk.at[b], b_sem.at[b])
+
+    for i, (name, src, dst) in enumerate(order):
+        loads[name] = pltpu.make_async_copy(src, dst, l_sem.at[i])
+        loads[name].start()
+        if name == "dy":
+            for b in range(blocks):
+                block_copy(hid_in, b).start()
+
+    def need(*names):
+        for name in names:
+            loads.pop(name).wait()
+
+    ex.barrier()
+    sums[1].scatter()
+    sums[0].spread(s0_ref[...])
+    groups = []
+    for i, refs in enumerate((
+        (part_d, rc_d, ry_d, out_d, got1_d, mid_d, got2_d, full_d),
+        (part_u, rc_u, ry_u, out_u, got1_u, mid_u, got2_u, full_u),
+        (part_q, rc_q, ry_q, out_q, got1_q, mid_q, got2_q, full_q),
+        (part_k, rc_k, ry_k, out_k, got1_k, mid_k, got2_k, full_k),
+    )):
+        two = TwoLevel(ex, *refs[3:], t_send.at[i], t_recv.at[i])
+        groups.append(Reduce(ex, *refs[:3], two, c_send.at[i], c_recv.at[i]))
+    down, up, query, key = groups
+    build_features(rand_ref, rbd, rt)
+
+    need("dy")
+    tr[...] = dy[...].T
+
+    def down_block(b, carry):
+        block_copy(hid_in, b).wait()
+        v = dot(tr[...], blk[b]).T
+        n = 512 // chunk
+        flat = part_d.at[b * n // ex.ns] if n == ex.ns else None
+        v = v.reshape(n, chunk, width).astype(BF16)
+        if flat is not None:
+            flat[...] = v
         else:
-            in_specs.append(whole_spec(item.shape))
-        args.append(item)
-    out_shape = [jax.ShapeDtypeStruct((total, c), BF16) for c in outs_tiled]
-    out_specs = [tile_spec(c, off) for c in outs_tiled]
-    for shape, dtype in outs_whole:
-        out_shape.append(jax.ShapeDtypeStruct(shape, dtype))
-        out_specs.append(pl.BlockSpec(shape, functools.partial(lambda n, i: (0,) * n, len(shape))))
-    alias = {}
-    if previous is not None:
-        for k, a in enumerate(previous):
-            alias[len(args)] = k
-            args.append(a)
-            in_specs.append(anyspec())
-    n_alias = 0 if previous is None else len(previous)
+            per = n // ex.ns
+            for i in range(per):
+                part_d[b * per + i] = v[i * ex.ns : (i + 1) * ex.ns]
+        block_copy(dpre_in, b).start()
+        return carry
+
+    lax.fori_loop(0, blocks, down_block, 0)
+    down.core_send()
+    need("a2")
+    tr[...] = a2[...].T
+
+    def up_block(b, carry):
+        block_copy(dpre_in, b).wait()
+        v = dot(tr[...], blk[b])
+        for f in range(ex.nf):
+            one = v[f * shard : (f + 1) * shard].reshape(quarter, chunk, 512)
+            part_u[f, pl.ds(b * quarter, quarter)] = one.astype(BF16)
+        return carry
+
+    lax.fori_loop(0, blocks, up_block, 0)
+    up.core_send()
+    sums[1].spread(sums[1].reduce())
+    down.core_sum()
+
+    def small(left_t, right, group, which):
+        v = dot(left_t, right)
+        for half in range(2):
+            for f in range(ex.nf):
+                one = v[f * shard : (f + 1) * shard, 256 * half : 256 * half + 256].reshape(quarter, chunk, 256)
+                group.part[f, quarter * (2 * which + half) : quarter * (2 * which + half + 1)] = one.astype(BF16)
+
+    need("att", "dmid")
+    small(att[...].T, dmid[...], query, 1)
+    need("a1", "dq")
+    tr[...] = a1[...].T
+    small(tr[...], dq[...], query, 0)
+    query.core_send()
+    up.core_sum()
+    need("vv", "fk", "ks")
+
+    def ident(mb):
+        if seqs == 2:
+            return 0, 1
+        return ids_ref[mb : mb + 1, 0:1], ids_ref[mb : mb + 1, toks - 1 : toks]
+
+    def kv_part(mb):
+        first_id, last_id = ident(mb)
+        build_b(p_full.at[mb], b_ref, first_id, last_id, seqs, False)
+
+        def body(t, carry):
+            r = rows_at(t + mb * tiles, TILE)
+            ids = ids_ref[mb : mb + 1, pl.ds(pl.multiple_of(t * TILE, TILE), TILE)]
+            last = last_lanes(ids, last_id)
+            lane = lax.broadcasted_iota(jnp.int32, (TILE, 128), 1)
+            sel = jnp.logical_xor(lane < 64, last)
+            ones_a = jnp.where(sel, 1.0, 0.0).astype(BF16)
+            ones_b = jnp.where(sel, 0.0, 1.0).astype(BF16)
+
+            def swap(v):
+                return jnp.where(last, pltpu.roll(v, 64, 1), v)
+
+            for p in range(pairs):
+                ps = slice(128 * p, 128 * p + 128)
+                v = swap(vv[r, ps].astype(F32))
+                la = jnp.concatenate([jnp.where(sel, v, 0.0).astype(BF16), ones_a], axis=1)
+                lb = jnp.concatenate([jnp.where(sel, 0.0, v).astype(BF16), ones_b], axis=1)
+                base = 2 * feats * p
+                fa = fk[r, base : base + feats]
+                fb = fk[r, base + feats : base + 2 * feats]
+                ga = (dot(la, b_ref[2 * p]) * fa.astype(F32)).astype(BF16)
+                gb = (dot(lb, b_ref[2 * p + 1]) * fb.astype(F32)).astype(BF16)
+                o = dot(jnp.concatenate([ga, gb], axis=1), rt[p])
+                dk[r, ps] = (factor * (o[:, :128] - ks[r, ps].astype(F32) * o[:, 128:])).astype(BF16)
+                va = dot_nt(fa, b_ref[2 * p, :128])
+                vb = dot_nt(fb, b_ref[2 * p + 1, :128])
+                dv[r, ps] = swap(jnp.where(sel, va, vb)).astype(BF16)
+            return carry
+
+        lax.fori_loop(0, tiles, body, 0)
+
+    g1 = gain_ref[0:1].astype(F32)
+    gs[...] = jnp.zeros_like(gs)
+    gs[0, 1:2, :] = gg_ref[...]
+
+    def dx_copy(g, slot):
+        return pltpu.make_async_copy(t_dx.at[slot], dx_o.at[rows_at(g, TILE), :], x_sem.at[slot])
+
+    def x_part(mb):
+        def body(t, carry):
+            g = t + mb * tiles
+            slot = g % 2
+            r = rows_at(g, TILE)
+
+            @pl.when(g >= 2)
+            def _():
+                dx_copy(g - 2, slot).wait()
+
+            da1 = dot_nt(dq[r, :], wq[...]) + dot_nt(dk[r, :], wk[...]) + dot_nt(dv[r, :], wv[...])
+            normed, rescale = norm_parts(x[r, :].astype(F32))
+            gs[0, 0:1, :] += jnp.sum(da1 * normed, axis=0, keepdims=True)
+            t_dx[slot] = (dmid[r, :].astype(F32) + norm_back(da1, normed, rescale, g1)).astype(BF16)
+            dx_copy(g, slot).start()
+            return carry
+
+        lax.fori_loop(0, tiles, body, 0)
+
+    sums[0].finish()
+    kv_part(0)
+    down.y_sum()
+    query.core_sum()
+    need("wq", "wk", "wv", "x")
+    x_part(0)
+    down.two.sum1()
+    sums[1].finish()
+    kv_part(1)
+    small(tr[...], dk[...], key, 0)
+    small(tr[...], dv[...], key, 1)
+    key.core_send()
+    up.y_sum()
+    down.two.sum2()
+    key.core_sum()
+    query.y_sum()
+    up.two.sum1()
+    x_part(1)
+    def gain_copy(level, j, peer):
+        return ex.copy(gs.at[level], gr.at[j], n_send.at[j], n_recv.at[j], peer)
+
+    def gain_level(level, jobs):
+        for j, peer in jobs:
+            gain_copy(level, j, peer).start()
+        return jobs
+
+    def gain_sum(level, jobs):
+        total = gs[level]
+        for j, peer in jobs:
+            gain_copy(level, j, peer).wait_recv()
+            total = total + gr[j]
+        return total
+
+    jobs0 = gain_level(0, [(0, (ex.s, ex.partner))])
+    down.two.send4()
+    key.y_sum()
+    gs[1] = gain_sum(0, jobs0)
+    jobs1 = gain_level(1, [(k, (ex.s, ex.y_to(k))) for k in range(1, ex.ny)])
+    query.two.sum1()
+    up.two.sum2()
+    down.two.finish()
+    wd_g[...] = full_d[...].astype(F32).reshape(wd_g.shape)
+    gs[2] = gain_sum(1, jobs1)
+    jobs2 = gain_level(2, [(ex.ny - 1 + k, ex.seq_peer(k)) for k in range(1, ex.ns)])
+    key.two.sum1()
+    query.two.sum2()
+    up.two.send4()
+    key.two.sum2()
+    query.two.send4()
+    up.two.finish()
+    for b in range(blocks):
+        wu_g[:, 512 * b : 512 * b + 512] = full_u[quarter * b : quarter * b + quarter].astype(F32).reshape(shard, 512)
+    gains = gain_sum(2, jobs2)
+    mine = jnp.zeros((gains.shape[0], shard), F32)
+    for f in range(ex.nf):
+        mine = mine + jnp.where(ex.f == f, gains[:, f * shard : f * shard + shard], 0.0)
+    g1_o[...] = mine[0:1]
+    g2_o[...] = mine[1:2]
+    key.two.send4()
+
+    def finish(group, full, refs):
+        group.two.finish()
+        for which, ref in enumerate(refs):
+            for half in range(2):
+                i = quarter * (2 * which + half)
+                ref[:, 256 * half : 256 * half + 256] = full[i : i + quarter].astype(F32).reshape(shard, 256)
+
+    finish(query, full_q, (wq_g, wo_g))
+    finish(key, full_k, (wk_g, wv_g))
+    last = micro * tiles - 1
+    for g in (last - 1, last):
+        dx_copy(g, g % 2).wait()
+    for level, jobs in enumerate((jobs0, jobs1, jobs2)):
+        for j, peer in jobs:
+            gain_copy(level, j, peer).wait_send()
+    sums[1].scatter_settle()
+    for one in sums:
+        one.spread_settle()
+    ex.drain()
+
+
+def back(big, small, *, micro, seqs, nf, ns, shard, factor):
+    x, _, hid = big[:3]
+    rand = small[1]
+    total, width = x.shape
+    heads, _, feats = rand.shape
+    rows = 128 + PAD
+    hidden = hid.shape[1]
+    ny = nf // 2
+    slow = 4 if ns % 4 == 0 else 1
+    fast = ns // slow
+    chunk = 4 * shard // ns
+    hbm = pl.BlockSpec(memory_space=pl.ANY)
+    vmem = pl.BlockSpec(memory_space=pltpu.VMEM)
+    v = pltpu.VMEM
+    dma = pltpu.SemaphoreType.DMA
+
+    def f32(*shape):
+        return jax.ShapeDtypeStruct(shape, F32)
+
+    out_shape = [jax.ShapeDtypeStruct((total, width), BF16), f32(1, shard), f32(1, shard)]
+    out_shape += [f32(shard, width)] * 4 + [f32(shard, hidden), f32(hidden // nf, width)]
+    token = v((total, width), BF16)
+    scratch = [token, token, v((hidden // 512, total, 512), BF16), token, token, token, token, token, token, token]
+    scratch += [v((total, heads * feats), BF16)] + [v((width, width), BF16)] * 3 + [token, token, v((width, total), BF16)]
+    scratch += [v((2, TILE, width), BF16), v((heads // 4, 256, 4 * feats), BF16), v((heads // 2, 2 * feats, 256), BF16)]
+    scratch += [v((heads, 256, feats), BF16), v((ns - 1, rows, feats), BF16), v((2, ns, rows, feats), BF16)]
+    for cols in (512, 512, 256, 256):
+        scratch += [v((nf, ns, chunk, cols), BF16), v((ny, ns, chunk, cols), BF16), v((ny - 1, ns, chunk, cols), BF16)]
+        scratch += [v((ns, chunk, cols), BF16), v((fast - 1, slow, chunk, cols), BF16), v((slow, chunk, cols), BF16)]
+        scratch += [v((slow - 1, chunk, cols), BF16), v((ns, chunk, cols), BF16)]
+    jobs = 1 + (ny - 1) + (ns - 1)
+    scratch += [v((3, 8, width), F32), v((jobs, 8, width), F32)]
+    peers = max(fast, slow) - 1
+    scratch += [dma((13,)), dma((hidden // 512,)), dma((2,)), dma((ns - 1,)), dma((ns - 1,)), dma((2, ns - 1)), dma((2, ns - 1))]
+    scratch += [dma((4, 2 * ny - 1))] * 2 + [dma((4, 4, peers))] * 2 + [dma((jobs,))] * 2
     return pl.pallas_call(
-        functools.partial(body, n_alias=n_alias, **static),
-        grid=(tiles,),
-        in_specs=in_specs,
-        out_specs=out_specs,
+        functools.partial(back_kernel, micro=micro, seqs=seqs, factor=factor),
+        in_specs=[hbm] * len(big) + [vmem] * len(small),
+        out_specs=[hbm] + [vmem] * 8,
         out_shape=out_shape,
         scratch_shapes=scratch,
-        input_output_aliases=alias,
-        compiler_params=pltpu.CompilerParams(dimension_semantics=("arbitrary",)),
-        cost_estimate=pl.CostEstimate(flops=int(flops), bytes_accessed=1 << 20, transcendentals=0),
-        name=name,
-    )(*args)
-
-
-def back_features(rand):
-    heads, dim, feats = rand.shape
-    eye = jnp.eye(2, dtype=rand.dtype)
-    pairs = rand.reshape(heads // 2, 2, dim, feats)
-    left = jnp.einsum("padf,ab->pafbd", pairs, eye).reshape(heads // 2, 2 * feats, 2 * dim)
-    right = jnp.broadcast_to(eye[None, :, None, :, None], (heads // 2, 2, feats, 2, dim))
-    return jnp.concatenate([left, right.reshape(left.shape).astype(left.dtype)], axis=2)
-
-
-def expand(pick, repeat):
-    heads, _, feats = pick.shape
-    first, second = pick[:, :64], pick[:, 64:128]
-    z1, z2 = pick[:, 128:129], pick[:, 129:130]
-    if repeat:
-        z1, z2 = (jnp.broadcast_to(z, (heads, 64, feats)) for z in (z1, z2))
-    else:
-        z1, z2 = (jnp.pad(z, ((0, 0), (0, 63), (0, 0))) for z in (z1, z2))
-    even = jnp.concatenate([first, second, z1, z2], axis=1)
-    odd = jnp.concatenate([second, first, z2, z1], axis=1)
-    parity = (jnp.arange(heads) % 2 == 0)[:, None, None]
-    return jnp.where(parity, even, odd)
-
-
-def place(local, ids, seqs):
-    if seqs == 2:
-        return local[:, None]
-    slots = jnp.arange(seqs, dtype=jnp.int32)
-    first = (slots == ids[0]).astype(BF16).reshape(1, seqs // 2, 2, 1, 1)
-    last = (slots == ids[-1]).astype(BF16).reshape(1, seqs // 2, 2, 1, 1)
-    heads, _, feats = local.shape
-    rows = local[:, :128].reshape(heads, 1, 2, 64, feats)
-    z = local[:, 128:130].reshape(heads, 1, 2, 1, feats)
-
-    def put(v):
-        return first * v[:, :, 0:1] + last * v[:, :, 1:2]
-
-    body = put(rows).reshape(heads, seqs // 2, 128, feats)
-    tail = jnp.pad(put(z).reshape(heads, seqs // 2, 2, feats), ((0, 0), (0, 0), (0, PAD - 2), (0, 0)))
-    return jnp.concatenate([body, tail], axis=2)
-
-
-def pick_two(dense, ids, seqs):
-    if seqs == 2:
-        return dense[:, 0]
-    heads, _, _, feats = dense.shape
-    rows = dense[:, :, :128].reshape(heads, seqs, 64, feats)
-    z = dense[:, :, 128:130].reshape(heads, seqs, 1, feats)
-
-    def get(k):
-        return (lax.dynamic_index_in_dim(rows, k, 1, False), lax.dynamic_index_in_dim(z, k, 1, False))
-
-    r1, z1 = get(ids[0])
-    r2, z2 = get(ids[-1])
-    return jnp.pad(jnp.concatenate([r1, r2, z1, z2], axis=1), ((0, 0), (0, PAD - 2), (0, 0)))
-
-
-def sum_seq(dense):
-    return lax.psum(dense, "seq")
-
-
-def gather(w):
-    return lax.all_gather(w, "fsdp", axis=0, tiled=True)
+        compiler_params=pltpu.CompilerParams(collective_id=1, has_side_effects=True, vmem_limit_bytes=63 << 20),
+        name="back",
+    )(*big, *small)
 
 
 def per_device(block_input, seq_ids, rand, ln1_gain, w_query, w_key, w_value, w_out, ln2_gain, w_up, w_down, cotangent):
@@ -671,47 +1001,17 @@
     row = jnp.arange(PAD)[:, None]
     gains = jnp.where(row == 0, jnp.tile(ln1_gain, nf)[None, :], jnp.tile(ln2_gain, nf)[None, :])
     gains = jnp.where(jnp.logical_and(mine, row < 2), gains, jnp.zeros_like(gains))
-    out, att, a2, hid, dpre, dmid, dq, a1, ks, vv, fk, wq, wk, wv, parts, gains, g2_grad = front(
+    out, att, a2, hid, dpre, dmid, dq, a1, ks, vv, fk, wq, wk, wv, part, total, gains, gg = front(
         x, dy, ids, rand, gains, w_key, w_value, w_query, w_out, w_up, w_down,
         micro=micro, seqs=seqs, nf=nf, ns=ns, factor=factor,
     )
-    last = (ids == (1 if seqs == 2 else ids[:, -1:])).reshape(-1)
-    last_cols = jnp.broadcast_to(last.astype(BF16)[:, None], (micro * toks, 128))
-    rt = back_features(rand)
-    g1 = gains[0:1]
-    grads = []
-    for mb in range(micro):
-        dense = lax.psum(parts[mb], "seq").reshape(heads, seqs // 2, 128 + PAD, feats)
-        grads.append(pick_two(dense, ids[mb], seqs))
-    static = dict(feats=feats, factor=factor)
-    unit = 2.0 * toks * 256 * 256
-    keep = None
-    g1_grad = 0.0
-    for mb in range(micro):
-        b = expand(grads[mb], False)
-        r = call(second_kernel, mb, tiles, [x, dmid, fk, ks, vv, last_cols, dq], [b, g1, wq, wk, wv, rt], None,
-                 [width, width, width], [((1, width), F32)], [], keep, 44 * unit, "second", **static)
-        keep = r[:3]
-        g1_grad = g1_grad + r[3]
-    dx, dk, dv = keep
-
-    def weight_grad(left, right):
-        return lax.dot_general(left, right, (((0,), (0,)), ((), ())), preferred_element_type=F32).astype(BF16)
-
-    totals = (
-        g1_grad.reshape(-1).astype(BF16),
-        weight_grad(a1, dq),
-        weight_grad(a1, dk),
-        weight_grad(a1, dv),
-        weight_grad(att, dmid),
-        g2_grad.reshape(-1).astype(BF16),
-        weight_grad(a2, dpre),
-        weight_grad(hid, dy),
+    dx, g1g, g2g, wqg, wkg, wvg, wog, wug, wdg = back(
+        [x, dy, hid, dpre, a2, att, dmid, dq, a1, ks, vv, fk, wq, wk, wv],
+        [ids, rand, gains, gg, total, part[0]],
+        micro=micro, seqs=seqs, nf=nf, ns=ns, shard=shard, factor=factor,
     )
-    totals = [lax.psum_scatter(t, "fsdp", scatter_dimension=0, tiled=True) for t in totals]
-    totals = [lax.psum(t, "seq").astype(F32) for t in totals]
     shape = block_input.shape
-    return (out.reshape(shape), dx.reshape(shape), *totals)
+    return (out.reshape(shape), dx.reshape(shape), g1g[0], wqg, wkg, wvg, wog, g2g[0], wug, wdg)
 
 
 def solution(mesh):

time: 444 us -> 188 us (0.42)
  waiting for transfers between devices: 227 us -> 0 us
  Pallas kernels: 116 us -> 175 us
  blocking collectives: 27.9 us -> 0 us
  matrix products: 27.5 us -> 0 us
  between operations: 16.6 us -> 0.71 us
  other arithmetic: 14.2 us -> 0.69 us
    psum x2 -> x0, waiting for transfers between devices: 133 us -> none  [the longest x1 73.2 us: per_device(): lax.psum(parts[mb], 'seq').reshape(heads, seqs // 2, 128 + PAD, feats)]
    reduce_scatter x6 -> x0, waiting for transfers between devices: 93.8 us -> none  [per_device(): lax.psum_scatter(t, 'fsdp', scatter_dimension=0, tiled=True)]
    pallas_call x2 -> x1, Pallas kernels: 18.7 us -> 94 us  [back(): pl.pallas_call(functools.partial(back_kernel, micro=micro, seqs=seqs, fac...]
    dot_general x6 -> x0, matrix products: 27.5 us -> none  [weight_grad(): lax.dot_general(left, right, (((0,), (0,)), ((), ())), preferred_element_...]
    psum x1 -> x0, blocking collectives: 22.2 us -> none  [per_device(): totals = [lax.psum(t, 'seq').astype(F32) for t in totals]]
    pallas_call x1, Pallas kernels: 96.9 us -> 80.5 us  [front(): pl.pallas_call(functools.partial(front_kernel, micro=micro, seqs=seqs, fa...]
    convert_element_type x11 -> x0, other arithmetic: 9.88 us -> none  [the longest x8 9.81 us: per_device(): totals = [lax.psum(t, 'seq').astype(F32) for t in totals]]
    unnamed x34 -> x29, local copies, waits for them, and re-layouts: 4.57 us -> 11 us
  transfers between devices with their start and end apart: 8 -> 0, of which waited for: 6 -> 0; matrix products, arithmetic and copies ran while one was open for 9% -> 0% of each run, Pallas kernels for 4% -> 0%
where the time goes in v2:
time: 188 us
  Pallas kernels  175 us (93%)
  local copies, waits for them, and re-layouts  11.7 us (6%)
    pallas_call x1, Pallas kernels, back(): pl.pallas_call(functools.partial(back_kernel, micro=micro, seqs=seqs, fac...  94 us
    pallas_call x1, Pallas kernels, front(): pl.pallas_call(functools.partial(front_kernel, micro=micro, seqs=seqs, fa...  80.5 us
    unnamed x29, local copies, waits for them, and re-layouts  11 us

profile of v2, /device:TPU:0, one launch (start us, length us, event | category | flops | bytes accessed | tf_op | source)
XLA Modules:
  0.0 187.7 jit_solution(15047923443250419586)
XLA Ops:
  0.7 0.7 broadcast_bitcast_fusion
  1.3 1.3 copy.26
  2.6 0.7 and_select_fusion.gains_in
  3.3 80.5 %front.1 = (bf16[1536,512]{1,0:T(8,128)(2,1)}, bf16[1536,512]{1,0:T(8,128)(2,1)}, bf16[1536,512]{1,0:T(8,128)(2,1)}, bf16[1536,2048]{1,0:T(8,128)(2,1)}, bf16[15...) custom-call(bf16[1536,512]{1,0:T(8,128)(2,1)} %bitcast.18, ...), custom_call_target="tpu_custom_call" | custom-call | tf_op jit(solution)/shard_map/front/pallas_call | solution.py:557
  83.9 94.0 %back.1 = (bf16[1536,512]{1,0:T(8,128)(2,1)}, f32[1,128]{1,0:T(1,128)}, f32[1,128]{1,0:T(1,128)}, f32[128,512]{1,0:T(8,128)}, f32[128,512]{1,0:T(8,128)}, /*inde...) custom-call(bf16[1536,512]{1,0:T(8,128)(2,1)} %bitcast.19, ...), custom_call_target="tpu_custom_call" | custom-call | tf_op jit(solution)/shard_map/back/pallas_call | solution.py:978
  177.9 0.0 copy-start
  177.9 2.8 %copy.37 = bf16[2,1,768,512]{3,2,1,0:T(8,128)(2,1)} copy(bf16[2,1,768,512]{3,2,1,0:T(8,128)(2,1)} %bitcast.22) | data formatting | bytes 3145728
  180.7 0.0 copy-done
  180.7 0.0 copy-start.4
  180.7 1.1 copy.38
  181.9 0.0 copy-done.8
  181.9 0.5 copy.39
  182.4 0.0 copy-done.6
  182.4 0.7 copy.40
  183.1 0.0 copy-done.5
  183.1 0.7 copy.41
  183.8 0.0 copy-done.4
  183.8 0.7 copy.42
  184.5 0.0 copy-done.3
  184.5 0.7 copy.43
  185.2 0.0 copy-done.7
  185.2 0.5 copy.44
  185.7 1.0 copy.45
  186.7 1.0 copy.46
  (11 shorter events, 0.0 us)
Async XLA Ops:
  177.9 2.8 %copy-start = (bf16[1536,512]{1,0:T(8,128)(2,1)S(1)}, bf16[1536,512]{1,0:T(8,128)(2,1)}, u32[]{:S(2)}) copy-start(bf16[1536,512]{1,0:T(8,128)(2,1)} %get-tuple-element.55) | copy-start | bytes 4718596
  180.7 1.2 copy-start.8
  180.7 1.7 copy-start.6
  180.7 2.4 %copy-start.5 = (f32[128,512]{1,0:T(8,128)S(1)}, f32[128,512]{1,0:T(8,128)}, u32[]{:S(2)}) copy-start(f32[128,512]{1,0:T(8,128)} %get-tuple-element.92) | copy-start | bytes 786436
  180.7 3.1 %copy-start.4 = (f32[128,512]{1,0:T(8,128)S(1)}, f32[128,512]{1,0:T(8,128)}, u32[]{:S(2)}) copy-start(f32[128,512]{1,0:T(8,128)} %get-tuple-element.93) | copy-start | bytes 786436
  181.9 2.6 %copy-start.3 = (f32[128,512]{1,0:T(8,128)S(1)}, f32[128,512]{1,0:T(8,128)}, u32[]{:S(2)}) copy-start(f32[128,512]{1,0:T(8,128)} %get-tuple-element.94) | copy-start | bytes 786436
  181.9 3.3 %copy-start.7 = (f32[1,128]{1,0:T(1,128)S(1)}, f32[1,128]{1,0:T(1,128)}, u32[]{:S(2)}) copy-start(f32[1,128]{1,0:T(1,128)} %get-tuple-element.61) | copy-start | bytes 1540
  181.9 3.9 %copy-start.2 = (f32[128,2048]{1,0:T(8,128)S(1)}, f32[128,2048]{1,0:T(8,128)}, u32[]{:S(2)}) copy-start(f32[128,2048]{1,0:T(8,128)} %get-tuple-element.96) | copy-start | bytes 3145732
  183.8 2.9 %copy-start.1 = (f32[512,512]{1,0:T(8,128)S(1)}, f32[512,512]{1,0:T(8,128)}, u32[]{:S(2)}) copy-start(f32[512,512]{1,0:T(8,128)} %get-tuple-element.97) | copy-start | bytes 3145732

commit v3 on v2

--- a/solution.py
+++ b/solution.py
@@ -88,13 +88,20 @@
     def y_to(self, k):
         return ((self.y + k) % self.ny) * 2 + self.c
 
-    def barrier(self):
+    def greet(self):
         sem = pltpu.get_barrier_semaphore()
         peers = [self.seq_peer(k) for k in range(1, self.ns)]
         peers += [(self.s, self.partner)] + [(self.s, self.y_to(k)) for k in range(1, self.ny)]
         for peer in peers:
             pl.semaphore_signal(sem, inc=1, device_id=peer, device_id_type=MESH_ID)
-        pl.semaphore_wait(sem, len(peers))
+        self.peers = len(peers)
+
+    def meet(self):
+        pl.semaphore_wait(pltpu.get_barrier_semaphore(), self.peers)
+
+    def barrier(self):
+        self.greet()
+        self.meet()
 
     def copy(self, src, dst, send, recv, peer):
         return pltpu.make_async_remote_copy(
@@ -102,13 +109,15 @@
         )
 
     def start(self, *args):
-        c = self.copy(*args)
-        c.start()
-        self.pending.append(c)
+        self.launch(lambda: self.copy(*args))
+
+    def launch(self, make):
+        make().start()
+        self.pending.append(make)
 
     def drain(self):
-        for c in self.pending:
-            c.wait_send()
+        for make in self.pending:
+            make().wait_send()
         self.pending = []
 
 
@@ -151,75 +160,77 @@
     def __init__(self, ex, out, got, full, sems, seqs):
         self.ex, self.out, self.got, self.full = ex, out, got, full
         self.s1, self.r1, self.s2, self.r2 = sems
-        self.rows = out.shape[1]
-        self.edge = ex.ns // (2 * seqs) if seqs == 2 else 0
-        if self.edge:
+        self.sparse = seqs == 2
+        self.edge = ex.ns // (2 * seqs)
+        if self.sparse:
             got[...] = jnp.zeros_like(got)
             full[...] = jnp.zeros_like(full)
 
-    def by_place(self, place, body):
-        if not self.edge:
-            body(pl.ds(0, self.rows))
+    def holds(self, chunk, device):
+        return device < self.ex.ns - self.edge if chunk < self.ex.ns // 2 else device >= self.edge
+
+    def chunks_of(self, device):
+        return self.order(device, [o for o in range(self.ex.ns) if o != device and self.holds(o, device)])
+
+    def devices_of(self, chunk):
+        return self.order(chunk, [d for d in range(self.ex.ns) if d != chunk and self.holds(chunk, d)])
+
+    def order(self, device, others):
+        return sorted(others, key=lambda d: (-abs(d // 2 - device // 2), (d - device) % self.ex.ns))
+
+    def each(self, peers, body):
+        ex = self.ex
+        if not self.sparse:
+            for k in range(1, ex.ns):
+                body((ex.s + k) % ex.ns)
             return
-        low, high = place < self.edge, place >= self.ex.ns - self.edge
-        half = 64 + PAD
-
-        @pl.when(low)
-        def _():
-            body(pl.ds(0, half))
-
-        @pl.when(high)
-        def _():
-            body(pl.ds(64, half))
-
-        @pl.when(jnp.logical_not(jnp.logical_or(low, high)))
-        def _():
-            body(pl.ds(0, self.rows))
-
-    def others(self):
-        return range(1, self.ex.ns)
-
-    def scatter_copy(self, k, part):
-        peer = self.ex.seq_peer(k)
-        return self.ex.copy(self.out.at[peer[0], part], self.got.at[k - 1, part], self.s1.at[k - 1], self.r1.at[k - 1], peer)
-
-    def spread_copy(self, k, index, part):
-        ref = self.full.at[index, part]
-        return self.ex.copy(ref, ref, self.s2.at[k - 1], self.r2.at[k - 1], self.ex.seq_peer(k))
+        for device in range(ex.ns):
+
+            @pl.when(ex.s == device)
+            def _(device=device):
+                for peer in peers(device):
+                    body(peer)
+
+    def out_copy(self, peer):
+        ex = self.ex
+        return ex.copy(self.out.at[peer], self.got.at[ex.s], self.s1.at[peer], self.r1.at[ex.s], (peer, ex.f))
+
+    def got_copy(self, peer):
+        ref = self.got.at[peer]
+        return self.ex.copy(ref, ref, self.s1.at[peer], self.r1.at[peer], (peer, self.ex.f))
+
+    def spread_copy(self, peer):
+        ex = self.ex
+        ref = self.full.at[ex.s]
+        return ex.copy(ref, ref, self.s2.at[peer], self.r2.at[ex.s], (peer, ex.f))
+
+    def full_copy(self, peer):
+        ref = self.full.at[peer]
+        return self.ex.copy(ref, ref, self.s2.at[peer], self.r2.at[peer], (peer, self.ex.f))
 
     def scatter(self):
-        self.by_place(self.ex.s, lambda part: [self.scatter_copy(k, part).start() for k in self.others()])
+        self.each(self.chunks_of, lambda p: self.out_copy(p).start())
 
     def scatter_settle(self):
-        self.by_place(self.ex.s, lambda part: [self.scatter_copy(k, part).wait_send() for k in self.others()])
-
-    def from_place(self, k):
-        return (self.ex.s + self.ex.ns - k) % self.ex.ns
+        self.each(self.chunks_of, lambda p: self.out_copy(p).wait_send())
 
     def reduce(self):
         ex = self.ex
-        for k in self.others():
-            self.by_place(self.from_place(k), lambda part, k=k: self.scatter_copy(k, part).wait_recv())
+        self.each(self.devices_of, lambda p: self.got_copy(p).wait_recv())
         total = self.out[ex.s].astype(F32)
-        for k in self.others():
-            total = total + self.got[k - 1].astype(F32)
+        for k in range(ex.ns) if self.sparse else range(1, ex.ns):
+            total = total + self.got[k if self.sparse else (ex.s + k) % ex.ns].astype(F32)
         return total.astype(BF16)
 
     def spread(self, total):
         self.full[self.ex.s] = total
-        for k in self.others():
-            to = (self.ex.s + k) % self.ex.ns
-            self.by_place(to, lambda part, k=k: self.spread_copy(k, self.ex.s, part).start())
+        self.each(self.devices_of, lambda p: self.spread_copy(p).start())
 
     def spread_settle(self):
-        for k in self.others():
-            to = (self.ex.s + k) % self.ex.ns
-            self.by_place(to, lambda part, k=k: self.spread_copy(k, self.ex.s, part).wait_send())
+        self.each(self.devices_of, lambda p: self.spread_copy(p).wait_send())
 
     def finish(self):
-        self.by_place(
-            self.ex.s, lambda part: [self.spread_copy(k, self.from_place(k), part).wait_recv() for k in self.others()]
-        )
+        self.each(self.chunks_of, lambda p: self.full_copy(p).wait_recv())
 
 
 def mask_rows(ids, last_id):
@@ -236,7 +247,17 @@
 def put_chunks(acc_ref, out_ref, first_id, last_id, seqs):
     heads = acc_ref.shape[0]
     if seqs == 2:
-        out_ref[...] = acc_ref[...].astype(BF16)
+        owners = out_ref.shape[0] // 2
+        per = heads // owners
+        row = lax.broadcasted_iota(jnp.int32, (PAD, acc_ref.shape[2]), 0)
+        for i in range(out_ref.shape[0]):
+            slot, base = i // owners, per * (i % owners)
+            at = (64 + PAD) * slot
+            z = jnp.zeros(row.shape, F32)
+            for j in range(per):
+                z = jnp.where(row == j, acc_ref[base + j, 64 + slot : 65 + slot], z)
+            rows = [acc_ref[base + j, at : at + 64] for j in range(per)]
+            out_ref[i] = jnp.concatenate([*rows, z], axis=0).astype(BF16)
         return
     groups = seqs // 2
 
@@ -254,10 +275,14 @@
     lax.fori_loop(0, heads, body, 0)
 
 
-def take_slots(full_ref, h, first_id, last_id, seqs):
+def take_slots(full_ref, h, heads, first_id, last_id, seqs):
     if seqs == 2:
-        a = full_ref[h].astype(F32)
-        return a[:64], a[64 + PAD :], a[64:65], a[65:66]
+        owners = full_ref.shape[0] // 2
+        per = heads // owners
+        j = h % per
+        a, b = (full_ref[k * owners + h // per].astype(F32) for k in range(2))
+        z = 64 * per + j
+        return a[64 * j : 64 * j + 64], b[64 * j : 64 * j + 64], a[z : z + 1], b[z : z + 1]
     groups = seqs // 2
     picks = [None] * 4
     for g in range(groups):
@@ -274,7 +299,7 @@
 
 def build_b(full_ref, b_ref, first_id, last_id, seqs, repeat):
     for h in range(b_ref.shape[0]):
-        r1, r2, z1, z2 = take_slots(full_ref, h, first_id, last_id, seqs)
+        r1, r2, z1, z2 = take_slots(full_ref, h, b_ref.shape[0], first_id, last_id, seqs)
         if h % 2:
             r1, r2, z1, z2 = r2, r1, z2, z1
         shape = r1.shape
@@ -306,10 +331,10 @@
 
 
 def front_kernel(
-    x_ref, dy_ref, ids_ref, rand_ref, gains_in, wk_in, wv_in, wq_in, wo_in, wu_in, wd_in,
+    x_ref, dy_ref, ids_ref, rand_ref, g1_in, g2_in, wk_in, wv_in, wq_in, wo_in, wu_in, wd_in,
     out_o, att_o, a2_o, hid_o, dpre_o, dmid_o, dq_o, a1_o, ks_o, vv_o, fk_o, wq_o, wk_o, wv_o, p_o, s_o, gain_o, gg_o,
     a1, ks, vv, fk, qs, fq, t_out, t_att, t_a2, t_hid, t_dpre, t_dmid, t_dq,
-    gains, wk, wv, wq, wo, wu, wd, rbd, rt, b_ref, acc, p_out, p_got, p_full,
+    gains_in, gains, wk, wv, wq, wo, wu, wd, rbd, rt, b_ref, acc, p_out, p_got, p_full,
     w_send, w_recv, w_local, r_send, r_recv, g_send, g_recv, o_sem, t_sem,
     *, micro, seqs, factor,
 ):
@@ -323,6 +348,11 @@
         Sum(ex, p_out.at[mb], p_got.at[mb], p_full.at[mb], (r_send.at[mb], r_recv.at[mb], g_send.at[mb], g_recv.at[mb]), seqs)
         for mb in range(micro)
     ]
+    place = lax.broadcasted_iota(jnp.int32, (1, width), 1) // g1_in.shape[1] == ex.f
+    gains_in[...] = jnp.zeros_like(gains_in)
+    for i, g in enumerate((g1_in, g2_in)):
+        wide = jnp.concatenate([g[...].astype(F32)] * ex.nf, axis=1)
+        gains_in[i : i + 1, :] = jnp.where(place, wide, 0.0).astype(BF16)
     ex.barrier()
     pieces = []
     for i, (shard, full) in enumerate(
@@ -332,9 +362,9 @@
     for piece in pieces:
         piece.begin()
     build_features(rand_ref, rbd, rt)
-    for piece in pieces[:3]:
+    for piece in pieces[:2]:
         piece.forward()
-    for piece in pieces[:3]:
+    for piece in pieces[:2]:
         piece.finish()
     gain_rows = gains.shape[0] // ex.nf
     both = gains[0:gain_rows, :].astype(F32)
@@ -347,10 +377,10 @@
     def ident(mb):
         if seqs == 2:
             return 0, 1
-        return ids_ref[mb : mb + 1, 0:1], ids_ref[mb : mb + 1, toks - 1 : toks]
+        return ids_ref[mb, :, 0:1], ids_ref[mb, :, toks - 1 : toks]
 
     def ids_of(mb, t):
-        return ids_ref[mb : mb + 1, pl.ds(pl.multiple_of(t * TILE, TILE), TILE)]
+        return ids_ref[mb, :, pl.ds(pl.multiple_of(t * TILE, TILE), TILE)]
 
     outs = []
 
@@ -363,16 +393,25 @@
         acc[...] = jnp.zeros_like(acc)
         first_id, last_id = ident(mb)
 
-        def keys(t, carry, mb=mb, last_id=last_id):
+        def keys(t, carry, mb=mb):
             r = rows_at(t + mb * tiles, TILE)
             normed, _ = norm_parts(x_ref[r, :].astype(F32))
             low = (normed * g1).astype(BF16)
             a1[r, :] = low
             k = (dot(low, wk[...]) * factor).astype(BF16)
             ks[r, :] = k
-            v = dot(low, wv[...]).astype(BF16)
+            features(k, rbd, fk.at[r, :], feats)
+            return carry
+
+        lax.fori_loop(0, tiles, keys, 0)
+        if mb == 0:
+            pieces[2].forward()
+            pieces[2].finish()
+
+        def values(t, carry, mb=mb, last_id=last_id):
+            r = rows_at(t + mb * tiles, TILE)
+            v = dot(a1[r, :], wv[...]).astype(BF16)
             vv[r, :] = v
-            features(k, rbd, fk.at[r, :], feats)
             vt = v.T
             mask_t = mask_rows(ids_of(mb, t), last_id)
             for h in range(heads):
@@ -380,7 +419,7 @@
                 acc[h] += dot(lt, fk[r, feats * h : feats * h + feats])
             return carry
 
-        lax.fori_loop(0, tiles, keys, 0)
+        lax.fori_loop(0, tiles, values, 0)
         put_chunks(acc, p_out.at[mb], first_id, last_id, seqs)
         if mb == 0:
             sums[mb].scatter()
@@ -440,6 +479,13 @@
                 def _():
                     for other in sums[1:]:
                         other.spread(other.reduce())
+
+            if mb == 1:
+
+                @pl.when(t == 1)
+                def _():
+                    sums[0].spread_settle()
+                    sums[0].spread(sums[0].reduce())
 
             ids = ids_of(mb, t)
             last = last_lanes(ids, last_id)
@@ -513,7 +559,8 @@
             sums[0].scatter()
         else:
             put_chunks(acc, p_o.at[mb - 1], first_id, last_id, seqs)
-    s_o[...] = sums[0].reduce()
+    sums[0].finish()
+    emit(p_full.at[0], s_o, o_sem.at[7])
     last_tile = micro * tiles - 1
     for g in (last_tile - 1, last_tile):
         for c in tile_copies(g, g % 2):
@@ -526,7 +573,7 @@
     ex.drain()
 
 
-def front(x, dy, ids, rand, gains, wk, wv, wq, wo, wu, wd, *, micro, seqs, nf, ns, factor):
+def front(x, dy, ids, rand, g1, g2, wk, wv, wq, wo, wu, wd, *, micro, seqs, nf, ns, factor):
     total, width = x.shape
     heads, _, feats = rand.shape
     hidden = wu.shape[1]
@@ -541,63 +588,57 @@
     out_shape = [
         bf(total, width), bf(total, width), bf(total, width), bf(total, hidden), bf(total, hidden), bf(total, width),
         bf(total, width), bf(total, width), bf(total, width), bf(total, width), bf(total, heads * feats),
-        bf(width, width), bf(width, width), bf(width, width), bf(micro - 1, chunks, rows, feats), bf(rows, feats),
+        bf(width, width), bf(width, width), bf(width, width), bf(micro - 1, chunks, rows, feats), bf(ns, rows, feats),
         bf(PAD, width), jax.ShapeDtypeStruct((1, width), F32),
     ]
     v = pltpu.VMEM
     dma = pltpu.SemaphoreType.DMA
     scratch = [v((total, width), BF16)] * 3 + [v((total, heads * feats), BF16), v((total, width), BF16), v((total, heads * feats), BF16)]
     scratch += [v((2, TILE, width), BF16)] * 3 + [v((2, TILE, hidden), BF16)] * 2 + [v((2, TILE, width), BF16)] * 2
-    scratch += [v((nf * PAD, width), BF16)] + [v((width, width), BF16)] * 4 + [v((width, hidden), BF16), v((hidden, width), BF16)]
+    scratch += [v((PAD, width), BF16), v((nf * PAD, width), BF16)] + [v((width, width), BF16)] * 4 + [v((width, hidden), BF16), v((hidden, width), BF16)]
     scratch += [v((heads // 4, 256, 4 * feats), BF16), v((heads // 2, 2 * feats, 256), BF16), v((heads, 256, feats), BF16)]
     scratch += [v((heads, rows, feats), F32), v((micro, chunks, rows, feats), BF16)]
-    scratch += [v((micro, ns - 1, rows, feats), BF16), v((micro, ns, rows, feats), BF16)]
+    scratch += [v((micro, ns, rows, feats), BF16), v((micro, ns, rows, feats), BF16)]
     kinds = nf - 1
-    scratch += [dma((7, kinds)), dma((7, kinds)), dma((7,))] + [dma((micro, ns - 1))] * 4 + [dma((7,)), dma((2, 7))]
+    scratch += [dma((7, kinds)), dma((7, kinds)), dma((7,))] + [dma((micro, ns))] * 4 + [dma((8,)), dma((2, 7))]
     return pl.pallas_call(
         functools.partial(front_kernel, micro=micro, seqs=seqs, factor=factor),
-        in_specs=[vmem] * 4 + [hbm] * 7,
-        out_specs=[hbm] * 14 + [vmem] * 4,
+        in_specs=[vmem] * 6 + [hbm] * 6,
+        out_specs=[hbm] * 14 + [vmem, hbm, vmem, vmem],
         out_shape=out_shape,
         scratch_shapes=scratch,
         compiler_params=pltpu.CompilerParams(collective_id=0, has_side_effects=True, vmem_limit_bytes=63 << 20),
         name="front",
-    )(x, dy, ids, rand, gains, wk, wv, wq, wo, wu, wd)
-
-
-class TwoLevel:
-    def __init__(self, ex, out, got1, mid, got2, full, send, recv):
-        self.ex, self.out, self.got1, self.mid, self.got2, self.full = ex, out, got1, mid, got2, full
-        self.send, self.recv = send, recv
-        self.slow = 4 if ex.ns % 4 == 0 else 1
-        self.fast = ex.ns // self.slow
+    )(x, dy, ids, rand, g1, g2, wk, wv, wq, wo, wu, wd)
+
+
+class SeqSum:
+    def __init__(self, ex, refs, send, recv):
+        self.ex, self.send, self.recv = ex, send, recv
+        self.out, self.got1, self.mid, self.got2, self.full = refs
+        self.fast = ex.ns // 4
         self.z, self.x = ex.s // self.fast, ex.s % self.fast
-        self.sent = []
-
-    def device(self, z, x):
-        return (z * self.fast + x, self.ex.f)
+
+    def copy(self, phase, k, src, dst, z, x):
+        return self.ex.copy(src, dst, self.send.at[phase, k - 1], self.recv.at[phase, k - 1], (z * self.fast + x, self.ex.f))
 
     def fast_copy(self, phase, k, src, dst):
-        j = k - 1
-        peer = self.device(self.z, (self.x + k) % self.fast)
-        return self.ex.copy(src, dst, self.send.at[phase, j], self.recv.at[phase, j], peer)
+        return self.copy(phase, k, src, dst, self.z, (self.x + k) % self.fast)
 
     def slow_copy(self, phase, k, src, dst):
-        j = k - 1
-        peer = self.device((self.z + k) % self.slow, self.x)
-        return self.ex.copy(src, dst, self.send.at[phase, j], self.recv.at[phase, j], peer)
-
-    def start(self, c):
-        c.start()
-        self.ex.pending.append(c)
+        return self.copy(phase, k, src, dst, (self.z + k) % 4, self.x)
 
     def block(self, x):
-        return pl.ds(x * self.slow, self.slow)
+        return pl.ds(x * 4, 4)
 
     def send1(self):
         for k in range(1, self.fast):
-            src = self.out.at[self.block((self.x + k) % self.fast)]
-            self.start(self.fast_copy(0, k, src, self.got1.at[k - 1]))
+
+            def make(k=k):
+                src = self.out.at[self.block((self.x + k) % self.fast)]
+                return self.fast_copy(0, k, src, self.got1.at[k - 1])
+
+            self.ex.launch(make)
 
     def sum1(self):
         for k in range(1, self.fast):
@@ -606,27 +647,35 @@
         for k in range(1, self.fast):
             total = total + self.got1[k - 1].astype(F32)
         self.mid[...] = total.astype(BF16)
-        for k in range(1, self.slow):
-            self.start(self.slow_copy(1, k, self.mid.at[(self.z + k) % self.slow], self.got2.at[k - 1]))
+        for k in (2, 1, 3):
+            self.ex.launch(lambda k=k: self.slow_copy(1, k, self.mid.at[(self.z + k) % 4], self.got2.at[k - 1]))
 
     def sum2(self):
-        for k in range(1, self.slow):
+        for k in range(1, 4):
             self.slow_copy(1, k, self.got2.at[k - 1], self.got2.at[k - 1]).wait_recv()
         total = self.mid[self.z].astype(F32)
-        for k in range(1, self.slow):
+        for k in range(1, 4):
             total = total + self.got2[k - 1].astype(F32)
-        at = self.x * self.slow + self.z
-        self.full[at] = total.astype(BF16)
-        for k in range(1, self.slow):
-            self.start(self.slow_copy(2, k, self.full.at[at], self.full.at[at]))
-
-    def send4(self):
-        for k in range(1, self.slow):
-            part = self.full.at[self.x * self.slow + (self.z + self.slow - k) % self.slow]
+        self.full[self.x * 4 + self.z] = total.astype(BF16)
+        for k in (2, 1, 3):
+
+            def make(k=k):
+                mine = self.full.at[self.x * 4 + self.z]
+                return self.slow_copy(2, k, mine, mine)
+
+            self.ex.launch(make)
+
+    def send_fast(self):
+        for k in range(1, 4):
+            part = self.full.at[self.x * 4 + (self.z + 4 - k) % 4]
             self.slow_copy(2, k, part, part).wait_recv()
-        mine = self.full.at[self.block(self.x)]
         for k in range(1, self.fast):
-            self.start(self.fast_copy(3, k, mine, mine))
+
+            def make(k=k):
+                mine = self.full.at[self.block(self.x)]
+                return self.fast_copy(3, k, mine, mine)
+
+            self.ex.launch(make)
 
     def finish(self):
         for k in range(1, self.fast):
@@ -635,8 +684,9 @@
 
 
 class Reduce:
-    def __init__(self, ex, part, rc, ry, two, send, recv):
-        self.ex, self.part, self.rc, self.ry, self.two, self.send, self.recv = ex, part, rc, ry, two, send, recv
+    def __init__(self, ex, part, rc, ry, seq, send, recv):
+        self.ex, self.part, self.rc, self.ry, self.seq, self.send, self.recv = ex, part, rc, ry, seq, send, recv
+        self.steps = iter([self.core_sum, self.y_sum, seq.sum1, seq.sum2, seq.send_fast, seq.finish])
 
     def core_copy(self, yy):
         ex = self.ex
@@ -645,9 +695,7 @@
 
     def core_send(self):
         for yy in range(self.ex.ny):
-            c = self.core_copy(yy)
-            c.start()
-            self.ex.pending.append(c)
+            self.ex.launch(lambda yy=yy: self.core_copy(yy))
 
     def y_copy(self, k):
         ex = self.ex
@@ -657,36 +705,33 @@
 
     def core_sum(self):
         ex = self.ex
-        for yy in range(ex.ny):
+        for k in range(1, ex.ny):
+            yy = (ex.y + k) % ex.ny
+            f = ex.y_to(k)
             self.core_copy(yy).wait_recv()
-            f = yy * 2 + ex.c
             self.part[f] = (self.part[f].astype(F32) + self.rc[yy].astype(F32)).astype(BF16)
-        for k in range(1, ex.ny):
-            c = self.y_copy(k)
-            c.start()
-            ex.pending.append(c)
+            ex.launch(lambda k=k: self.y_copy(k))
 
     def y_sum(self):
         ex = self.ex
+        self.core_copy(ex.y).wait_recv()
+        total = self.part[ex.f].astype(F32) + self.rc[ex.y].astype(F32)
         for k in range(1, ex.ny):
             self.y_copy(k).wait_recv()
-        total = self.part[ex.f].astype(F32)
-        for k in range(1, ex.ny):
             total = total + self.ry[k - 1].astype(F32)
-        self.two.out[...] = total.astype(BF16)
-        self.two.send1()
+        self.seq.out[...] = total.astype(BF16)
+        self.seq.send1()
+
+
+PIECES = 6
 
 
 def back_kernel(
     x_in, dy_in, hid_in, dpre_in, a2_in, att_in, dmid_in, dq_in, a1_in, ks_in, vv_in, fk_in, wq_in, wk_in, wv_in,
-    ids_ref, rand_ref, gain_ref, gg_ref, s0_ref, p1_ref,
-    dx_o, g1_o, g2_o, wq_g, wk_g, wv_g, wo_g, wu_g, wd_g,
+    ids_ref, rand_ref, gain_ref, gg_ref, p0_ref, p1_ref,
+    dx_o, g1_o, g2_o, res_o,
     x, dy, blk, a2, att, dmid, dq, a1, ks, vv, fk, wq, wk, wv, dk, dv, tr, t_dx, rbd, rt, b_ref,
-    p_got, p_full,
-    part_d, rc_d, ry_d, out_d, got1_d, mid_d, got2_d, full_d,
-    part_u, rc_u, ry_u, out_u, got1_u, mid_u, got2_u, full_u,
-    part_q, rc_q, ry_q, out_q, got1_q, mid_q, got2_q, full_q,
-    part_k, rc_k, ry_k, out_k, got1_k, mid_k, got2_k, full_k,
+    p_got, p_full, part, rc, ry, s_out, s_got1, s_mid, s_got2,
     gs, gr,
     l_sem, b_sem, x_sem, r_send, r_recv, g_send, g_recv, c_send, c_recv, t_send, t_recv, n_send, n_recv,
     *, micro, seqs, factor,
@@ -700,14 +745,14 @@
     hidden = hid_in.shape[1]
     blocks = hidden // 512
     quarter = ex.ns // 4
-    chunk = out_d.shape[1]
+    chunk = res_o.shape[2]
     shard = quarter * chunk
-    sems = [(r_send, r_recv, g_send.at[mb], g_recv.at[mb]) for mb in range(2)]
-    sums = [Sum(ex, p1_ref, p_got, p_full.at[mb], sems[mb], seqs) for mb in range(2)]
-
+    kv_sum = Sum(ex, p1_ref, p_got, p_full, (r_send, r_recv, g_send, g_recv), seqs)
+
+    ex.greet()
     loads = {}
     order = (
-        ("dy", dy_in, dy), ("a2", a2_in, a2), ("att", att_in, att), ("dmid", dmid_in, dmid), ("a1", a1_in, a1), ("dq", dq_in, dq),
+        ("att", att_in, att), ("dmid", dmid_in, dmid), ("a1", a1_in, a1), ("dq", dq_in, dq), ("dy", dy_in, dy), ("a2", a2_in, a2),
         ("vv", vv_in, vv), ("fk", fk_in, fk), ("ks", ks_in, ks), ("wq", wq_in, wq), ("wk", wk_in, wk), ("wv", wv_in, wv),
         ("x", x_in, x),
     )
@@ -726,85 +771,100 @@
         for name in names:
             loads.pop(name).wait()
 
-    ex.barrier()
-    sums[1].scatter()
-    sums[0].spread(s0_ref[...])
-    groups = []
-    for i, refs in enumerate((
-        (part_d, rc_d, ry_d, out_d, got1_d, mid_d, got2_d, full_d),
-        (part_u, rc_u, ry_u, out_u, got1_u, mid_u, got2_u, full_u),
-        (part_q, rc_q, ry_q, out_q, got1_q, mid_q, got2_q, full_q),
-        (part_k, rc_k, ry_k, out_k, got1_k, mid_k, got2_k, full_k),
-    )):
-        two = TwoLevel(ex, *refs[3:], t_send.at[i], t_recv.at[i])
-        groups.append(Reduce(ex, *refs[:3], two, c_send.at[i], c_recv.at[i]))
-    down, up, query, key = groups
-    build_features(rand_ref, rbd, rt)
-
-    need("dy")
-    tr[...] = dy[...].T
-
-    def down_block(b, carry):
-        block_copy(hid_in, b).wait()
-        v = dot(tr[...], blk[b]).T
-        n = 512 // chunk
-        flat = part_d.at[b * n // ex.ns] if n == ex.ns else None
-        v = v.reshape(n, chunk, width).astype(BF16)
-        if flat is not None:
-            flat[...] = v
-        else:
-            per = n // ex.ns
-            for i in range(per):
-                part_d[b * per + i] = v[i * ex.ns : (i + 1) * ex.ns]
-        block_copy(dpre_in, b).start()
-        return carry
-
-    lax.fori_loop(0, blocks, down_block, 0)
-    down.core_send()
-    need("a2")
-    tr[...] = a2[...].T
-
-    def up_block(b, carry):
-        block_copy(dpre_in, b).wait()
-        v = dot(tr[...], blk[b])
-        for f in range(ex.nf):
-            one = v[f * shard : (f + 1) * shard].reshape(quarter, chunk, 512)
-            part_u[f, pl.ds(b * quarter, quarter)] = one.astype(BF16)
-        return carry
-
-    lax.fori_loop(0, blocks, up_block, 0)
-    up.core_send()
-    sums[1].spread(sums[1].reduce())
-    down.core_sum()
-
-    def small(left_t, right, group, which):
+    ex.meet()
+    kv_sum.scatter()
+    pieces = []
+    for i in range(PIECES):
+        seq = SeqSum(ex, (s_out.at[i], s_got1.at[i], s_mid.at[i], s_got2.at[i], res_o.at[i]), t_send.at[i], t_recv.at[i])
+        pieces.append(Reduce(ex, part.at[i], rc.at[i], ry.at[i], seq, c_send.at[i], c_recv.at[i]))
+    q, d1, d2, u1, u2, k = pieces
+
+    def go(*which):
+        for one in which:
+            next(one.steps)()
+
+    def go_at(t, plan):
+        for when, which in plan.items():
+
+            @pl.when(t == when)
+            def _(which=which):
+                go(*which)
+
+    def small(left_t, right, piece, which):
         v = dot(left_t, right)
         for half in range(2):
             for f in range(ex.nf):
                 one = v[f * shard : (f + 1) * shard, 256 * half : 256 * half + 256].reshape(quarter, chunk, 256)
-                group.part[f, quarter * (2 * which + half) : quarter * (2 * which + half + 1)] = one.astype(BF16)
+                piece.part[f, quarter * (2 * which + half) : quarter * (2 * which + half + 1)] = one.astype(BF16)
 
     need("att", "dmid")
-    small(att[...].T, dmid[...], query, 1)
+    small(att[...].T, dmid[...], q, 1)
     need("a1", "dq")
+    small(a1[...].T, dq[...], q, 0)
+    q.core_send()
+    need("dy")
+    tr[...] = dy[...].T
+    per = 512 // chunk // ex.ns
+
+    def down_block(i, carry):
+        b = (i + (ex.y + 1) % ex.ny * (blocks // ex.ny)) % blocks
+        block_copy(hid_in, b).wait()
+        v = dot(tr[...], blk[b]).T
+        block_copy(dpre_in, b).start()
+        for half, piece in enumerate((d1, d2)):
+            one = v[:, 256 * half : 256 * half + 256].reshape(512 // chunk, chunk, 256).astype(BF16)
+            for j in range(per):
+                f = b * per + j
+                piece.part[f] = one[j * ex.ns : (j + 1) * ex.ns]
+
+                @pl.when(f % 2 != ex.c)
+                def _(f=f, piece=piece):
+                    piece.core_copy(f // 2).start()
+
+        go_at(i, {1: (q,)})
+        return carry
+
+    lax.fori_loop(0, blocks, down_block, 0)
+    for piece in (d1, d2):
+        ex.pending += [lambda yy=yy, piece=piece: piece.core_copy(yy) for yy in range(ex.ny)]
+    go(d1, d2)
+    kv_sum.spread(kv_sum.reduce())
+    build_features(rand_ref, rbd, rt)
+    need("a2")
+    tr[...] = a2[...].T
+
+    def up_block(b, carry):
+        block_copy(dpre_in, b).wait()
+        v = dot(tr[...], blk[b])
+        for half in range(2):
+            for f in range(ex.nf):
+                one = v[f * shard : (f + 1) * shard, 256 * half : 256 * half + 256].reshape(quarter, chunk, 256)
+                part[3 + b // 2, f, pl.ds((b % 2 * 2 + half) * quarter, quarter)] = one.astype(BF16)
+
+        @pl.when(b == 1)
+        def _():
+            u1.core_send()
+
+        go_at(b, {2: (q,), 3: (u1,)})
+        return carry
+
+    lax.fori_loop(0, blocks, up_block, 0)
+    u2.core_send()
     tr[...] = a1[...].T
-    small(tr[...], dq[...], query, 0)
-    query.core_send()
-    up.core_sum()
     need("vv", "fk", "ks")
 
     def ident(mb):
         if seqs == 2:
             return 0, 1
-        return ids_ref[mb : mb + 1, 0:1], ids_ref[mb : mb + 1, toks - 1 : toks]
-
-    def kv_part(mb):
+        return ids_ref[mb, :, 0:1], ids_ref[mb, :, toks - 1 : toks]
+
+    def kv_part(mb, full, plan):
         first_id, last_id = ident(mb)
-        build_b(p_full.at[mb], b_ref, first_id, last_id, seqs, False)
+        build_b(full, b_ref, first_id, last_id, seqs, False)
 
         def body(t, carry):
             r = rows_at(t + mb * tiles, TILE)
-            ids = ids_ref[mb : mb + 1, pl.ds(pl.multiple_of(t * TILE, TILE), TILE)]
+            ids = ids_ref[mb, :, pl.ds(pl.multiple_of(t * TILE, TILE), TILE)]
             last = last_lanes(ids, last_id)
             lane = lax.broadcasted_iota(jnp.int32, (TILE, 128), 1)
             sel = jnp.logical_xor(lane < 64, last)
@@ -829,6 +889,7 @@
                 va = dot_nt(fa, b_ref[2 * p, :128])
                 vb = dot_nt(fb, b_ref[2 * p + 1, :128])
                 dv[r, ps] = swap(jnp.where(sel, va, vb)).astype(BF16)
+            go_at(t, plan)
             return carry
 
         lax.fori_loop(0, tiles, body, 0)
@@ -840,7 +901,7 @@
     def dx_copy(g, slot):
         return pltpu.make_async_copy(t_dx.at[slot], dx_o.at[rows_at(g, TILE), :], x_sem.at[slot])
 
-    def x_part(mb):
+    def x_part(mb, plan):
         def body(t, carry):
             g = t + mb * tiles
             slot = g % 2
@@ -855,28 +916,21 @@
             gs[0, 0:1, :] += jnp.sum(da1 * normed, axis=0, keepdims=True)
             t_dx[slot] = (dmid[r, :].astype(F32) + norm_back(da1, normed, rescale, g1)).astype(BF16)
             dx_copy(g, slot).start()
+            go_at(t, plan)
             return carry
 
         lax.fori_loop(0, tiles, body, 0)
 
-    sums[0].finish()
-    kv_part(0)
-    down.y_sum()
-    query.core_sum()
+    kv_part(0, p0_ref, {0: (u2,), 1: (d1, q), 2: ()})
+    kv_sum.finish()
+    kv_part(1, p_full, {1: (d1, d2, q)})
+    small(tr[...], dk[...], k, 0)
+    small(tr[...], dv[...], k, 1)
+    k.core_send()
+    go(u1, d2, d1)
     need("wq", "wk", "wv", "x")
-    x_part(0)
-    down.two.sum1()
-    sums[1].finish()
-    kv_part(1)
-    small(tr[...], dk[...], key, 0)
-    small(tr[...], dv[...], key, 1)
-    key.core_send()
-    up.y_sum()
-    down.two.sum2()
-    key.core_sum()
-    query.y_sum()
-    up.two.sum1()
-    x_part(1)
+    x_part(0, {1: (k, q), 2: (u1, u2)})
+    x_part(1, {0: (d2,), 2: (q, d1)})
     def gain_copy(level, j, peer):
         return ex.copy(gs.at[level], gr.at[j], n_send.at[j], n_recv.at[j], peer)
 
@@ -893,50 +947,30 @@
         return total
 
     jobs0 = gain_level(0, [(0, (ex.s, ex.partner))])
-    down.two.send4()
-    key.y_sum()
+    go(k, u2, u1)
     gs[1] = gain_sum(0, jobs0)
     jobs1 = gain_level(1, [(k, (ex.s, ex.y_to(k))) for k in range(1, ex.ny)])
-    query.two.sum1()
-    up.two.sum2()
-    down.two.finish()
-    wd_g[...] = full_d[...].astype(F32).reshape(wd_g.shape)
+    go(d1, d2, k, u2)
     gs[2] = gain_sum(1, jobs1)
     jobs2 = gain_level(2, [(ex.ny - 1 + k, ex.seq_peer(k)) for k in range(1, ex.ns)])
-    key.two.sum1()
-    query.two.sum2()
-    up.two.send4()
-    key.two.sum2()
-    query.two.send4()
-    up.two.finish()
-    for b in range(blocks):
-        wu_g[:, 512 * b : 512 * b + 512] = full_u[quarter * b : quarter * b + quarter].astype(F32).reshape(shard, 512)
+    go(d2, u1, k, u1, u2)
     gains = gain_sum(2, jobs2)
     mine = jnp.zeros((gains.shape[0], shard), F32)
     for f in range(ex.nf):
         mine = mine + jnp.where(ex.f == f, gains[:, f * shard : f * shard + shard], 0.0)
     g1_o[...] = mine[0:1]
     g2_o[...] = mine[1:2]
-    key.two.send4()
-
-    def finish(group, full, refs):
-        group.two.finish()
-        for which, ref in enumerate(refs):
-            for half in range(2):
-                i = quarter * (2 * which + half)
-                ref[:, 256 * half : 256 * half + 256] = full[i : i + quarter].astype(F32).reshape(shard, 256)
-
-    finish(query, full_q, (wq_g, wo_g))
-    finish(key, full_k, (wk_g, wv_g))
+    go(k, u2, k)
+    for piece in pieces:
+        assert next(piece.steps, None) is None
     last = micro * tiles - 1
     for g in (last - 1, last):
         dx_copy(g, g % 2).wait()
     for level, jobs in enumerate((jobs0, jobs1, jobs2)):
         for j, peer in jobs:
             gain_copy(level, j, peer).wait_send()
-    sums[1].scatter_settle()
-    for one in sums:
-        one.spread_settle()
+    kv_sum.scatter_settle()
+    kv_sum.spread_settle()
     ex.drain()
 
 
@@ -948,7 +982,7 @@
     rows = 128 + PAD
     hidden = hid.shape[1]
     ny = nf // 2
-    slow = 4 if ns % 4 == 0 else 1
+    slow = 4
     fast = ns // slow
     chunk = 4 * shard // ns
     hbm = pl.BlockSpec(memory_space=pl.ANY)
@@ -960,30 +994,96 @@
         return jax.ShapeDtypeStruct(shape, F32)
 
     out_shape = [jax.ShapeDtypeStruct((total, width), BF16), f32(1, shard), f32(1, shard)]
-    out_shape += [f32(shard, width)] * 4 + [f32(shard, hidden), f32(hidden // nf, width)]
+    out_shape += [jax.ShapeDtypeStruct((PIECES, ns, chunk, 256), BF16)]
     token = v((total, width), BF16)
     scratch = [token, token, v((hidden // 512, total, 512), BF16), token, token, token, token, token, token, token]
     scratch += [v((total, heads * feats), BF16)] + [v((width, width), BF16)] * 3 + [token, token, v((width, total), BF16)]
     scratch += [v((2, TILE, width), BF16), v((heads // 4, 256, 4 * feats), BF16), v((heads // 2, 2 * feats, 256), BF16)]
-    scratch += [v((heads, 256, feats), BF16), v((ns - 1, rows, feats), BF16), v((2, ns, rows, feats), BF16)]
-    for cols in (512, 512, 256, 256):
-        scratch += [v((nf, ns, chunk, cols), BF16), v((ny, ns, chunk, cols), BF16), v((ny - 1, ns, chunk, cols), BF16)]
-        scratch += [v((ns, chunk, cols), BF16), v((fast - 1, slow, chunk, cols), BF16), v((slow, chunk, cols), BF16)]
-        scratch += [v((slow - 1, chunk, cols), BF16), v((ns, chunk, cols), BF16)]
+    scratch += [v((heads, 256, feats), BF16), v((ns, rows, feats), BF16), v((ns, rows, feats), BF16)]
+    for lead in ((nf, ns), (ny, ns), (ny - 1, ns), (ns,), (fast - 1, slow), (slow,), (slow - 1,)):
+        scratch.append(v((PIECES, *lead, chunk, 256), BF16))
     jobs = 1 + (ny - 1) + (ns - 1)
     scratch += [v((3, 8, width), F32), v((jobs, 8, width), F32)]
     peers = max(fast, slow) - 1
-    scratch += [dma((13,)), dma((hidden // 512,)), dma((2,)), dma((ns - 1,)), dma((ns - 1,)), dma((2, ns - 1)), dma((2, ns - 1))]
-    scratch += [dma((4, 2 * ny - 1))] * 2 + [dma((4, 4, peers))] * 2 + [dma((jobs,))] * 2
+    scratch += [dma((13,)), dma((hidden // 512,)), dma((2,)), *([dma((ns,))] * 4)]
+    scratch += [dma((PIECES, 2 * ny - 1))] * 2 + [dma((PIECES, 4, peers))] * 2 + [dma((jobs,))] * 2
     return pl.pallas_call(
         functools.partial(back_kernel, micro=micro, seqs=seqs, factor=factor),
         in_specs=[hbm] * len(big) + [vmem] * len(small),
-        out_specs=[hbm] + [vmem] * 8,
+        out_specs=[hbm] + [vmem] * 3,
         out_shape=out_shape,
         scratch_shapes=scratch,
         compiler_params=pltpu.CompilerParams(collective_id=1, has_side_effects=True, vmem_limit_bytes=63 << 20),
         name="back",
     )(*big, *small)
+
+
+def results_kernel(out, dx, q, d1, d2, u1, u2, k, g1, g2, out_o, dx_o, wq, wo, wk, wv, wu, wd, g1_o, g2_o):
+    out_o[...] = out[...]
+    dx_o[...] = dx[...]
+    g1_o[...] = g1[...]
+    g2_o[...] = g2[...]
+
+    def wide(a):
+        a = a.astype(F32)
+        return a.reshape(a.shape[0] * a.shape[1], a.shape[2])
+
+    wd[:, :256] = wide(d1[...])
+    wd[:, 256:] = wide(d2[...])
+    step = pl.program_id(0)
+
+    def up(piece):
+        half = piece.shape[0] // 2
+        wu[:, :256] = wide(piece[:half])
+        wu[:, 256:] = wide(piece[half:])
+
+    @pl.when(step < 2)
+    def _():
+        wq[...] = wide(q[...])
+        wk[...] = wide(k[...])
+        up(u1)
+
+    @pl.when(step >= 2)
+    def _():
+        wo[...] = wide(q[...])
+        wv[...] = wide(k[...])
+        up(u2)
+
+
+def results(out, dx, res, g1, g2, shard):
+    total, width = out.shape
+    _, ns, chunk, cols = res.shape
+    quarter = ns // 4
+    rows = pl.BlockSpec((total // 4, width), lambda i: (i, 0))
+    gain = pl.BlockSpec((1, shard), lambda i: (0, 0))
+
+    def piece(g):
+        return pl.BlockSpec((None, quarter, chunk, cols), lambda i: (g, i, 0, 0))
+
+    def low(i):
+        return jnp.minimum(i, 1)
+
+    def high(i):
+        return jnp.maximum(i - 2, 0)
+
+    def wider(g, of):
+        return pl.BlockSpec((None, 2 * quarter, chunk, cols), lambda i: (g, of(i), 0, 0))
+
+    first = pl.BlockSpec((shard, cols), lambda i: (0, low(i)))
+    second = pl.BlockSpec((shard, cols), lambda i: (0, high(i)))
+    half = jax.ShapeDtypeStruct((shard, 2 * cols), F32)
+    token = jax.ShapeDtypeStruct((total, width), BF16)
+    gain_shape = jax.ShapeDtypeStruct((1, shard), F32)
+    return pl.pallas_call(
+        results_kernel,
+        grid=(4,),
+        in_specs=[rows, rows, piece(0), piece(1), piece(2), wider(3, low), wider(4, high), piece(5), gain, gain],
+        out_specs=[rows, rows, first, second, first, second]
+        + [pl.BlockSpec((shard, 2 * cols), lambda i: (0, i)), pl.BlockSpec((shard, 2 * cols), lambda i: (i, 0)), gain, gain],
+        out_shape=[token, token, half, half, half, half]
+        + [jax.ShapeDtypeStruct((shard, 8 * cols), F32), jax.ShapeDtypeStruct((4 * shard, 2 * cols), F32), gain_shape, gain_shape],
+        name="results",
+    )(out, dx, res, res, res, res, res, res, g1, g2)
 
 
 def per_device(block_input, seq_ids, rand, ln1_gain, w_query, w_key, w_value, w_out, ln2_gain, w_up, w_down, cotangent):
@@ -992,25 +1092,20 @@
     factor = dim ** (-0.25)
     ns, nf = lax.axis_size("seq"), lax.axis_size("fsdp")
     seqs = max(2, ns // 4)
-    tiles = toks // TILE
     x = block_input.reshape(micro * toks, width)
     dy = cotangent.reshape(micro * toks, width)
-    ids = seq_ids.reshape(micro, toks)
     shard = ln1_gain.shape[0]
-    mine = (jnp.arange(width) // shard == lax.axis_index("fsdp"))[None, :]
-    row = jnp.arange(PAD)[:, None]
-    gains = jnp.where(row == 0, jnp.tile(ln1_gain, nf)[None, :], jnp.tile(ln2_gain, nf)[None, :])
-    gains = jnp.where(jnp.logical_and(mine, row < 2), gains, jnp.zeros_like(gains))
     out, att, a2, hid, dpre, dmid, dq, a1, ks, vv, fk, wq, wk, wv, part, total, gains, gg = front(
-        x, dy, ids, rand, gains, w_key, w_value, w_query, w_out, w_up, w_down,
+        x, dy, seq_ids, rand, ln1_gain.reshape(1, shard), ln2_gain.reshape(1, shard), w_key, w_value, w_query, w_out, w_up, w_down,
         micro=micro, seqs=seqs, nf=nf, ns=ns, factor=factor,
     )
-    dx, g1g, g2g, wqg, wkg, wvg, wog, wug, wdg = back(
+    dx, g1g, g2g, res = back(
         [x, dy, hid, dpre, a2, att, dmid, dq, a1, ks, vv, fk, wq, wk, wv],
-        [ids, rand, gains, gg, total, part[0]],
+        [seq_ids, rand, gains, gg, total, part[0]],
         micro=micro, seqs=seqs, nf=nf, ns=ns, shard=shard, factor=factor,
     )
     shape = block_input.shape
+    out, dx, wqg, wog, wkg, wvg, wug, wdg, g1g, g2g = results(out, dx, res, g1g, g2g, shard)
     return (out.reshape(shape), dx.reshape(shape), g1g[0], wqg, wkg, wvg, wog, g2g[0], wug, wdg)
 
 

time: 188 us -> 162 us (0.86)
  Pallas kernels: 175 us -> 161 us
  local copies, waits for them, and re-layouts: 11.7 us -> 0 us
    pallas_call x1, Pallas kernels: 94 us -> 74.6 us  [back(): pl.pallas_call(functools.partial(back_kernel, micro=micro, seqs=seqs, fac...]
    unnamed x29 -> x0, local copies, waits for them, and re-layouts: 11 us -> none
    pallas_call x0 -> x1, Pallas kernels: none -> 5.41 us  [results(): pl.pallas_call(results_kernel, grid=(4,), in_specs=[rows, rows, piece(0),...]
where the time goes in v3:
time: 162 us
  Pallas kernels  161 us (99%)
    pallas_call x1, Pallas kernels, front(): pl.pallas_call(functools.partial(front_kernel, micro=micro, seqs=seqs, fa...  81 us
    pallas_call x1, Pallas kernels, back(): pl.pallas_call(functools.partial(back_kernel, micro=micro, seqs=seqs, fac...  74.6 us
    pallas_call x1, Pallas kernels, results(): pl.pallas_call(results_kernel, grid=(4,), in_specs=[rows, rows, piece(0),...  5.41 us

profile of v3, /device:TPU:0, one launch (start us, length us, event | category | flops | bytes accessed | tf_op | source)
XLA Modules:
  0.0 161.9 jit_solution(6559625748868608259)
XLA Ops:
  0.6 81.0 %front.1 = (bf16[1536,512]{1,0:T(8,128)(2,1)}, bf16[1536,512]{1,0:T(8,128)(2,1)}, bf16[1536,512]{1,0:T(8,128)(2,1)}, bf16[1536,2048]{1,0:T(8,128)(2,1)}, bf16[15...) custom-call(bf16[1536,512]{1,0:T(8,128)(2,1)} %bitcast.13, ...), custom_call_target="tpu_custom_call" | custom-call | tf_op jit(solution)/shard_map/front/pallas_call | solution.py:604
  81.7 74.6 %back.1 = (bf16[1536,512]{1,0:T(8,128)(2,1)}, f32[1,128]{1,0:T(1,128)}, f32[1,128]{1,0:T(1,128)}, bf16[6,8,64,256]{3,2,1,0:T(8,128)(2,1)}) custom-call(bf16[1536,512]{1,0:T(8,128)(2,1)} %bitcast.14, bf16[1536,512]{1,0:T(8,128)(2,1)} %bitcast.16, bf16[1536,2048]{1,0:T(8,128)(2,1)} %get-tuple-element.43.hid_in, bf16[1536,2048]{1,0:T(8,128)(2,1)} %get-tuple-element.44.dpre_in, ...), custom_call_target="tpu_custom_call" | custom-call | tf_op jit(solution)/shard_map/back/pallas_call | solution.py:1010
  156.3 5.4 %results.1 = (bf16[1536,512]{1,0:T(8,128)(2,1)}, bf16[1536,512]{1,0:T(8,128)(2,1)}, f32[128,512]{1,0:T(8,128)}, f32[128,512]{1,0:T(8,128)}, f32[128,512]{1,0:T(8...) custom-call(bf16[1536,512]{1,0:T(8,128)(2,1)} %get-tuple-element.42., ...), custom_call_target="tpu_custom_call" | custom-call | tf_op jit(solution)/shard_map/results/pallas_call | solution.py:1077

commit v4 on v3

--- a/solution.py
+++ b/solution.py
@@ -13,7 +13,8 @@
 F32 = jnp.float32
 BF16 = jnp.bfloat16
 PAD = 16
-SPREAD_AT = 3
+SCATTER_AT = 3
+AR2_AT = 1
 
 
 def dot(a, b):
@@ -331,16 +332,21 @@
 
 
 def front_kernel(
-    x_ref, dy_ref, ids_ref, rand_ref, g1_in, g2_in, wk_in, wv_in, wq_in, wo_in, wu_in, wd_in,
+    x_in, dy_in, ids_ref, rand_ref, g1_in, g2_in, wk_in, wv_in, wq_in, wo_in, wu_in, wd_in,
     out_o, att_o, a2_o, hid_o, dpre_o, dmid_o, dq_o, a1_o, ks_o, vv_o, fk_o, wq_o, wk_o, wv_o, p_o, s_o, gain_o, gg_o,
-    a1, ks, vv, fk, qs, fq, t_out, t_att, t_a2, t_hid, t_dpre, t_dmid, t_dq,
+    x_ref, dy_ref,
+    a1, ks, vv, fk, qs, fq, t_out, t_att, t_a2, t_hid, t_dpre, t_dmid, t_dq, att_s, inv_s, mix_s,
     gains_in, gains, wk, wv, wq, wo, wu, wd, rbd, rt, b_ref, acc, p_out, p_got, p_full,
     w_send, w_recv, w_local, r_send, r_recv, g_send, g_recv, o_sem, t_sem,
     *, micro, seqs, factor,
 ):
     ex = Exchange()
     heads, _, feats = rand_ref.shape
-    total, width = x_ref.shape
+    total, width = x_in.shape
+    x_load = pltpu.make_async_copy(x_in, x_ref, o_sem.at[8])
+    dy_load = pltpu.make_async_copy(dy_in, dy_ref, o_sem.at[9])
+    x_load.start()
+    dy_load.start()
     toks = total // micro
     tiles = toks // TILE
     pairs = width // 128
@@ -348,15 +354,16 @@
         Sum(ex, p_out.at[mb], p_got.at[mb], p_full.at[mb], (r_send.at[mb], r_recv.at[mb], g_send.at[mb], g_recv.at[mb]), seqs)
         for mb in range(micro)
     ]
+    ex.greet()
     place = lax.broadcasted_iota(jnp.int32, (1, width), 1) // g1_in.shape[1] == ex.f
     gains_in[...] = jnp.zeros_like(gains_in)
     for i, g in enumerate((g1_in, g2_in)):
         wide = jnp.concatenate([g[...].astype(F32)] * ex.nf, axis=1)
         gains_in[i : i + 1, :] = jnp.where(place, wide, 0.0).astype(BF16)
-    ex.barrier()
+    ex.meet()
     pieces = []
     for i, (shard, full) in enumerate(
-        ((gains_in, gains), (wk_in, wk), (wv_in, wv), (wq_in, wq), (wo_in, wo), (wu_in, wu), (wd_in, wd))
+        ((gains_in, gains), (wk_in, wk), (wv_in, wv), (wq_in, wq), (wo_in, wo), (wd_in, wd), (wu_in, wu))
     ):
         pieces.append(Gather(ex, shard, full, w_send.at[i], w_recv.at[i], w_local.at[i]))
     for piece in pieces:
@@ -373,6 +380,7 @@
     gain_o[...] = both.astype(BF16)
     g1, g2 = both[0:1], both[1:2]
     gg_o[...] = jnp.zeros_like(gg_o)
+    x_load.wait()
 
     def ident(mb):
         if seqs == 2:
@@ -425,8 +433,10 @@
             sums[mb].scatter()
     for i, (src, dst) in enumerate(((a1, a1_o), (ks, ks_o), (vv, vv_o), (fk, fk_o))):
         emit(src, dst, o_sem.at[i])
+    fk_out = outs.pop()
     pieces[3].forward()
     pieces[3].finish()
+    sums[0].spread(sums[0].reduce())
 
     def queries(t, carry):
         r = rows_at(t, TILE)
@@ -436,19 +446,32 @@
         return carry
 
     def queries_and_sums(t, carry):
-        @pl.when(t == SPREAD_AT)
+        @pl.when(t == SCATTER_AT)
         def _():
-            sums[0].spread(sums[0].reduce())
             for other in sums[1:]:
                 other.scatter()
 
         return queries(t, carry)
 
     lax.fori_loop(0, micro * tiles, queries_and_sums, 0)
-    for piece in pieces[4:]:
+    for piece in pieces[4:6]:
         piece.forward()
-    for piece in pieces[4:]:
+    for piece in pieces[4:6]:
         piece.finish()
+
+    dy_load.wait()
+    fk_out.wait()
+    dh = fk
+
+    def hidden_grads(t, carry):
+        r = rows_at(t, TILE)
+        dy = dy_ref[r, :]
+        for j in range(wd.shape[0] // 256):
+            js = slice(256 * j, 256 * j + 256)
+            dh[r, js] = dot_nt(dy, wd[js, :]).astype(BF16)
+        return carry
+
+    lax.fori_loop(0, micro * tiles, hidden_grads, 0)
     for i, (src, dst) in enumerate(((wq, wq_o), (wk, wk_o), (wv, wv_o))):
         emit(src, dst, o_sem.at[4 + i])
     tiled = ((t_out, out_o), (t_att, att_o), (t_a2, a2_o), (t_hid, hid_o), (t_dpre, dpre_o), (t_dmid, dmid_o), (t_dq, dq_o))
@@ -463,6 +486,27 @@
         build_b(p_full.at[mb], b_ref, first_id, last_id, seqs, True)
         acc[...] = jnp.zeros_like(acc)
 
+        def attend(t, carry, mb=mb, last_id=last_id):
+            r = rows_at(t + mb * tiles, TILE)
+            own = rows_at(t, TILE)
+            last = last_lanes(ids_of(mb, t), last_id)
+            lane = lax.broadcasted_iota(jnp.int32, (TILE, 128), 1)
+            sel = jnp.logical_xor(lane < 64, last)
+
+            def swap(v):
+                return jnp.where(last, pltpu.roll(v, 64, 1), v)
+
+            for p in range(pairs):
+                base = 2 * feats * p
+                ps = slice(128 * p, 128 * p + 128)
+                a = dot_nt(fq[r, base : base + feats], b_ref[2 * p])
+                b = dot_nt(fq[r, base + feats : base + 2 * feats], b_ref[2 * p + 1])
+                inv = 1.0 / jnp.where(sel, a[:, 128:], b[:, 128:])
+                att_s[own, ps] = swap(jnp.where(sel, a[:, :128], b[:, :128]) * inv)
+                inv_s[own, ps] = swap(inv)
+            mix_s[own, :] = x_ref[r, :].astype(F32) + dot(att_s[own, :].astype(BF16), wo[...])
+            return carry
+
         def mid(t, carry, mb=mb, last_id=last_id):
             g = t + mb * tiles
             slot = g % 2
@@ -473,16 +517,9 @@
                 for c in tile_copies(g - 2, slot):
                     c.wait()
 
-            if mb == 0:
-
-                @pl.when(t == 1)
-                def _():
-                    for other in sums[1:]:
-                        other.spread(other.reduce())
-
             if mb == 1:
 
-                @pl.when(t == 1)
+                @pl.when(t == AR2_AT)
                 def _():
                     sums[0].spread_settle()
                     sums[0].spread(sums[0].reduce())
@@ -496,19 +533,9 @@
             def swap(v):
                 return jnp.where(last, pltpu.roll(v, 64, 1), v)
 
-            att_parts, inv_parts = [], []
-            for p in range(pairs):
-                base = 2 * feats * p
-                a = dot_nt(fq[r, base : base + feats], b_ref[2 * p])
-                b = dot_nt(fq[r, base + feats : base + 2 * feats], b_ref[2 * p + 1])
-                inv = 1.0 / jnp.where(sel, a[:, 128:], b[:, 128:])
-                att_parts.append(swap(jnp.where(sel, a[:, :128], b[:, :128]) * inv))
-                inv_parts.append(swap(inv))
-            att = jnp.concatenate(att_parts, axis=1)
-            inv = jnp.concatenate(inv_parts, axis=1)
-            att_low = att.astype(BF16)
-            t_att[slot] = att_low
-            mixed = x_ref[r, :].astype(F32) + dot(att_low, wo[...])
+            own = rows_at(t, TILE)
+            att, inv, mixed = att_s[own, :], inv_s[own, :], mix_s[own, :]
+            t_att[slot] = att.astype(BF16)
             normed, rescale = norm_parts(mixed)
             a2 = (normed * g2).astype(BF16)
             t_a2[slot] = a2
@@ -516,11 +543,10 @@
             for j in range(wu.shape[1] // 256):
                 js = slice(256 * j, 256 * j + 256)
                 pre = dot(a2, wu[:, js])
-                dh = dot_nt(dy, wd[js, :])
                 cdf = 0.5 * (1.0 + lax.erf(pre * 0.7071067811865476))
                 slope = cdf + pre * jnp.exp(-0.5 * pre * pre) * 0.3989422804014327
                 t_hid[slot, :, js] = (pre * cdf).astype(BF16)
-                t_dpre[slot, :, js] = (dh * slope).astype(BF16)
+                t_dpre[slot, :, js] = (dh[r, js].astype(F32) * slope).astype(BF16)
             t_out[slot] = (mixed + dot(t_hid[slot], wd[...])).astype(BF16)
             da2 = dot_nt(t_dpre[slot], wu[...])
             gg_o[...] += jnp.sum(da2 * normed, axis=0, keepdims=True)
@@ -552,6 +578,12 @@
                 c.start()
             return carry
 
+        lax.fori_loop(0, tiles, attend, 0)
+        if mb == 0:
+            for other in sums[1:]:
+                other.spread(other.reduce())
+            pieces[6].forward()
+            pieces[6].finish()
         lax.fori_loop(0, tiles, mid, 0)
         if mb == 0:
             sums[0].scatter_settle()
@@ -593,17 +625,18 @@
     ]
     v = pltpu.VMEM
     dma = pltpu.SemaphoreType.DMA
-    scratch = [v((total, width), BF16)] * 3 + [v((total, heads * feats), BF16), v((total, width), BF16), v((total, heads * feats), BF16)]
+    scratch = [v((total, width), BF16)] * 5 + [v((total, heads * feats), BF16), v((total, width), BF16), v((total, heads * feats), BF16)]
     scratch += [v((2, TILE, width), BF16)] * 3 + [v((2, TILE, hidden), BF16)] * 2 + [v((2, TILE, width), BF16)] * 2
+    scratch += [v((total // micro, width), F32)] * 3
     scratch += [v((PAD, width), BF16), v((nf * PAD, width), BF16)] + [v((width, width), BF16)] * 4 + [v((width, hidden), BF16), v((hidden, width), BF16)]
     scratch += [v((heads // 4, 256, 4 * feats), BF16), v((heads // 2, 2 * feats, 256), BF16), v((heads, 256, feats), BF16)]
     scratch += [v((heads, rows, feats), F32), v((micro, chunks, rows, feats), BF16)]
     scratch += [v((micro, ns, rows, feats), BF16), v((micro, ns, rows, feats), BF16)]
     kinds = nf - 1
-    scratch += [dma((7, kinds)), dma((7, kinds)), dma((7,))] + [dma((micro, ns))] * 4 + [dma((8,)), dma((2, 7))]
+    scratch += [dma((7, kinds)), dma((7, kinds)), dma((7,))] + [dma((micro, ns))] * 4 + [dma((10,)), dma((2, 7))]
     return pl.pallas_call(
         functools.partial(front_kernel, micro=micro, seqs=seqs, factor=factor),
-        in_specs=[vmem] * 6 + [hbm] * 6,
+        in_specs=[hbm] * 2 + [vmem] * 4 + [hbm] * 6,
         out_specs=[hbm] * 14 + [vmem, hbm, vmem, vmem],
         out_shape=out_shape,
         scratch_shapes=scratch,
@@ -827,8 +860,8 @@
     lax.fori_loop(0, blocks, down_block, 0)
     for piece in (d1, d2):
         ex.pending += [lambda yy=yy, piece=piece: piece.core_copy(yy) for yy in range(ex.ny)]
+    kv_sum.spread(kv_sum.reduce())
     go(d1, d2)
-    kv_sum.spread(kv_sum.reduce())
     build_features(rand_ref, rbd, rt)
     need("a2")
     tr[...] = a2[...].T

time: 162 us -> 155 us (0.957)
  Pallas kernels: 161 us -> 153 us
    pallas_call x1, Pallas kernels: 81 us -> 75.5 us  [front(): pl.pallas_call(functools.partial(front_kernel, micro=micro, seqs=seqs, fa...]
    pallas_call x1, Pallas kernels: 74.6 us -> 72.5 us  [back(): pl.pallas_call(functools.partial(back_kernel, micro=micro, seqs=seqs, fac...]
where the time goes in v4:
time: 155 us; the launch traced here: 154 us
  Pallas kernels  153 us (99%)
    pallas_call x1, Pallas kernels, front(): pl.pallas_call(functools.partial(front_kernel, micro=micro, seqs=seqs, fa...  75.5 us
    pallas_call x1, Pallas kernels, back(): pl.pallas_call(functools.partial(back_kernel, micro=micro, seqs=seqs, fac...  72.5 us
    pallas_call x1, Pallas kernels, results(): pl.pallas_call(results_kernel, grid=(4,), in_specs=[rows, rows, piece(0),...  5.41 us

profile of v4, /device:TPU:0, one launch (start us, length us, event | category | flops | bytes accessed | tf_op | source)
XLA Modules:
  0.0 154.3 jit_solution(5727854524831002014)
XLA Ops:
  0.6 75.5 %front.1 = (bf16[1536,512]{1,0:T(8,128)(2,1)}, bf16[1536,512]{1,0:T(8,128)(2,1)}, bf16[1536,512]{1,0:T(8,128)(2,1)}, bf16[1536,2048]{1,0:T(8,128)(2,1)}, bf16[15...) custom-call(bf16[1536,512]{1,0:T(8,128)(2,1)} %bitcast.13, ...), custom_call_target="tpu_custom_call" | custom-call | tf_op jit(solution)/shard_map/front/pallas_call | solution.py:637
  76.2 72.5 %back.1 = (bf16[1536,512]{1,0:T(8,128)(2,1)}, f32[1,128]{1,0:T(1,128)}, f32[1,128]{1,0:T(1,128)}, bf16[6,8,64,256]{3,2,1,0:T(8,128)(2,1)}) custom-call(bf16[1536,512]{1,0:T(8,128)(2,1)} %bitcast.14, bf16[1536,512]{1,0:T(8,128)(2,1)} %bitcast.16, bf16[1536,2048]{1,0:T(8,128)(2,1)} %get-tuple-element.43.hid_in, bf16[1536,2048]{1,0:T(8,128)(2,1)} %get-tuple-element.44.dpre_in, ...), custom_call_target="tpu_custom_call" | custom-call | tf_op jit(solution)/shard_map/back/pallas_call | solution.py:1043
  148.7 5.4 %results.1 = (bf16[1536,512]{1,0:T(8,128)(2,1)}, bf16[1536,512]{1,0:T(8,128)(2,1)}, f32[128,512]{1,0:T(8,128)}, f32[128,512]{1,0:T(8,128)}, f32[128,512]{1,0:T(8...) custom-call(bf16[1536,512]{1,0:T(8,128)(2,1)} %get-tuple-element.42., ...), custom_call_target="tpu_custom_call" | custom-call | tf_op jit(solution)/shard_map/results/pallas_call | solution.py:1110

commit v5 on v4

--- a/solution.py
+++ b/solution.py
@@ -13,7 +13,7 @@
 F32 = jnp.float32
 BF16 = jnp.bfloat16
 PAD = 16
-SCATTER_AT = 3
+SCATTER_AT = 5
 AR2_AT = 1
 
 
@@ -804,8 +804,6 @@
         for name in names:
             loads.pop(name).wait()
 
-    ex.meet()
-    kv_sum.scatter()
     pieces = []
     for i in range(PIECES):
         seq = SeqSum(ex, (s_out.at[i], s_got1.at[i], s_mid.at[i], s_got2.at[i], res_o.at[i]), t_send.at[i], t_recv.at[i])
@@ -832,6 +830,8 @@
 
     need("att", "dmid")
     small(att[...].T, dmid[...], q, 1)
+    ex.meet()
+    kv_sum.scatter()
     need("a1", "dq")
     small(a1[...].T, dq[...], q, 0)
     q.core_send()

time: 155 us -> 155 us (level)
  no operation moved by 1% of the time
where the time goes in v5:
time: 155 us; the launch traced here: 154 us
  Pallas kernels  154 us (99%)
    pallas_call x1, Pallas kernels, front(): pl.pallas_call(functools.partial(front_kernel, micro=micro, seqs=seqs, fa...  75.5 us
    pallas_call x1, Pallas kernels, back(): pl.pallas_call(functools.partial(back_kernel, micro=micro, seqs=seqs, fac...  72.6 us
    pallas_call x1, Pallas kernels, results(): pl.pallas_call(results_kernel, grid=(4,), in_specs=[rows, rows, piece(0),...  5.41 us

profile of v5, /device:TPU:0, one launch (start us, length us, event | category | flops | bytes accessed | tf_op | source)
XLA Modules:
  0.0 154.4 jit_solution(6408114628423562932)
XLA Ops:
  0.6 75.5 %front.1 = (bf16[1536,512]{1,0:T(8,128)(2,1)}, bf16[1536,512]{1,0:T(8,128)(2,1)}, bf16[1536,512]{1,0:T(8,128)(2,1)}, bf16[1536,2048]{1,0:T(8,128)(2,1)}, bf16[15...) custom-call(bf16[1536,512]{1,0:T(8,128)(2,1)} %bitcast.13, ...), custom_call_target="tpu_custom_call" | custom-call | tf_op jit(solution)/shard_map/front/pallas_call | solution.py:637
  76.2 72.6 %back.1 = (bf16[1536,512]{1,0:T(8,128)(2,1)}, f32[1,128]{1,0:T(1,128)}, f32[1,128]{1,0:T(1,128)}, bf16[6,8,64,256]{3,2,1,0:T(8,128)(2,1)}) custom-call(bf16[1536,512]{1,0:T(8,128)(2,1)} %bitcast.14, bf16[1536,512]{1,0:T(8,128)(2,1)} %bitcast.16, bf16[1536,2048]{1,0:T(8,128)(2,1)} %get-tuple-element.43.hid_in, bf16[1536,2048]{1,0:T(8,128)(2,1)} %get-tuple-element.44.dpre_in, ...), custom_call_target="tpu_custom_call" | custom-call | tf_op jit(solution)/shard_map/back/pallas_call | solution.py:1043
  148.8 5.4 %results.1 = (bf16[1536,512]{1,0:T(8,128)(2,1)}, bf16[1536,512]{1,0:T(8,128)(2,1)}, f32[128,512]{1,0:T(8,128)}, f32[128,512]{1,0:T(8,128)}, f32[128,512]{1,0:T(8...) custom-call(bf16[1536,512]{1,0:T(8,128)(2,1)} %get-tuple-element.42., ...), custom_call_target="tpu_custom_call" | custom-call | tf_op jit(solution)/shard_map/results/pallas_call | solution.py:1110
